TPU v7x, 256 devices: a whole 4x4x8 slice. The times are simulated.
256 devices in a mesh: seq: 64 (over z, y, core), rep: 4 (over x).
Axes of the slice: x: 4, y: 4, z: 8, core: 2. Of those that a mesh axis runs over, the one named last changes fastest.
Arguments:
- inputs: bfloat16 [4, 8192, 1024], P('rep', 'seq'), may hold values from -6 to 6
- weight_t: bfloat16 [3072, 1024], P('seq', 'rep'), may hold values from -0.1875 to 0.1875
- states: float32 [4, 8192, 1024], P('rep', 'seq'), may hold values from -0.9 to 0.9
- doc_ids: int32 [4, 8192], P('rep', 'seq'), may hold values from 0 to 31, never falling along the last dimension, each value on 1 to 512 neighbouring positions
- recur: float32 [3, 1024], replicated, may hold values from -1 to 1
- bias: float32 [3, 1024], replicated, may hold values from -8 to 3, as said below
- out_grad: bfloat16 [4, 8192, 1024], P('rep', 'seq'), may hold values from -6 to 6
Outputs:
- input_grad: bfloat16 [4, 8192, 1024], P('rep', 'seq')
- weight_grad: float32 [3072, 1024], P('seq', 'rep')
- param_grad: float32 [6, 1024], replicated
Inputs may be any that keep to these rules, and one draw needn't show every extreme that they name: `doc_ids`: within each sequence the numbers never fall; every document has 1 to 512 tokens, and some document has exactly 512. `bias`: row 0 lies between -8 and -1, rows 1 and 2 between -3 and 3.
All inputs are finite; a program needn't handle non-finite values.
Results may differ from a plain program's by a relative error of at most 0.0095.
Values may be sent and summed in bfloat16 or wider, within the bound.
No kernel may reach another device: no remote copies, remote signals or barrier semaphores. Data moves between devices by JAX's collectives and lax.ppermute only.
A program may use at most 128 MiB of HBM per device.

v0:
```python
import functools
import math

import jax
import jax.numpy as jnp
from jax import lax
from jax.sharding import Mesh
from jax.sharding import PartitionSpec as P

SEQ = ("seq_0", "seq_1", "seq_2")
SEQ_REP = ("seq_0", "seq_1", "seq_2", "rep")


def copy_for_each(x, axis):
    copies = jnp.broadcast_to(x, (lax.axis_size(axis), *x.shape))
    return lax.all_to_all(copies, axis, split_axis=0, concat_axis=0, tiled=True)


def joined_along(parts, dim):
    dims = list(parts.shape[1:])
    dims[dim] *= parts.shape[0]
    return jnp.moveaxis(parts, 0, dim).reshape(dims)


def collect(x, axis, dim):
    parts = copy_for_each(x, axis)
    return joined_along(parts, dim)


def shifted(block, axis, distance):
    devices = range(lax.axis_size(axis))
    route = [(i - distance, i) for i in devices if i - distance in devices]
    return lax.ppermute(block, axis, route)


def gathered_once(x, axis):
    leaves = jax.tree.leaves(x)
    sequence = sorted(range(len(leaves)), key=lambda k: -leaves[k].size)
    width = (1, *leaves[sequence[0]].shape)[-1]
    lines = [
        jnp.pad(leaves[k].reshape(-1), (0, -leaves[k].size % width)).reshape(-1, width)
        for k in sequence
    ]
    both, at, found = (copy_for_each(jnp.concatenate(lines), axis), 0, {})
    for k, line in zip(sequence, lines):
        piece = both[:, at : at + len(line)].reshape(len(both), -1)
        found[k] = piece[:, : leaves[k].size].reshape(-1, *leaves[k].shape)
        at += len(line)
    numbers = iter(range(len(leaves)))
    return jax.tree.map(lambda _: found[next(numbers)], x)


def combined_pairwise(pieces, combine):
    while len(jax.tree.leaves(pieces)[0]) > 1:
        pieces = jax.vmap(combine)(
            *(jax.tree.map(lambda part: part[side::2], pieces) for side in (0, 1))
        )
    return jax.tree.map(lambda part: part[0], pieces)


def carried_in(x, axis, combine, identity):
    count, here = (lax.axis_size(axis), lax.axis_index(axis))
    passed = jnp.arange(count) > here

    def kept(part, zero, own):
        part = jnp.where(
            passed.reshape(-1, *(1 for _ in own.shape)), part, jnp.asarray(zero, own.dtype)
        )
        return part[::-1]

    pieces = gathered_once(x, axis)
    return combined_pairwise(jax.tree.map(kept, pieces, identity, x), combine)


def split_up(x, dim, count):
    before, after = (x.shape[:dim], x.shape[dim + 1 :])
    return jnp.moveaxis(x.reshape(*before, count, -1, *after), dim, 0)


def sum_at_owner(x, axis, dim):
    parts = split_up(x, dim, lax.axis_size(axis))
    arrived = lax.all_to_all(parts, axis, split_axis=0, concat_axis=0, tiled=True)
    return arrived.astype(jnp.float32).sum(axis=0)


def by_axis(x, axes):
    return functools.reduce(lax.psum, axes, x)


def compose(earlier, later):
    return (later[0] * earlier[0], later[1] + later[0] * earlier[1])


def local(inputs, weight_t, states, doc_ids, recur, bias, out_grad):
    feats = inputs[0]
    hidden_now = states[0]
    ids_float = doc_ids[0].astype(jnp.float32)
    count = feats.shape[0]
    width = hidden_now.shape[1]
    columns = collect(weight_t, "rep", 1)
    contract_last = (((1,), (1,)), ((), ()))
    full_weight = lax.all_gather(columns, SEQ, axis=0, tiled=True)
    preact = lax.dot_general(feats, full_weight, contract_last, preferred_element_type=jnp.float32)
    tail_state, tail_id = shifted((hidden_now[-1:], ids_float[-1:]), SEQ, 1)
    first_same = jnp.where(
        (ids_float[0] == tail_id[0]) & (lax.axis_index(SEQ) > 0), 1.0, 0.0
    ).astype(jnp.float32)
    same = jnp.concatenate(
        [first_same[None], (ids_float[1:] == ids_float[:-1]).astype(jnp.float32)]
    )
    prior = jnp.concatenate([tail_state, hidden_now[:-1]], 0) * same[:, None]
    gate_z = jax.nn.sigmoid(preact[:, :width] + recur[0] * prior + bias[0])
    gate_r = jax.nn.sigmoid(preact[:, width : 2 * width] + recur[1] * prior + bias[1])
    gate_c = jnp.tanh(preact[:, 2 * width :] + recur[2] * gate_r * prior + bias[2])
    jacobian = same[:, None] * (
        1.0
        - gate_z
        + (gate_c - prior) * gate_z * (1.0 - gate_z) * recur[0]
        + gate_z
        * (1.0 - gate_c * gate_c)
        * recur[2]
        * (gate_r + prior * gate_r * (1.0 - gate_r) * recur[1])
    )
    upstream = out_grad[0].astype(jnp.float32)
    next_row = shifted(jacobian[:1], SEQ, -1)
    factor = jnp.concatenate([jacobian[1:], next_row], 0)
    product, local_adj = lax.associative_scan(compose, (factor, upstream), reverse=True, axis=0)
    ones_row = jnp.ones((1, width), jnp.float32)
    zeros_row = jnp.zeros((1, width), jnp.float32)
    _, entering = carried_in((product[:1], local_adj[:1]), SEQ, compose, (ones_row, zeros_row))
    adjoint = local_adj + product * entering
    grad_z = adjoint * (gate_c - prior) * gate_z * (1.0 - gate_z)
    grad_c = adjoint * gate_z * (1.0 - gate_c * gate_c)
    grad_r = grad_c * recur[2] * prior * gate_r * (1.0 - gate_r)
    grad_pre = jnp.concatenate([grad_z, grad_r, grad_c], 1).astype(jnp.bfloat16)
    input_grad = jnp.dot(grad_pre, full_weight, preferred_element_type=jnp.float32)
    tokens_all = count * inputs.shape[0] * lax.axis_size(SEQ) * lax.axis_size("rep")
    normal_factor = 1.0 / math.sqrt(tokens_all)
    row_share = lax.psum_scatter(
        lax.dot_general(
            grad_pre, feats, (((0,), (0,)), ((), ())), preferred_element_type=jnp.float32
        ),
        SEQ,
        scatter_dimension=0,
        tiled=True,
    )
    weight_grad = sum_at_owner(row_share.astype(jnp.bfloat16), "rep", 1) * normal_factor
    stats = jnp.stack(
        [
            grad_z.sum(0),
            grad_r.sum(0),
            grad_c.sum(0),
            (grad_z * prior).sum(0),
            (grad_r * prior).sum(0),
            (grad_c * gate_r * prior).sum(0),
        ]
    )
    param_grad = by_axis(stats, SEQ_REP) * normal_factor
    return (input_grad.astype(jnp.bfloat16)[None], weight_grad, param_grad)


def solution(mesh):
    torus = Mesh(
        mesh.devices.reshape(8, 4, 2, mesh.shape["rep"]), ("seq_0", "seq_1", "seq_2", "rep")
    )
    in_specs = (
        P("rep", SEQ, None),
        P(SEQ, "rep"),
        P("rep", SEQ, None),
        P("rep", SEQ),
        P(),
        P(),
        P("rep", SEQ, None),
    )
    out_specs = (P("rep", SEQ, None), P(SEQ, "rep"), P())
    return jax.shard_map(local, mesh=torus, in_specs=in_specs, out_specs=out_specs, check_vma=False)
```

profile of v0, /device:TPU:2, one launch (start us, length us, event | category | flops | bytes accessed | tf_op | source)
XLA Modules:
  0.0 406.0 jit_solution(11852315016412689403)
XLA Ops:
  8.1 9.0 %all_to_all.15 = bf16[4,48,256]{2,1,0:T(8,128)(2,1)S(1)} all-to-all(bf16[4,48,256]{2,1,0:T(8,128)(2,1)S(1)} %broadcast_in_dim.35), channel_id=1, replica_groups=mesh['seq_0'=8,'seq_1'=4,'seq_2'=2,'rep'=4] {'rep'}, dimensions={0} | all-to-all | bytes 196608 | tf_op jit(solution)/shard_map/all_to_all | solution.py:16
  18.9 1.9 collective-permute-start
  21.6 3.6 collective-permute-start.1
  27.0 1.9 fusion.33
  30.4 70.1 %all-gather.2.cloned.1.call-done = bf16[3072,1024]{1,0:T(8,128)(2,1)} async-done(((bf16[48,1024]{1,0:T(8,128)(2,1)}), bf16[3072,1024]{1,0:T(8,128)(2,1)}) %all-gather.2.cloned.1.call-update) | async-done | bytes 6291472 | tf_op jit(solution)/shard_map/all_gather | solution.py:102
  100.5 5.0 %fusion.16 = f32[128,3072]{1,0:T(8,128)S(1)} fusion(bf16[3072,1024]{1,0:T(8,128)(2,1)} %all-gather.2.cloned.1.call-done, bf16[1,128,1024]{2,1,0:T(8,128)(2,1)S(1)} %copy-done), kind=kOutput, calls=%fused_computation.39 | convolution fusion | flops 805306368 | bytes 8126464 | tf_op jit(solution)/shard_map/dot_general | solution.py:103
  106.3 1.3 collective-permute-start.2
  107.6 1.4 slice_bitcast_fusion.1
  111.3 4.3 %slice.416 = f32[64,1024]{1,0:T(8,128)} reverse(f32[64,1024]{1,0:T(8,128)} %slice.415), dimensions={0} | reverse | bytes 524288 | tf_op jit(solution)/shard_map/slice | solution.py:127
  115.6 4.3 %slice.420 = f32[64,1024]{1,0:T(8,128)} reverse(f32[64,1024]{1,0:T(8,128)} %slice.419), dimensions={0} | reverse | bytes 524288 | tf_op jit(solution)/shard_map/slice | solution.py:127
  120.0 4.3 %slice.391 = f32[63,1024]{1,0:T(8,128)} reverse(f32[63,1024]{1,0:T(8,128)} %slice.390), dimensions={0} | reverse | bytes 516096 | tf_op jit(solution)/shard_map/slice | solution.py:127
  125.5 4.3 %slice.418 = f32[64,1024]{1,0:T(8,128)} reverse(f32[64,1024]{1,0:T(8,128)} %slice.417), dimensions={0} | reverse | bytes 524288 | tf_op jit(solution)/shard_map/slice | solution.py:127
  129.8 2.5 slice.424
  132.4 1.2 fusion.34
  135.7 1.1 fusion.35
  143.5 1.4 fusion.37
  144.9 1.4 slice.446
  146.3 1.4 slice.448
  147.6 1.4 slice.452
  149.0 1.4 slice.447
  150.4 1.4 slice.449
  151.8 1.4 fusion.40
  154.4 1.3 slice.454
  155.7 1.3 slice.456
  158.4 1.4 fusion.39
  159.9 1.4 slice.444
  161.2 1.3 slice.541
  163.8 1.3 slice.519
  169.5 2.5 slice.414
  182.1 1.1 pad.99
  183.1 1.7 pad_maximum_fusion.5
  184.8 2.6 pad.112
  187.5 2.6 pad.113
  190.9 1.0 broadcast_in_dim.37
  191.9 9.2 %all-to-all-start.1 = ((f32[64,2,1024]{2,1,0:T(2,128)}), f32[64,2,1024]{2,1,0:T(2,128)}, u32[]{:S(2)}, u32[]{:S(2)}) async-start(f32[64,2,1024]{2,1,0:T(2,128)} %broadcast_in_dim.37), calls=%async_computation.1 | async-start | bytes 1048576 | tf_op jit(solution)/shard_map/all_to_all | solution.py:16
  204.1 3.4 rev.5
  207.6 10.9 %all-to-all-done.1 = f32[64,2,1024]{2,1,0:T(2,128)} async-done(((f32[64,2,1024]{2,1,0:T(2,128)}), f32[64,2,1024]{2,1,0:T(2,128)}, u32[]{:S(2)}, u32[]{:S(2)}) %all-to-all-start.1) | async-done | bytes 524320 | tf_op jit(solution)/shard_map/all_to_all | solution.py:16
  218.5 1.9 broadcast_select_fusion
  221.2 1.0 multiply_reduce_fusion
  223.1 6.4 %fusion.13 = f32[3072,1024]{1,0:T(8,128)} fusion(bf16[128,1024]{1,0:T(8,128)(2,1)S(1)} %get-tuple-element.11, bf16[128,1024]{1,0:T(8,128)(2,1)S(1)} %get-tuple-element.10, bf16[128,1024]{1,0:T(8,128)(2,1)S(1)} %get-tuple-element.9, bf16[1,128,1024]{2,1,0:T(8,128)(2,1)S(1)} %copy-done), kind=kOutput, calls=%fused_computation.32 | convolution fusion | flops 807665664 | bytes 13631488 | tf_op jit(solution)/shard_map/dot_general | solution.py:140
  229.5 28.7 %psum.28 = f32[6,1024]{1,0:T(8,128)S(1)} all-reduce(f32[6,1024]{1,0:T(8,128)S(1)} %stack.27), channel_id=1, replica_groups=mesh['seq_0'=8,'seq_1'=4,'seq_2'=2,'rep'=4] {'seq_0'}, use_global_device_ids=true, to_apply=%region_8.9 | all-reduce | flops 6144 | bytes 49152 | tf_op jit(solution)/shard_map/psum | solution.py:87
  258.3 16.3 %psum.29 = f32[6,1024]{1,0:T(8,128)S(1)} all-reduce(f32[6,1024]{1,0:T(8,128)S(1)} %psum.28), channel_id=1, replica_groups=mesh['seq_0'=8,'seq_1'=4,'seq_2'=2,'rep'=4] {'seq_1'}, use_global_device_ids=true, to_apply=%region_9.10 | all-reduce | flops 6144 | bytes 49152 | tf_op jit(solution)/shard_map/psum | solution.py:87
  274.6 3.4 psum.30
  278.0 14.1 %psum.31 = f32[6,1024]{1,0:T(8,128)S(1)} all-reduce(f32[6,1024]{1,0:T(8,128)S(1)} %psum.30), channel_id=1, replica_groups=mesh['seq_0'=8,'seq_1'=4,'seq_2'=2,'rep'=4] {'rep'}, use_global_device_ids=true, to_apply=%region_11.12 | all-reduce | flops 6144 | bytes 49152 | tf_op jit(solution)/shard_map/psum | solution.py:87
  292.1 4.6 %fusion = bf16[1,128,1024]{2,1,0:T(8,128)(2,1)} fusion(bf16[3072,1024]{1,0:T(8,128)(2,1)} %all-gather.2.cloned.1.call-done, bf16[128,1024]{1,0:T(8,128)(2,1)S(1)} %copy-done.9, bf16[128,1024]{1,0:T(8,128)(2,1)S(1)} %copy-done.7, bf16[128,1024]{1,0:T(8,128)(2,1)S(1)} %copy-done.5), kind=kOutput, calls=%fused_computation.1 | convolution fusion | flops 807796736 | bytes 7340032 | tf_op jit(solution)/shard_map/dot_general | solution.py:136
  296.7 91.0 %reduce-scatter.2.cloned.1.call-done = f32[48,1024]{1,0:T(8,128)} async-done(((f32[3072,1024]{1,0:T(8,128)}), f32[48,1024]{1,0:T(8,128)}) %reduce-scatter.2.cloned.1.call-update) | async-done | bytes 196624 | tf_op jit(solution)/shard_map/reduce_scatter | solution.py:139
  389.3 4.8 %all-to-all-start.2 = ((bf16[4,48,256]{2,1,0:T(8,128)(2,1)}), bf16[4,48,256]{2,1,0:T(8,128)(2,1)S(1)}, u32[]{:S(2)}, u32[]{:S(2)}) async-start(bf16[4,48,256]{2,1,0:T(8,128)(2,1)} %bitcast.45), calls=%async_computation.3 | async-start | bytes 196608 | tf_op jit(solution)/shard_map/all_to_all | solution.py:82
  394.7 3.7 all-to-all-done.2
  (206 shorter events, 44.7 us)
Async XLA Ops:
  7.2 93.3 %copy-start = (bf16[1,128,1024]{2,1,0:T(8,128)(2,1)S(1)}, bf16[1,128,1024]{2,1,0:T(8,128)(2,1)}, u32[]{:S(2)}) copy-start(bf16[1,128,1024]{2,1,0:T(8,128)(2,1)} %param.7) | copy-start | bytes 786436
  7.2 21.7 %copy-start.12 = (f32[1,128,1024]{2,1,0:T(8,128)S(1)}, f32[1,128,1024]{2,1,0:T(8,128)}, u32[]{:S(2)}) copy-start(f32[1,128,1024]{2,1,0:T(8,128)} %param.9) | copy-start | bytes 1572868
  7.2 93.3 %all-gather.2.cloned.1.call-start = ((), (), s32[]{:S(2)}) async-start(), calls=%async_computation.4 | async-start | bytes 6389760 | tf_op jit(solution)/shard_map/all_gather | solution.py:102
  18.9 10.0 %collective-permute-start = (f32[1]{0:T(128)}, f32[1]{0:T(128)}, u32[]{:S(2)}, u32[]{:S(2)}) collective-permute-start(f32[1]{0:T(128)} %bitcast.3), channel_id=1, source_target_pairs={{0,4},{4,8},{8,12},{12,16},{16,20},{20,24},{24,28},{28,32},{32,36}... | collective-permute-start | bytes 20 | tf_op jit(solution)/shard_map/ppermute | solution.py:33
  21.6 83.9 %collective-permute-start.1 = (f32[1,1024]{1,0:T(1,128)S(1)}, f32[1,1024]{1,0:T(1,128)S(1)}, u32[]{:S(2)}, u32[]{:S(2)}) collective-permute-start(f32[1,1024]{1,0:T(1,128)S(1)} %slice_bitcast_fusion.2), channel_id=1, source_target_pairs={{0,4},{4,8},{8,12},{12,16},{16,20},{20,24},{24,28},{28,32},{32,36}... | collective-permute-start | bytes 12296 | tf_op jit(solution)/shard_map/ppermute | solution.py:33
  26.1 79.3 %copy-start.16 = (f32[1,1024]{1,0:T(1,128)}, f32[1,1024]{1,0:T(1,128)S(1)}, u32[]{:S(2)}) copy-start(f32[1,1024]{1,0:T(1,128)S(1)} %get-tuple-element.58) | copy-start | bytes 12292
  26.1 79.3 %copy-start.18 = (f32[1,1024]{1,0:T(1,128)}, f32[1,1024]{1,0:T(1,128)S(1)}, u32[]{:S(2)}) copy-start(f32[1,1024]{1,0:T(1,128)S(1)} %get-tuple-element.59) | copy-start | bytes 12292
  26.1 79.3 %copy-start.20 = (f32[1,1024]{1,0:T(1,128)}, f32[1,1024]{1,0:T(1,128)S(1)}, u32[]{:S(2)}) copy-start(f32[1,1024]{1,0:T(1,128)S(1)} %get-tuple-element.60) | copy-start | bytes 12292
  27.0 78.5 %copy-start.22 = (f32[1,1024]{1,0:T(1,128)}, f32[1,1024]{1,0:T(1,128)S(1)}, u32[]{:S(2)}) copy-start(f32[1,1024]{1,0:T(1,128)S(1)} %get-tuple-element.55) | copy-start | bytes 12292
  27.0 78.5 %copy-start.24 = (f32[1,1024]{1,0:T(1,128)}, f32[1,1024]{1,0:T(1,128)S(1)}, u32[]{:S(2)}) copy-start(f32[1,1024]{1,0:T(1,128)S(1)} %get-tuple-element.56) | copy-start | bytes 12292
  27.0 78.5 %copy-start.26 = (f32[1,1024]{1,0:T(1,128)}, f32[1,1024]{1,0:T(1,128)S(1)}, u32[]{:S(2)}) copy-start(f32[1,1024]{1,0:T(1,128)S(1)} %get-tuple-element.57) | copy-start | bytes 12292
  30.4 75.1 %copy-start.39 = (f32[128]{0:T(128)}, f32[128]{0:T(128)S(1)}, u32[]{:S(2)}) copy-start(f32[128]{0:T(128)S(1)} %pad_maximum_fusion.17) | copy-start | bytes 1540
  105.5 4.3 %copy-start.37 = (f32[1,1024]{1,0:T(1,128)}, f32[1,1024]{1,0:T(1,128)S(1)}, u32[]{:S(2)}) copy-start(f32[1,1024]{1,0:T(1,128)S(1)} %collective-permute-done.1) | copy-start | bytes 12292
  106.3 18.0 %collective-permute-start.2 = (f32[1,1024]{1,0:T(1,128)S(1)}, f32[1,1024]{1,0:T(1,128)S(1)}, u32[]{:S(2)}, u32[]{:S(2)}) collective-permute-start(f32[1,1024]{1,0:T(1,128)S(1)} %slice.515), channel_id=1, source_target_pairs={{4,0},{8,4},{12,8},{16,12},{20,16},{24,20},{28,24},{32,28},{36,32}... | collective-permute-start | bytes 12296 | tf_op jit(solution)/shard_map/ppermute | solution.py:33
  124.4 5.5 %copy-start.28 = (f32[1,1024]{1,0:T(1,128)}, f32[1,1024]{1,0:T(1,128)S(1)}, u32[]{:S(2)}) copy-start(f32[1,1024]{1,0:T(1,128)S(1)} %collective-permute-done.2) | copy-start | bytes 12292
  159.9 14.4 %copy-start.15 = (f32[3,1024]{1,0:T(4,128)S(1)}, f32[3,1024]{1,0:T(4,128)}, u32[]{:S(2)}) copy-start(f32[3,1024]{1,0:T(4,128)} %slice.446) | copy-start | bytes 36868
  168.3 9.2 %copy-start.13 = (f32[15,1024]{1,0:T(8,128)S(1)}, f32[15,1024]{1,0:T(8,128)}, u32[]{:S(2)}) copy-start(f32[15,1024]{1,0:T(8,128)} %slice.432) | copy-start | bytes 184324
  168.3 9.2 %copy-start.14 = (f32[15,1024]{1,0:T(8,128)S(1)}, f32[15,1024]{1,0:T(8,128)}, u32[]{:S(2)}) copy-start(f32[15,1024]{1,0:T(8,128)} %slice.430) | copy-start | bytes 184324
  168.9 8.4 %copy-start.36 = (f32[1,1024]{1,0:T(1,128)S(1)}, f32[1,1024]{1,0:T(1,128)}, u32[]{:S(2)}) copy-start(f32[1,1024]{1,0:T(1,128)} %slice.540) | copy-start | bytes 12292
  168.9 8.5 %copy-start.35 = (f32[1,1024]{1,0:T(1,128)S(1)}, f32[1,1024]{1,0:T(1,128)}, u32[]{:S(2)}) copy-start(f32[1,1024]{1,0:T(1,128)} %slice.518) | copy-start | bytes 12292
  168.9 8.6 %copy-start.34 = (f32[1,1024]{1,0:T(1,128)S(1)}, f32[1,1024]{1,0:T(1,128)}, u32[]{:S(2)}) copy-start(f32[1,1024]{1,0:T(1,128)} %slice.539) | copy-start | bytes 12292
  176.6 1.2 copy-start.33
  177.6 1.0 copy-start.32
  177.7 0.9 copy-start.31
  179.6 1.5 copy-start.10
  179.7 1.5 copy-start.11
  180.4 1.6 copy-start.30
  182.0 1.2 copy-start.29
  191.9 26.6 %all-to-all-start.1 = ((f32[64,2,1024]{2,1,0:T(2,128)}), f32[64,2,1024]{2,1,0:T(2,128)}, u32[]{:S(2)}, u32[]{:S(2)}) async-start(f32[64,2,1024]{2,1,0:T(2,128)} %broadcast_in_dim.37), calls=%async_computation.1 | async-start | bytes 1048576 | tf_op jit(solution)/shard_map/all_to_all | solution.py:16
  201.1 186.7 %reduce-scatter.2.cloned.1.call-start = ((), (), s32[]{:S(2)}) async-start(), calls=%async_computation.5 | async-start | bytes 12779520 | tf_op jit(solution)/shard_map/reduce_scatter | solution.py:139
  201.3 1.2 copy-start.1
  201.3 1.4 copy-start.2
  202.7 1.2 copy-start.3
  220.4 0.7 copy-start.17
  220.4 0.7 copy-start.19
  220.4 0.7 copy-start.21
  220.4 0.7 copy-start.23
  220.4 0.7 copy-start.25
  220.4 0.7 copy-start.27
  220.5 0.7 copy-start.38
  220.5 0.7 copy-start.40
  222.2 0.7 copy-start.4
  222.2 0.8 copy-start.6
  222.2 0.9 copy-start.8
  229.5 62.6 %copy-start.5 = (bf16[128,1024]{1,0:T(8,128)(2,1)S(1)}, bf16[128,1024]{1,0:T(8,128)(2,1)}, u32[]{:S(2)}) copy-start(bf16[128,1024]{1,0:T(8,128)(2,1)} %copy-done.4) | copy-start | bytes 786436
  229.5 62.6 %copy-start.7 = (bf16[128,1024]{1,0:T(8,128)(2,1)S(1)}, bf16[128,1024]{1,0:T(8,128)(2,1)}, u32[]{:S(2)}) copy-start(bf16[128,1024]{1,0:T(8,128)(2,1)} %copy-done.6) | copy-start | bytes 786436
  229.5 62.6 %copy-start.9 = (bf16[128,1024]{1,0:T(8,128)(2,1)S(1)}, bf16[128,1024]{1,0:T(8,128)(2,1)}, u32[]{:S(2)}) copy-start(bf16[128,1024]{1,0:T(8,128)(2,1)} %copy-done.8) | copy-start | bytes 786436
  389.3 9.2 %all-to-all-start.2 = ((bf16[4,48,256]{2,1,0:T(8,128)(2,1)}), bf16[4,48,256]{2,1,0:T(8,128)(2,1)S(1)}, u32[]{:S(2)}, u32[]{:S(2)}) async-start(bf16[4,48,256]{2,1,0:T(8,128)(2,1)} %bitcast.45), calls=%async_computation.3 | async-start | bytes 196608 | tf_op jit(solution)/shard_map/all_to_all | solution.py:82
Sparse Core Ops, SparseCore 0:
  17.8 82.6 all-gather.1
  229.6 158.0 reduce-scatter.1
where the time goes:
time: 410 us; the launch traced here: 406 us
  waiting for transfers between devices  176 us (43%)
  local copies, waits for them, and re-layouts  75.4 us (18%)
  blocking collectives  71.5 us (17%)
  other arithmetic  30 us (7%)
  starting transfers between devices  21 us (5%)
  between operations  16.4 us (4%)
  matrix products  16 us (4%)
    reduce_scatter x1, waiting for transfers between devices, local(): lax.psum_scatter(lax.dot_general(grad_pre, feats, (((0,), (0,)), ((), ())...  91 us
    all_gather x1, waiting for transfers between devices, local(): full_weight = lax.all_gather(columns, SEQ, axis=0, tiled=True)  70.1 us
    psum x4, blocking collectives, by_axis(): return functools.reduce(lax.psum, axes, x)  62.5 us
    slice x49, local copies, waits for them, and re-layouts, local(): lax.associative_scan(compose, (factor, upstream), reverse=True, axis=0)  55.3 us
    all_to_all x1, waiting for transfers between devices, copy_for_each(): return lax.all_to_all(copies, axis, split_axis=0, concat_axis=0, tiled=True)  10.9 us
    mul x16, other arithmetic, compose(): return (later[0] * earlier[0], later[1] + later[0] * earlier[1])  10.4 us
    all_to_all x1, starting transfers between devices, copy_for_each(): return lax.all_to_all(copies, axis, split_axis=0, concat_axis=0, tiled=True)  9.17 us
    all_to_all x1, blocking collectives, copy_for_each(): return lax.all_to_all(copies, axis, split_axis=0, concat_axis=0, tiled=True)  8.96 us
  transfers between devices with their start and end apart: 7, of which 4 were waited for; matrix products, arithmetic and copies ran while one was open for 9% of the time, Pallas kernels for 0%

commit v1 on v0

v1 whole, which is shorter than its diff:
```python
import functools
import math

import jax
import jax.numpy as jnp
from jax import lax
from jax.experimental import pallas as pl
from jax.experimental.pallas import tpu as pltpu
from jax.sharding import Mesh
from jax.sharding import PartitionSpec as P

SEQ = ("z", "y", "c")
ALL = ("z", "y", "c", "x")
NZ, NY, NC, NX = 8, 4, 2, 4
T = 128
F = 1024
H = 1024
W = 128
UNIT = 16
CB = F // 4
FAR = 2.0
CHUNK = 32
BF = jnp.bfloat16
F32 = jnp.float32


def piece_route(k):
    route = []
    for s in range(NZ * NY * NC):
        unit = 3 * s + k
        hidden = unit % 64
        share = hidden // 8
        for x in range(NX):
            z, y, c, xx = hidden % 8, x, share // 4, share % 4
            route.append((s * NX + x, ((z * NY + y) * NC + c) * NX + xx))
    return route


def around(a, axis, k):
    n = lax.axis_size(axis)
    return lax.ppermute(a, axis, [(i, (i + k) % n) for i in range(n)])


def along(a, axis, n, k):
    return lax.ppermute(a, axis, [(i, i + k) for i in range(n) if 0 <= i + k < n])


def call(body, outs, args, scratch=(), name=None):
    vmem = pl.BlockSpec(memory_space=pltpu.VMEM)
    return pl.pallas_call(
        body,
        out_shape=[jax.ShapeDtypeStruct(s, d) for s, d in outs],
        in_specs=[pl.BlockSpec(memory_space=pltpu.SMEM)] + [vmem] * (len(args) - 1),
        out_specs=[vmem] * len(outs),
        scratch_shapes=list(scratch),
        name=name,
    )(*args)


def at(start, size, step):
    return pl.ds(pl.multiple_of(start, step), size)


def split2(v):
    high = v.astype(BF)
    return high, (v - high.astype(F32)).astype(BF)


MSG = F + 3 * 2 * W


def messages_body(idx, inputs, states, ids, grads, tail, *outs):
    first = (idx[0] == 0) & (idx[1] == 0) & (idx[2] == 0)
    row = lax.broadcasted_iota(jnp.int32, (T, W), 0)
    before = jnp.where(row == 0, tail[1:2, 0:W], pltpu.roll(ids[...], 1, 0))
    same = (before == ids[...]) & ((row > 0) | jnp.logical_not(first))
    for k in range(NX):
        to = lax.rem(idx[3] + k, NX)
        outs[k][:, 0:F] = inputs[...]
        for c in range(NC):
            lanes = at(c * 512 + to * W, W, W)
            prior = jnp.where(row == 0, tail[0:1, lanes], pltpu.roll(states[:, lanes], 1, 0))
            high, low = split2(jnp.where(same, prior, FAR))
            outs[k][:, F + c * W : F + (c + 1) * W] = high
            outs[k][:, F + (2 + c) * W : F + (3 + c) * W] = low
            outs[k][:, F + (4 + c) * W : F + (5 + c) * W] = grads[:, lanes]


def forward_body(idx, recur, bias, *refs):
    blocks, refs = refs[:8], refs[8:]
    parts, refs = refs[:4], refs[4:]
    az, ac, ar, pr, rp, loc, fac, ends, weight, pre, jac, upg = refs
    z, y, c, x = idx[0], idx[1], idx[2], idx[3]
    share = c * 4 + x
    for kz in range(NZ):
        unit = lax.rem(z - kz + NZ, NZ)
        turn = lax.rem(share * 8 + unit, 3)
        for g in range(3):
            src = at(kz * 48 + lax.rem(g + turn, 3) * UNIT, UNIT, UNIT)
            dst = at(g * W + unit * UNIT, UNIT, UNIT)
            for ky in range(NY):
                weight[lax.rem(y - ky + NY, NY), dst, :] = parts[ky][src, :]
    feats = jnp.concatenate([b[:, 0:F] for k in range(4) for b in (blocks[k], blocks[4 + k])], 0)
    rows = jnp.concatenate([weight[b] for b in range(4)], 1)
    pre[...] = lax.dot_general(feats, rows, (((1,), (1,)), ((), ())), preferred_element_type=F32)
    lanes = at(share * W, W, W)
    rz, rr, rc = (recur[g : g + 1, lanes] for g in range(3))
    bz, br, bc = (bias[g : g + 1, lanes] for g in range(3))
    for k in range(4):
        jac[k, 2 * T : 2 * T + 8, :] = jnp.ones((8, W), F32)
        for side in range(2):
            block = blocks[k + 4 * side]
            base = k * 256 + side * T
            half = lax.rem(c + side, 2) * T

            def step(i, carry, block=block, base=base, half=half, k=k):
                own = at(i * CHUNK, CHUNK, CHUNK)
                here = at(base + i * CHUNK, CHUNK, CHUNK)
                when = at(half + i * CHUNK, CHUNK, CHUNK)
                coded = block[own, at(F + c * W, W, W)].astype(F32) + block[
                    own, at(F + 2 * W + c * W, W, W)
                ].astype(F32)
                same = coded < 1.5
                prior = jnp.where(same, coded, 0.0)
                gz = jax.nn.sigmoid(pre[here, 0:W] + rz * prior + bz)
                gr = jax.nn.sigmoid(pre[here, W : 2 * W] + rr * prior + br)
                reset = gr * prior
                gc = jnp.tanh(pre[here, 2 * W : 3 * W] + rc * reset + bc)
                keep = 1.0 - gz
                fz = (gc - prior) * gz * keep
                fc = gz * (1.0 - gc * gc)
                side_r = prior * gr * (1.0 - gr)
                value = keep + fz * rz + fc * rc * (gr + side_r * rr)
                jac[k, when, :] = jnp.where(same, value, 0.0)
                upg[k, when, :] = block[own, at(F + 4 * W + c * W, W, W)].astype(F32)
                az[here, :] = fz
                ac[here, :] = fc
                ar[here, :] = fc * rc * side_r
                pr[here, :] = prior
                rp[here, :] = reset
                return carry

            lax.fori_loop(0, T // CHUNK, step, 0)
    sub = lax.broadcasted_iota(jnp.int32, (8, 8, W), 1)
    for k in range(4):
        for n in range(4):
            f = jac[k, n * 64 + 1 : n * 64 + 65, :].reshape(8, 8, W)
            a = upg[k, n * 64 : n * 64 + 64, :].reshape(8, 8, W)
            for d in (1, 2, 4):
                valid = sub < 8 - d
                a = jnp.where(valid, a + f * pltpu.roll(a, 8 - d, 1), a)
                f = jnp.where(valid, f * pltpu.roll(f, 8 - d, 1), f)
            loc[k * 256 + n * 64 : k * 256 + n * 64 + 64, :] = a.reshape(64, W)
            fac[k * 256 + n * 64 : k * 256 + n * 64 + 64, :] = f.reshape(64, W)

    def chain(i, carry):
        new = []
        for k in range(4):
            a0, f0 = carry[2 * k], carry[2 * k + 1]
            here = at(k * 256 + (31 - i) * 8, 8, 8)
            f = fac[here, :]
            a = loc[here, :] + f * a0
            f = f * f0
            loc[here, :] = a
            fac[here, :] = f
            new += [jnp.broadcast_to(a[0:1], (8, W)), jnp.broadcast_to(f[0:1], (8, W))]
        return tuple(new)

    start = (jnp.zeros((8, W), F32), jnp.ones((8, W), F32)) * 4
    last = lax.fori_loop(0, 32, chain, start, unroll=4)
    for k in range(4):
        ends[k : k + 1, :] = jac[k, 0:1, :] * last[2 * k + 1][0:1]
        ends[4 + k : 5 + k, :] = jac[k, 0:1, :] * last[2 * k][0:1]


def backward_body(idx, one, two, az, ac, ar, pr, rp, loc, fac, *refs):
    blocks, refs = refs[:8], refs[8:]
    grads, own, own_stats, *rest = refs
    sent, total = rest[:3], rest[3]
    y, c = idx[1], idx[2]
    enter = one[4:8, :] + one[0:4, :] * two[4:8, :]
    sums = (jnp.zeros((8, W), F32),) * 6
    for k in range(4):
        came = enter[k : k + 1]
        for side in range(2):
            base = k * 256 + side * T
            half = k * 256 + lax.rem(c + side, 2) * T

            def step(i, sums, base=base, half=half, came=came):
                here = at(base + i * CHUNK, CHUNK, CHUNK)
                when = at(half + i * CHUNK, CHUNK, CHUNK)
                adj = loc[when, :] + fac[when, :] * came
                gz, gc, gr = adj * az[here, :], adj * ac[here, :], adj * ar[here, :]
                prior = pr[here, :]
                grads[here, 0:W] = gz.astype(BF)
                grads[here, W : 2 * W] = gr.astype(BF)
                grads[here, 2 * W : 3 * W] = gc.astype(BF)
                terms = (gz, gr, gc, gz * prior, gr * prior, gc * rp[here, :])
                return tuple(s + t.reshape(CHUNK // 8, 8, W).sum(0) for s, t in zip(sums, terms))

            sums = lax.fori_loop(0, T // CHUNK, step, sums)
    own_stats[...] = jnp.zeros((8, W), F32)
    for n in range(6):
        own_stats[n : n + 1, :] = jnp.sum(sums[n], 0, keepdims=True)
    feats = jnp.concatenate([b[:, 0:F] for k in range(4) for b in (blocks[k], blocks[4 + k])], 0)
    whole = lax.dot_general(
        grads[...], feats, (((0,), (0,)), ((), ())), preferred_element_type=F32
    )
    for b in range(4):
        total[b] = whole[:, b * CB : (b + 1) * CB]
    own[...] = total[y]
    for k in range(1, 4):
        sent[k - 1][0:384, :] = total[lax.rem(y + k, NY)].astype(BF)
        put_stats(sent[k - 1], 384, own_stats[...])


def put_stats(ref, row, stats):
    pair = jnp.concatenate([stats, jnp.zeros_like(stats)], 0)
    high, low = split2(pair)
    ref[row : row + 16, 0:W] = high
    ref[row : row + 16, W : 2 * W] = low


def get_stats(ref, row):
    both = ref[row : row + 16, 0:W].astype(F32) + ref[row : row + 16, W : 2 * W].astype(F32)
    return both[0:8]


def input_grad_body(idx, grads, weight, mine, other):
    rows = jnp.concatenate([weight[b] for b in range(4)], 1)
    for k in range(4):
        part = jnp.dot(grads[k * 256 : k * 256 + 256, :], rows, preferred_element_type=F32)
        mine[k] = part[0:T]
        other[k] = part[T : 2 * T].astype(BF)


def core_sum_body(idx, mine, other, own, *sent):
    own[...] = mine[0] + other[0].astype(F32)
    for k in range(1, 4):
        sent[k - 1][...] = (mine[k] + other[k].astype(F32)).astype(BF)


def block_sum_body(idx, own, *refs):
    *came, out = refs
    out[...] = (own[...] + sum(r[...].astype(F32) for r in came)).astype(BF)


def y_sum_body(idx, own, own_stats, *refs):
    came, refs = refs[:3], refs[3:]
    piece, stats, *sent = refs[:9]
    total = refs[9]
    z = idx[0]
    total[...] = own[...] + sum(r[0:384, :].astype(F32) for r in came)
    stats[...] = own_stats[...] + sum(get_stats(r, 384) for r in came)
    for k in range(8):
        unit = lax.rem(z + k, NZ)
        for g in range(3):
            rows = total[at(g * W + unit * UNIT, UNIT, UNIT), :]
            if k == 0:
                piece[g * UNIT : (g + 1) * UNIT, :] = rows
            else:
                sent[k - 1][g * UNIT : (g + 1) * UNIT, :] = rows.astype(BF)
        if k:
            put_stats(sent[k - 1], 48, stats[...])


def z_sum_body(scale, idx, piece, stats, *refs):
    came, refs = refs[:7], refs[7:]
    outs, stats_out, total = refs[:3], refs[3], refs[4]
    z, c, x = idx[0], idx[2], idx[3]
    total[...] = (piece[...] + sum(r[0:48, :].astype(F32) for r in came)) * scale
    stats_out[...] = (stats[...] + sum(get_stats(r, 48) for r in came)) * scale
    hidden = (c * 4 + x) * 8 + z
    for k in range(3):
        gate = lax.rem(k + 3 - lax.rem(hidden, 3), 3)
        outs[k][...] = total[at(gate * UNIT, UNIT, UNIT), :]


def stats_body(idx, *refs):
    came, out, table = refs[:4], refs[4], refs[5]
    c, x = idx[2], idx[3]
    for k in range(4):
        for side in range(2):
            place = lax.rem(c + side, 2) * 4 + lax.rem(x - k + 4, 4)
            table[place] = came[k][side * 8 : side * 8 + 8, :]
    for n in range(8):
        out[:, n * W : (n + 1) * W] = table[n][0:6]


def local(inputs, weight_t, states, doc_ids, recur, bias, out_grad):
    device = lax.axis_index(ALL)
    sizes = jnp.array([NZ, NY, NC, NX], jnp.int32)
    idx = (device // jnp.array([32, 8, 4, 1], jnp.int32)) % sizes
    states, out_grad = states[0], out_grad[0]

    pieces = [
        lax.ppermute(weight_t[k * UNIT : (k + 1) * UNIT], ALL, piece_route(k)) for k in range(3)
    ]
    pieces = jnp.concatenate(pieces, 0)
    column = jnp.concatenate([pieces] + [around(pieces, "z", k) for k in range(1, NZ)], 0)
    parts = [column] + [around(column, "y", k) for k in range(1, NY)]

    ids = doc_ids[0].astype(F32)
    tail = jnp.concatenate([states[-1:], jnp.broadcast_to(ids[-1:], (1, H))], 0)
    tail = along(tail, SEQ, NZ * NY * NC, 1)
    ids = jnp.broadcast_to(ids[:, None], (T, W))
    sent = call(
        messages_body,
        [((T, MSG), BF)] * 4,
        (idx, inputs[0], states, ids, out_grad, tail),
        name="messages",
    )
    mine = [sent[0]] + [around(sent[k], "x", k) for k in range(1, NX)]
    other = [around(m, "c", 1) for m in mine]
    blocks = mine + other

    tokens = ((8 * T, W), F32)
    *kept, ends, weight = call(
        forward_body,
        [tokens] * 7 + [((8, W), F32), ((4, 3 * W, CB), BF)],
        (idx, recur, bias, *blocks, *parts),
        [
            pltpu.VMEM((8 * T, 3 * W), F32),
            pltpu.VMEM((4, 2 * T + 8, W), F32),
            pltpu.VMEM((4, 2 * T, W), F32),
        ],
        name="forward",
    )
    one = along(ends, ("z", "y"), NZ * NY, -1)
    two = along(ends, ("z", "y"), NZ * NY, -2)
    grads, own, stats, *sent = call(
        backward_body,
        [((8 * T, 3 * W), BF), ((3 * W, CB), F32), ((8, W), F32)] + [((400, CB), BF)] * 3,
        (idx, one, two, *kept, *blocks),
        [pltpu.VMEM((4, 3 * W, CB), F32)],
        name="backward",
    )
    came = [around(sent[k - 1], "y", k) for k in range(1, NY)]

    mine, other = call(
        input_grad_body,
        [((4, T, F), F32), ((4, T, F), BF)],
        (idx, grads, weight),
        name="input_grad",
    )
    other = around(other, "c", 1)
    block, *back = call(
        core_sum_body,
        [((T, F), F32)] + [((T, F), BF)] * 3,
        (idx, mine, other),
        name="core_sum",
    )
    back = [around(back[k - 1], "x", NX - k) for k in range(1, NX)]

    piece, stats, *sent = call(
        y_sum_body,
        [((48, CB), F32), ((8, W), F32)] + [((64, CB), BF)] * 7,
        (idx, own, stats, *came),
        [pltpu.VMEM((3 * W, CB), F32)],
        name="y_sum",
    )
    came = [around(sent[k - 1], "z", k) for k in range(1, NZ)]
    scale = 1.0 / math.sqrt(inputs.shape[0] * T * NZ * NY * NC * NX)
    *pieces, stats = call(
        functools.partial(z_sum_body, scale),
        [((UNIT, CB), F32)] * 3 + [((8, W), F32)],
        (idx, piece, stats, *came),
        [pltpu.VMEM((48, CB), F32)],
        name="z_sum",
    )
    pieces = [
        lax.ppermute(pieces[k], ALL, [(b, a) for a, b in piece_route(k)]) for k in range(3)
    ]
    weight_grad = jnp.concatenate(pieces, 0)
    stats = jnp.concatenate([stats, around(stats, "c", 1)], 0)
    stats = [stats] + [around(stats, "x", k) for k in range(1, NX)]
    (param_grad,) = call(
        stats_body,
        [((6, H), F32)],
        (idx, *stats),
        [pltpu.VMEM((8, 8, W), F32)],
        name="stats",
    )
    (input_grad,) = call(block_sum_body, [((T, F), BF)], (idx, block, *back), name="block_sum")
    return input_grad[None], weight_grad, param_grad


def solution(mesh):
    torus = Mesh(mesh.devices.reshape(NZ, NY, NC, NX), ALL)
    in_specs = (
        P("x", SEQ, None),
        P(SEQ, "x"),
        P("x", SEQ, None),
        P("x", SEQ),
        P(),
        P(),
        P("x", SEQ, None),
    )
    out_specs = (P("x", SEQ, None), P(SEQ, "x"), P())
    return jax.shard_map(local, mesh=torus, in_specs=in_specs, out_specs=out_specs, check_vma=False)
```

time: 410 us -> 217 us (0.53)
  the two profiles are of different devices: /device:TPU:2 before, /device:TPU:5 now
where the time goes in v1:
time: 217 us; the launch traced here: 216 us
  starting transfers between devices  95 us (44%)
  waiting for transfers between devices  77 us (35%)
  Pallas kernels  30.3 us (14%)
  local copies, waits for them, and re-layouts  10.1 us (5%)
  other arithmetic  2.75 us (1%)
    ppermute x35, waiting for transfers between devices, around(): return lax.ppermute(a, axis, [(i, (i + k) % n) for i in range(n)])  57 us
    ppermute x35, starting transfers between devices, around(): return lax.ppermute(a, axis, [(i, (i + k) % n) for i in range(n)])  53.9 us
    pallas_call x9, Pallas kernels, call(): pl.pallas_call(body, out_shape=[jax.ShapeDtypeStruct(s, d) for s, d in ou...  30.3 us
    ppermute x3, starting transfers between devices, local(): lax.ppermute(weight_t[k * UNIT:(k + 1) * UNIT], ALL, piece_route(k))  19.1 us
    ppermute x3, starting transfers between devices, local(): lax.ppermute(pieces[k], ALL, [(b, a) for a, b in piece_route(k)])  15.9 us
    ppermute x3, waiting for transfers between devices, local(): lax.ppermute(pieces[k], ALL, [(b, a) for a, b in piece_route(k)])  9.46 us
    ppermute x3, waiting for transfers between devices, local(): lax.ppermute(weight_t[k * UNIT:(k + 1) * UNIT], ALL, piece_route(k))  7.12 us
    unnamed x79, local copies, waits for them, and re-layouts  6.7 us
  transfers between devices with their start and end apart: 44, of which 15 were waited for; matrix products, arithmetic and copies ran while one was open for 3% of the time, Pallas kernels for 5%

profile of v1, /device:TPU:5, one launch (start us, length us, event | category | flops | bytes accessed | tf_op | source)
XLA Modules:
  0.0 216.3 jit_solution(14749476093153220174)
XLA Ops:
  1.4 9.4 %collective-permute-start.8 = (bf16[16,256]{1,0:T(8,128)(2,1)S(1)}, bf16[16,256]{1,0:T(8,128)(2,1)S(1)}, u32[]{:S(2)}, u32[]{:S(2)}) collective-permute-start(bf16[16,256]{1,0:T(8,128)(2,1)S(1)} %get-tuple-element.80), channel_id=1, source_target_pairs={{0,0},{1,8},{2,16},{3,24},{4,96},{5,104},{6,112},{7,120},{8,192},{... | collective-permute-start | bytes 24584 | tf_op jit(solution)/shard_map/ppermute | solution.py:297
  13.4 3.5 %collective-permute-start = (f32[2,1024]{1,0:T(2,128)S(1)}, f32[2,1024]{1,0:T(2,128)S(1)}, u32[]{:S(2)}, u32[]{:S(2)}) collective-permute-start(f32[2,1024]{1,0:T(2,128)S(1)} %concatenate.16), channel_id=1, source_target_pairs={{0,4},{4,8},{8,12},{12,16},{16,20},{20,24},{24,28},{28,32},{32,36}... | collective-permute-start | bytes 24584 | tf_op jit(solution)/shard_map/ppermute | solution.py:45
  17.0 3.8 %collective-permute-start.10 = (bf16[16,256]{1,0:T(8,128)(2,1)S(1)}, bf16[16,256]{1,0:T(8,128)(2,1)S(1)}, u32[]{:S(2)}, u32[]{:S(2)}) collective-permute-start(bf16[16,256]{1,0:T(8,128)(2,1)S(1)} %get-tuple-element.79), channel_id=1, source_target_pairs={{0,64},{1,72},{2,80},{3,88},{4,160},{5,168},{6,176},{7,184},{8,1},... | collective-permute-start | bytes 24584 | tf_op jit(solution)/shard_map/ppermute | solution.py:297
  20.7 6.0 %collective-permute-start.9 = (bf16[16,256]{1,0:T(8,128)(2,1)S(1)}, bf16[16,256]{1,0:T(8,128)(2,1)S(1)}, u32[]{:S(2)}, u32[]{:S(2)}) collective-permute-start(bf16[16,256]{1,0:T(8,128)(2,1)S(1)} %get-tuple-element.81), channel_id=1, source_target_pairs={{0,32},{1,40},{2,48},{3,56},{4,128},{5,136},{6,144},{7,152},{8,224... | collective-permute-start | bytes 24584 | tf_op jit(solution)/shard_map/ppermute | solution.py:297
  26.7 7.1 %collective-permute-done.9 = bf16[16,256]{1,0:T(8,128)(2,1)S(1)} collective-permute-done((bf16[16,256]{1,0:T(8,128)(2,1)S(1)}, bf16[16,256]{1,0:T(8,128)(2,1)S(1)}, u32[]{:S(2)}, u32[]{:S(2)}) %collective-permute-start.9) | collective-permute-done | bytes 8224 | tf_op jit(solution)/shard_map/ppermute | solution.py:297
  33.9 1.5 and_select_fusion.idx
  35.4 2.7 %collective-permute-start.17 = (bf16[48,256]{1,0:T(8,128)(2,1)S(1)}, bf16[48,256]{1,0:T(8,128)(2,1)S(1)}, u32[]{:S(2)}, u32[]{:S(2)}) collective-permute-start(bf16[48,256]{1,0:T(8,128)(2,1)S(1)} %get-tuple-element.82), channel_id=1, source_target_pairs={{0,224},{32,0},{64,32},{96,64},{128,96},{160,128},{192,160},{224,1... | collective-permute-start | bytes 73736 | tf_op jit(solution)/shard_map/ppermute | solution.py:41
  38.1 5.3 %collective-permute-start.14 = (bf16[48,256]{1,0:T(8,128)(2,1)S(1)}, bf16[48,256]{1,0:T(8,128)(2,1)S(1)}, u32[]{:S(2)}, u32[]{:S(2)}) collective-permute-start(bf16[48,256]{1,0:T(8,128)(2,1)S(1)} %get-tuple-element.82), channel_id=1, source_target_pairs={{0,128},{32,160},{64,192},{96,224},{128,0},{160,32},{192,64},{224,... | collective-permute-start | bytes 73736 | tf_op jit(solution)/shard_map/ppermute | solution.py:41
  44.2 2.5 %messages.1 = (bf16[128,1792]{1,0:T(8,128)(2,1)}, bf16[128,1792]{1,0:T(8,128)(2,1)}, bf16[128,1792]{1,0:T(8,128)(2,1)}, bf16[128,1792]{1,0:T(8,128)(2,1)}) custom-call(s32[4]{0:T(128)} %and_select_fusion.idx, bf16[128,1024]{1,0:T(8,128)(2,1)} %bitcast.10, f32[128,1024]{1,0:T(8,128)} %bitcast.9, f32[128,128]{1,0:T(8,128)} %broadcast_in_dim.4.ids, ...), custom_call_target="tpu_custom_call" | custom-call | tf_op jit(solution)/shard_map/messages/pallas_call | solution.py:50
  46.7 4.9 %collective-permute-done.12 = bf16[48,256]{1,0:T(8,128)(2,1)S(1)} collective-permute-done((bf16[48,256]{1,0:T(8,128)(2,1)S(1)}, bf16[48,256]{1,0:T(8,128)(2,1)S(1)}, u32[]{:S(2)}, u32[]{:S(2)}) %collective-permute-start.12) | collective-permute-done | bytes 24608 | tf_op jit(solution)/shard_map/ppermute | solution.py:41
  51.6 5.7 %collective-permute-done.13 = bf16[48,256]{1,0:T(8,128)(2,1)S(1)} collective-permute-done((bf16[48,256]{1,0:T(8,128)(2,1)S(1)}, bf16[48,256]{1,0:T(8,128)(2,1)S(1)}, u32[]{:S(2)}, u32[]{:S(2)}) %collective-permute-start.13) | collective-permute-done | bytes 24608 | tf_op jit(solution)/shard_map/ppermute | solution.py:41
  57.4 1.4 collective-permute-start.3
  58.9 2.0 collective-permute-start.20
  60.9 7.3 %collective-permute-start.4 = (bf16[128,1792]{1,0:T(8,128)(2,1)}, bf16[128,1792]{1,0:T(8,128)(2,1)S(1)}, u32[]{:S(2)}, u32[]{:S(2)}) collective-permute-start(bf16[128,1792]{1,0:T(8,128)(2,1)} %get-tuple-element.41.refs_0_), channel_id=1, source_target_pairs={{0,4},{4,0},{1,5},{5,1},{2,6},{6,2},{3,7},{7,3},{8,12},{12,8},{9,1... | collective-permute-start | bytes 1376264 | tf_op jit(solution)/shard_map/ppermute | solution.py:41
  68.3 9.9 %collective-permute-done.1.refs_1_ = bf16[128,1792]{1,0:T(8,128)(2,1)S(1)} collective-permute-done((bf16[128,1792]{1,0:T(8,128)(2,1)}, bf16[128,1792]{1,0:T(8,128)(2,1)S(1)}, u32[]{:S(2)}, u32[]{:S(2)}) %collective-permute-start.1) | collective-permute-done | bytes 458784 | tf_op jit(solution)/shard_map/ppermute | solution.py:41
  78.2 2.1 collective-permute-start.5
  80.4 1.7 collective-permute-start.7
  82.1 1.3 collective-permute-start.19
  83.4 6.6 %collective-permute-done.19.refs_10_ = bf16[384,256]{1,0:T(8,128)(2,1)S(1)} collective-permute-done((bf16[384,256]{1,0:T(8,128)(2,1)S(1)}, bf16[384,256]{1,0:T(8,128)(2,1)S(1)}, u32[]{:S(2)}, u32[]{:S(2)}) %collective-permute-start.19) | collective-permute-done | bytes 196640 | tf_op jit(solution)/shard_map/ppermute | solution.py:41
  90.0 6.7 %collective-permute-done.18.refs_9_ = bf16[384,256]{1,0:T(8,128)(2,1)S(1)} collective-permute-done((bf16[384,256]{1,0:T(8,128)(2,1)S(1)}, bf16[384,256]{1,0:T(8,128)(2,1)S(1)}, u32[]{:S(2)}, u32[]{:S(2)}) %collective-permute-start.18) | collective-permute-done | bytes 196640 | tf_op jit(solution)/shard_map/ppermute | solution.py:41
  98.9 7.6 %forward.1 = (f32[1024,128]{1,0:T(8,128)}, f32[1024,128]{1,0:T(8,128)}, f32[1024,128]{1,0:T(8,128)}, f32[1024,128]{1,0:T(8,128)}, f32[1024,128]{1,0:T(8,128)}, /...) custom-call(s32[4]{0:T(128)} %and_select_fusion.idx, ...), custom_call_target="tpu_custom_call" | custom-call | tf_op jit(solution)/shard_map/forward/pallas_call | solution.py:50
  109.1 3.5 %collective-permute-done.22.two = f32[8,128]{1,0:T(8,128)S(1)} collective-permute-done((f32[8,128]{1,0:T(8,128)}, f32[8,128]{1,0:T(8,128)S(1)}, u32[]{:S(2)}, u32[]{:S(2)}) %collective-permute-start.22) | collective-permute-done | bytes 4128 | tf_op jit(solution)/shard_map/ppermute | solution.py:45
  113.2 5.8 %backward.1 = (bf16[1024,384]{1,0:T(8,128)(2,1)}, f32[384,256]{1,0:T(8,128)}, f32[8,128]{1,0:T(8,128)}, bf16[400,256]{1,0:T(8,128)(2,1)}, bf16[400,256]{1,0:T(8,128)(2,1)}, /*index=5*/bf16[400,256]{1,0:T(8,128)(2,1)}) custom-call(s32[4]{0:T(128)} %and_select_fusion.idx, f32[8,128]{1,0:T(8,128)} %copy-done.31, f32[8,128]{1,0:T(8,128)} %copy-done.30, ...), custom_call_target="tpu_custom_call" | custom-call | tf_op jit(solution)/shard_map/backward/pallas_call | solution.py:50
  119.0 4.2 %input_grad.1 = (f32[4,128,1024]{2,1,0:T(8,128)}, bf16[4,128,1024]{2,1,0:T(8,128)(2,1)}) custom-call(s32[4]{0:T(128)} %and_select_fusion.idx, bf16[1024,384]{1,0:T(8,128)(2,1)} %get-tuple-element.53.grads, bf16[4,384,256]{2,1,0:T(8,128)(2,1)} %get-tuple-element.54.weight), custom_call_target="tpu_custom_call" | custom-call | tf_op jit(solution)/shard_map/input_grad/pallas_call | solution.py:50
  123.2 3.0 %collective-permute-start.23 = (bf16[4,128,1024]{2,1,0:T(8,128)(2,1)}, bf16[4,128,1024]{2,1,0:T(8,128)(2,1)S(1)}, u32[]{:S(2)}, u32[]{:S(2)}) collective-permute-start(bf16[4,128,1024]{2,1,0:T(8,128)(2,1)} %get-tuple-element.56), channel_id=1, source_target_pairs={{0,4},{4,0},{1,5},{5,1},{2,6},{6,2},{3,7},{7,3},{8,12},{12,8},{9,1... | collective-permute-start | bytes 3145736 | tf_op jit(solution)/shard_map/ppermute | solution.py:41
  126.2 1.6 collective-permute-start.27
  127.8 3.6 %collective-permute-start.28 = (bf16[400,256]{1,0:T(8,128)(2,1)}, bf16[400,256]{1,0:T(8,128)(2,1)S(1)}, u32[]{:S(2)}, u32[]{:S(2)}) collective-permute-start(bf16[400,256]{1,0:T(8,128)(2,1)} %get-tuple-element.64), channel_id=1, source_target_pairs={{0,16},{8,24},{16,0},{24,8},{1,17},{9,25},{17,1},{25,9},{2,18},{10... | collective-permute-start | bytes 614408 | tf_op jit(solution)/shard_map/ppermute | solution.py:41
  131.9 3.9 %collective-permute-done.27.refs_0_ = bf16[400,256]{1,0:T(8,128)(2,1)S(1)} collective-permute-done((bf16[400,256]{1,0:T(8,128)(2,1)}, bf16[400,256]{1,0:T(8,128)(2,1)S(1)}, u32[]{:S(2)}, u32[]{:S(2)}) %collective-permute-start.27) | collective-permute-done | bytes 204832 | tf_op jit(solution)/shard_map/ppermute | solution.py:41
  135.8 5.3 %collective-permute-done.28.refs_1_ = bf16[400,256]{1,0:T(8,128)(2,1)S(1)} collective-permute-done((bf16[400,256]{1,0:T(8,128)(2,1)}, bf16[400,256]{1,0:T(8,128)(2,1)S(1)}, u32[]{:S(2)}, u32[]{:S(2)}) %collective-permute-start.28) | collective-permute-done | bytes 204832 | tf_op jit(solution)/shard_map/ppermute | solution.py:41
  141.9 2.1 y_sum.1
  143.9 1.7 collective-permute-start.30
  146.6 4.5 %collective-permute-start.33 = (bf16[64,256]{1,0:T(8,128)(2,1)}, bf16[64,256]{1,0:T(8,128)(2,1)S(1)}, u32[]{:S(2)}, u32[]{:S(2)}) collective-permute-start(bf16[64,256]{1,0:T(8,128)(2,1)} %get-tuple-element.71), channel_id=1, source_target_pairs={{0,128},{32,160},{64,192},{96,224},{128,0},{160,32},{192,64},{224,... | collective-permute-start | bytes 98312 | tf_op jit(solution)/shard_map/ppermute | solution.py:41
  151.2 2.9 %collective-permute-start.35 = (bf16[64,256]{1,0:T(8,128)(2,1)}, bf16[64,256]{1,0:T(8,128)(2,1)S(1)}, u32[]{:S(2)}, u32[]{:S(2)}) collective-permute-start(bf16[64,256]{1,0:T(8,128)(2,1)} %get-tuple-element.73), channel_id=1, source_target_pairs={{0,192},{32,224},{64,0},{96,32},{128,64},{160,96},{192,128},{224,1... | collective-permute-start | bytes 98312 | tf_op jit(solution)/shard_map/ppermute | solution.py:41
  156.2 2.5 %collective-permute-done.35.refs_5_ = bf16[64,256]{1,0:T(8,128)(2,1)S(1)} collective-permute-done((bf16[64,256]{1,0:T(8,128)(2,1)}, bf16[64,256]{1,0:T(8,128)(2,1)S(1)}, u32[]{:S(2)}, u32[]{:S(2)}) %collective-permute-start.35) | collective-permute-done | bytes 32800 | tf_op jit(solution)/shard_map/ppermute | solution.py:41
  159.4 1.6 z_sum.1
  160.9 2.8 %collective-permute-start.40 = (f32[8,128]{1,0:T(8,128)}, f32[8,128]{1,0:T(8,128)S(1)}, u32[]{:S(2)}, u32[]{:S(2)}) collective-permute-start(f32[8,128]{1,0:T(8,128)} %get-tuple-element.78), channel_id=1, source_target_pairs={{0,4},{4,0},{1,5},{5,1},{2,6},{6,2},{3,7},{7,3},{8,12},{12,8},{9,1... | collective-permute-start | bytes 12296 | tf_op jit(solution)/shard_map/ppermute | solution.py:41
  165.4 3.0 %core_sum.1 = (f32[128,1024]{1,0:T(8,128)}, bf16[128,1024]{1,0:T(8,128)(2,1)}, bf16[128,1024]{1,0:T(8,128)(2,1)}, bf16[128,1024]{1,0:T(8,128)(2,1)}) custom-call(s32[4]{0:T(128)} %and_select_fusion.idx, f32[4,128,1024]{2,1,0:T(8,128)} %get-tuple-element.55.mine, bf16[4,128,1024]{2,1,0:T(8,128)(2,1)} %copy-done.7), custom_call_target="tpu_custom_call" | custom-call | tf_op jit(solution)/shard_map/core_sum/pallas_call | solution.py:50
  168.9 3.0 %collective-permute-start.25 = (bf16[128,1024]{1,0:T(8,128)(2,1)}, bf16[128,1024]{1,0:T(8,128)(2,1)S(1)}, u32[]{:S(2)}, u32[]{:S(2)}) collective-permute-start(bf16[128,1024]{1,0:T(8,128)(2,1)} %get-tuple-element.59), channel_id=1, source_target_pairs={{0,2},{1,3},{2,0},{3,1},{4,6},{5,7},{6,4},{7,5},{8,10},{9,11},{10,... | collective-permute-start | bytes 786440 | tf_op jit(solution)/shard_map/ppermute | solution.py:41
  172.0 1.5 collective-permute-start.43
  174.7 8.2 %collective-permute-done.43.refs_3_ = f32[16,128]{1,0:T(8,128)S(1)} collective-permute-done((f32[16,128]{1,0:T(8,128)S(1)}, f32[16,128]{1,0:T(8,128)S(1)}, u32[]{:S(2)}, u32[]{:S(2)}) %collective-permute-start.43) | collective-permute-done | bytes 8224 | tf_op jit(solution)/shard_map/ppermute | solution.py:41
  182.9 5.7 %collective-permute-start.37 = (f32[16,256]{1,0:T(8,128)S(1)}, f32[16,256]{1,0:T(8,128)S(1)}, u32[]{:S(2)}, u32[]{:S(2)}) collective-permute-start(f32[16,256]{1,0:T(8,128)S(1)} %copy-done.34), channel_id=1, source_target_pairs={{0,0},{8,1},{16,2},{24,3},{96,4},{104,5},{112,6},{120,7},{192,8},{... | collective-permute-start | bytes 49160 | tf_op jit(solution)/shard_map/ppermute | solution.py:372
  189.4 2.0 collective-permute-done.41.refs_1_
  191.5 8.3 %collective-permute-start.38 = (f32[16,256]{1,0:T(8,128)S(1)}, f32[16,256]{1,0:T(8,128)S(1)}, u32[]{:S(2)}, u32[]{:S(2)}) collective-permute-start(f32[16,256]{1,0:T(8,128)S(1)} %copy-done.33), channel_id=1, source_target_pairs={{32,0},{40,1},{48,2},{56,3},{128,4},{136,5},{144,6},{152,7},{224,8... | collective-permute-start | bytes 49160 | tf_op jit(solution)/shard_map/ppermute | solution.py:372
  199.8 1.9 collective-permute-start.39
  201.7 1.4 stats.1
  203.2 2.0 collective-permute-done.38
  205.2 7.4 %collective-permute-done.39 = f32[16,256]{1,0:T(8,128)S(1)} collective-permute-done((f32[16,256]{1,0:T(8,128)S(1)}, f32[16,256]{1,0:T(8,128)S(1)}, u32[]{:S(2)}, u32[]{:S(2)}) %collective-permute-start.39) | collective-permute-done | bytes 16416 | tf_op jit(solution)/shard_map/ppermute | solution.py:372
  214.2 2.1 block_sum.1
  (139 shorter events, 20.7 us)
Async XLA Ops:
  1.4 25.3 %collective-permute-start.8 = (bf16[16,256]{1,0:T(8,128)(2,1)S(1)}, bf16[16,256]{1,0:T(8,128)(2,1)S(1)}, u32[]{:S(2)}, u32[]{:S(2)}) collective-permute-start(bf16[16,256]{1,0:T(8,128)(2,1)S(1)} %get-tuple-element.80), channel_id=1, source_target_pairs={{0,0},{1,8},{2,16},{3,24},{4,96},{5,104},{6,112},{7,120},{8,192},{... | collective-permute-start | bytes 24584 | tf_op jit(solution)/shard_map/ppermute | solution.py:297
  13.4 24.7 %collective-permute-start = (f32[2,1024]{1,0:T(2,128)S(1)}, f32[2,1024]{1,0:T(2,128)S(1)}, u32[]{:S(2)}, u32[]{:S(2)}) collective-permute-start(f32[2,1024]{1,0:T(2,128)S(1)} %concatenate.16), channel_id=1, source_target_pairs={{0,4},{4,8},{8,12},{12,16},{16,20},{20,24},{24,28},{28,32},{32,36}... | collective-permute-start | bytes 24584 | tf_op jit(solution)/shard_map/ppermute | solution.py:45
  17.0 16.9 %collective-permute-start.10 = (bf16[16,256]{1,0:T(8,128)(2,1)S(1)}, bf16[16,256]{1,0:T(8,128)(2,1)S(1)}, u32[]{:S(2)}, u32[]{:S(2)}) collective-permute-start(bf16[16,256]{1,0:T(8,128)(2,1)S(1)} %get-tuple-element.79), channel_id=1, source_target_pairs={{0,64},{1,72},{2,80},{3,88},{4,160},{5,168},{6,176},{7,184},{8,1},... | collective-permute-start | bytes 24584 | tf_op jit(solution)/shard_map/ppermute | solution.py:297
  20.7 13.1 %collective-permute-start.9 = (bf16[16,256]{1,0:T(8,128)(2,1)S(1)}, bf16[16,256]{1,0:T(8,128)(2,1)S(1)}, u32[]{:S(2)}, u32[]{:S(2)}) collective-permute-start(bf16[16,256]{1,0:T(8,128)(2,1)S(1)} %get-tuple-element.81), channel_id=1, source_target_pairs={{0,32},{1,40},{2,48},{3,56},{4,128},{5,136},{6,144},{7,152},{8,224... | collective-permute-start | bytes 24584 | tf_op jit(solution)/shard_map/ppermute | solution.py:297
  33.8 12.8 %collective-permute-start.11 = (bf16[48,256]{1,0:T(8,128)(2,1)S(1)}, bf16[48,256]{1,0:T(8,128)(2,1)S(1)}, u32[]{:S(2)}, u32[]{:S(2)}) collective-permute-start(bf16[48,256]{1,0:T(8,128)(2,1)S(1)} %get-tuple-element.82), channel_id=1, source_target_pairs={{0,32},{32,64},{64,96},{96,128},{128,160},{160,192},{192,224},{224... | collective-permute-start | bytes 73736 | tf_op jit(solution)/shard_map/ppermute | solution.py:41
  35.4 23.5 %collective-permute-start.17 = (bf16[48,256]{1,0:T(8,128)(2,1)S(1)}, bf16[48,256]{1,0:T(8,128)(2,1)S(1)}, u32[]{:S(2)}, u32[]{:S(2)}) collective-permute-start(bf16[48,256]{1,0:T(8,128)(2,1)S(1)} %get-tuple-element.82), channel_id=1, source_target_pairs={{0,224},{32,0},{64,32},{96,64},{128,96},{160,128},{192,160},{224,1... | collective-permute-start | bytes 73736 | tf_op jit(solution)/shard_map/ppermute | solution.py:41
  38.1 20.8 %collective-permute-start.16 = (bf16[48,256]{1,0:T(8,128)(2,1)S(1)}, bf16[48,256]{1,0:T(8,128)(2,1)S(1)}, u32[]{:S(2)}, u32[]{:S(2)}) collective-permute-start(bf16[48,256]{1,0:T(8,128)(2,1)S(1)} %get-tuple-element.82), channel_id=1, source_target_pairs={{0,192},{32,224},{64,0},{96,32},{128,64},{160,96},{192,128},{224,1... | collective-permute-start | bytes 73736 | tf_op jit(solution)/shard_map/ppermute | solution.py:41
  38.1 19.3 %collective-permute-start.15 = (bf16[48,256]{1,0:T(8,128)(2,1)S(1)}, bf16[48,256]{1,0:T(8,128)(2,1)S(1)}, u32[]{:S(2)}, u32[]{:S(2)}) collective-permute-start(bf16[48,256]{1,0:T(8,128)(2,1)S(1)} %get-tuple-element.82), channel_id=1, source_target_pairs={{0,160},{32,192},{64,224},{96,0},{128,32},{160,64},{192,96},{224,1... | collective-permute-start | bytes 73736 | tf_op jit(solution)/shard_map/ppermute | solution.py:41
  38.1 19.1 %collective-permute-start.14 = (bf16[48,256]{1,0:T(8,128)(2,1)S(1)}, bf16[48,256]{1,0:T(8,128)(2,1)S(1)}, u32[]{:S(2)}, u32[]{:S(2)}) collective-permute-start(bf16[48,256]{1,0:T(8,128)(2,1)S(1)} %get-tuple-element.82), channel_id=1, source_target_pairs={{0,128},{32,160},{64,192},{96,224},{128,0},{160,32},{192,64},{224,... | collective-permute-start | bytes 73736 | tf_op jit(solution)/shard_map/ppermute | solution.py:41
  46.7 4.9 %collective-permute-start.12 = (bf16[48,256]{1,0:T(8,128)(2,1)S(1)}, bf16[48,256]{1,0:T(8,128)(2,1)S(1)}, u32[]{:S(2)}, u32[]{:S(2)}) collective-permute-start(bf16[48,256]{1,0:T(8,128)(2,1)S(1)} %get-tuple-element.82), channel_id=1, source_target_pairs={{0,64},{32,96},{64,128},{96,160},{128,192},{160,224},{192,0},{224,... | collective-permute-start | bytes 73736 | tf_op jit(solution)/shard_map/ppermute | solution.py:41
  51.6 5.7 %collective-permute-start.13 = (bf16[48,256]{1,0:T(8,128)(2,1)S(1)}, bf16[48,256]{1,0:T(8,128)(2,1)S(1)}, u32[]{:S(2)}, u32[]{:S(2)}) collective-permute-start(bf16[48,256]{1,0:T(8,128)(2,1)S(1)} %get-tuple-element.82), channel_id=1, source_target_pairs={{0,96},{32,128},{64,160},{96,192},{128,224},{160,0},{192,32},{224,... | collective-permute-start | bytes 73736 | tf_op jit(solution)/shard_map/ppermute | solution.py:41
  57.3 20.9 %collective-permute-start.1 = (bf16[128,1792]{1,0:T(8,128)(2,1)}, bf16[128,1792]{1,0:T(8,128)(2,1)S(1)}, u32[]{:S(2)}, u32[]{:S(2)}) collective-permute-start(bf16[128,1792]{1,0:T(8,128)(2,1)} %get-tuple-element.42), channel_id=1, source_target_pairs={{0,1},{1,2},{2,3},{3,0},{4,5},{5,6},{6,7},{7,4},{8,9},{9,10},{10,1... | collective-permute-start | bytes 1376264 | tf_op jit(solution)/shard_map/ppermute | solution.py:41
  57.3 23.0 %collective-permute-start.2 = (bf16[128,1792]{1,0:T(8,128)(2,1)}, bf16[128,1792]{1,0:T(8,128)(2,1)S(1)}, u32[]{:S(2)}, u32[]{:S(2)}) collective-permute-start(bf16[128,1792]{1,0:T(8,128)(2,1)} %get-tuple-element.43), channel_id=1, source_target_pairs={{0,2},{1,3},{2,0},{3,1},{4,6},{5,7},{6,4},{7,5},{8,10},{9,11},{10,... | collective-permute-start | bytes 1376264 | tf_op jit(solution)/shard_map/ppermute | solution.py:41
  57.4 23.0 %collective-permute-start.3 = (bf16[128,1792]{1,0:T(8,128)(2,1)}, bf16[128,1792]{1,0:T(8,128)(2,1)S(1)}, u32[]{:S(2)}, u32[]{:S(2)}) collective-permute-start(bf16[128,1792]{1,0:T(8,128)(2,1)} %get-tuple-element.44), channel_id=1, source_target_pairs={{0,3},{1,0},{2,1},{3,2},{4,7},{5,4},{6,5},{7,6},{8,11},{9,8},{10,9... | collective-permute-start | bytes 1376264 | tf_op jit(solution)/shard_map/ppermute | solution.py:41
  58.9 38.5 %copy-start.11 = (bf16[384,256]{1,0:T(8,128)(2,1)}, bf16[384,256]{1,0:T(8,128)(2,1)S(1)}, u32[]{:S(2)}) copy-start(bf16[384,256]{1,0:T(8,128)(2,1)S(1)} %constant_dynamic-update-slice_fusion.3.refs_8_) | copy-start | bytes 589828
  58.9 23.2 %collective-permute-start.20 = (bf16[384,256]{1,0:T(8,128)(2,1)S(1)}, bf16[384,256]{1,0:T(8,128)(2,1)S(1)}, u32[]{:S(2)}, u32[]{:S(2)}) collective-permute-start(bf16[384,256]{1,0:T(8,128)(2,1)S(1)} %constant_dynamic-update-slice_fusion.3.refs_8_), channel_id=1, source_target_pairs={{0,24},{8,0},{16,8},{24,16},{1,25},{9,1},{17,9},{25,17},{2,26},{10... | collective-permute-start | bytes 589832 | tf_op jit(solution)/shard_map/ppermute | solution.py:41
  60.9 35.8 %collective-permute-start.4 = (bf16[128,1792]{1,0:T(8,128)(2,1)}, bf16[128,1792]{1,0:T(8,128)(2,1)S(1)}, u32[]{:S(2)}, u32[]{:S(2)}) collective-permute-start(bf16[128,1792]{1,0:T(8,128)(2,1)} %get-tuple-element.41.refs_0_), channel_id=1, source_target_pairs={{0,4},{4,0},{1,5},{5,1},{2,6},{6,2},{3,7},{7,3},{8,12},{12,8},{9,1... | collective-permute-start | bytes 1376264 | tf_op jit(solution)/shard_map/ppermute | solution.py:41
  78.2 18.5 %collective-permute-start.5 = (bf16[128,1792]{1,0:T(8,128)(2,1)S(1)}, bf16[128,1792]{1,0:T(8,128)(2,1)S(1)}, u32[]{:S(2)}, u32[]{:S(2)}) collective-permute-start(bf16[128,1792]{1,0:T(8,128)(2,1)S(1)} %collective-permute-done.1.refs_1_), channel_id=1, source_target_pairs={{0,4},{4,0},{1,5},{5,1},{2,6},{6,2},{3,7},{7,3},{8,12},{12,8},{9,1... | collective-permute-start | bytes 1376264 | tf_op jit(solution)/shard_map/ppermute | solution.py:41
  80.3 16.5 %collective-permute-start.6 = (bf16[128,1792]{1,0:T(8,128)(2,1)S(1)}, bf16[128,1792]{1,0:T(8,128)(2,1)S(1)}, u32[]{:S(2)}, u32[]{:S(2)}) collective-permute-start(bf16[128,1792]{1,0:T(8,128)(2,1)S(1)} %collective-permute-done.2.refs_2_), channel_id=1, source_target_pairs={{0,4},{4,0},{1,5},{5,1},{2,6},{6,2},{3,7},{7,3},{8,12},{12,8},{9,1... | collective-permute-start | bytes 1376264 | tf_op jit(solution)/shard_map/ppermute | solution.py:41
  80.4 17.0 %collective-permute-start.7 = (bf16[128,1792]{1,0:T(8,128)(2,1)S(1)}, bf16[128,1792]{1,0:T(8,128)(2,1)S(1)}, u32[]{:S(2)}, u32[]{:S(2)}) collective-permute-start(bf16[128,1792]{1,0:T(8,128)(2,1)S(1)} %collective-permute-done.3.refs_3_), channel_id=1, source_target_pairs={{0,4},{4,0},{1,5},{5,1},{2,6},{6,2},{3,7},{7,3},{8,12},{12,8},{9,1... | collective-permute-start | bytes 1376264 | tf_op jit(solution)/shard_map/ppermute | solution.py:41
  82.1 7.9 %collective-permute-start.19 = (bf16[384,256]{1,0:T(8,128)(2,1)S(1)}, bf16[384,256]{1,0:T(8,128)(2,1)S(1)}, u32[]{:S(2)}, u32[]{:S(2)}) collective-permute-start(bf16[384,256]{1,0:T(8,128)(2,1)S(1)} %constant_dynamic-update-slice_fusion.3.refs_8_), channel_id=1, source_target_pairs={{0,16},{8,24},{16,0},{24,8},{1,17},{9,25},{17,1},{25,9},{2,18},{10... | collective-permute-start | bytes 589832 | tf_op jit(solution)/shard_map/ppermute | solution.py:41
  90.0 6.7 %collective-permute-start.18 = (bf16[384,256]{1,0:T(8,128)(2,1)S(1)}, bf16[384,256]{1,0:T(8,128)(2,1)S(1)}, u32[]{:S(2)}, u32[]{:S(2)}) collective-permute-start(bf16[384,256]{1,0:T(8,128)(2,1)S(1)} %constant_dynamic-update-slice_fusion.3.refs_8_), channel_id=1, source_target_pairs={{0,8},{8,16},{16,24},{24,0},{1,9},{9,17},{17,25},{25,1},{2,10},{10... | collective-permute-start | bytes 589832 | tf_op jit(solution)/shard_map/ppermute | solution.py:41
  106.5 6.1 %collective-permute-start.22 = (f32[8,128]{1,0:T(8,128)}, f32[8,128]{1,0:T(8,128)S(1)}, u32[]{:S(2)}, u32[]{:S(2)}) collective-permute-start(f32[8,128]{1,0:T(8,128)} %get-tuple-element.45), channel_id=1, source_target_pairs={{16,0},{24,8},{32,16},{40,24},{48,32},{56,40},{64,48},{72,56},{80,... | collective-permute-start | bytes 12296 | tf_op jit(solution)/shard_map/ppermute | solution.py:45
  107.8 4.8 %collective-permute-start.21 = (f32[8,128]{1,0:T(8,128)}, f32[8,128]{1,0:T(8,128)S(1)}, u32[]{:S(2)}, u32[]{:S(2)}) collective-permute-start(f32[8,128]{1,0:T(8,128)} %get-tuple-element.45), channel_id=1, source_target_pairs={{8,0},{16,8},{24,16},{32,24},{40,32},{48,40},{56,48},{64,56},{72,6... | collective-permute-start | bytes 12296 | tf_op jit(solution)/shard_map/ppermute | solution.py:45
  123.2 41.2 %collective-permute-start.23 = (bf16[4,128,1024]{2,1,0:T(8,128)(2,1)}, bf16[4,128,1024]{2,1,0:T(8,128)(2,1)S(1)}, u32[]{:S(2)}, u32[]{:S(2)}) collective-permute-start(bf16[4,128,1024]{2,1,0:T(8,128)(2,1)} %get-tuple-element.56), channel_id=1, source_target_pairs={{0,4},{4,0},{1,5},{5,1},{2,6},{6,2},{3,7},{7,3},{8,12},{12,8},{9,1... | collective-permute-start | bytes 3145736 | tf_op jit(solution)/shard_map/ppermute | solution.py:41
  126.2 9.6 %collective-permute-start.27 = (bf16[400,256]{1,0:T(8,128)(2,1)}, bf16[400,256]{1,0:T(8,128)(2,1)S(1)}, u32[]{:S(2)}, u32[]{:S(2)}) collective-permute-start(bf16[400,256]{1,0:T(8,128)(2,1)} %get-tuple-element.63), channel_id=1, source_target_pairs={{0,8},{8,16},{16,24},{24,0},{1,9},{9,17},{17,25},{25,1},{2,10},{10... | collective-permute-start | bytes 614408 | tf_op jit(solution)/shard_map/ppermute | solution.py:41
  127.8 13.3 %collective-permute-start.28 = (bf16[400,256]{1,0:T(8,128)(2,1)}, bf16[400,256]{1,0:T(8,128)(2,1)S(1)}, u32[]{:S(2)}, u32[]{:S(2)}) collective-permute-start(bf16[400,256]{1,0:T(8,128)(2,1)} %get-tuple-element.64), channel_id=1, source_target_pairs={{0,16},{8,24},{16,0},{24,8},{1,17},{9,25},{17,1},{25,9},{2,18},{10... | collective-permute-start | bytes 614408 | tf_op jit(solution)/shard_map/ppermute | solution.py:41
  131.3 9.8 %collective-permute-start.29 = (bf16[400,256]{1,0:T(8,128)(2,1)}, bf16[400,256]{1,0:T(8,128)(2,1)S(1)}, u32[]{:S(2)}, u32[]{:S(2)}) collective-permute-start(bf16[400,256]{1,0:T(8,128)(2,1)} %get-tuple-element.65), channel_id=1, source_target_pairs={{0,24},{8,0},{16,8},{24,16},{1,25},{9,1},{17,9},{25,17},{2,26},{10... | collective-permute-start | bytes 614408 | tf_op jit(solution)/shard_map/ppermute | solution.py:41
  143.9 7.2 %collective-permute-start.30 = (bf16[64,256]{1,0:T(8,128)(2,1)}, bf16[64,256]{1,0:T(8,128)(2,1)S(1)}, u32[]{:S(2)}, u32[]{:S(2)}) collective-permute-start(bf16[64,256]{1,0:T(8,128)(2,1)} %get-tuple-element.68), channel_id=1, source_target_pairs={{0,32},{32,64},{64,96},{96,128},{128,160},{160,192},{192,224},{224... | collective-permute-start | bytes 98312 | tf_op jit(solution)/shard_map/ppermute | solution.py:41
  145.7 5.5 %collective-permute-start.31 = (bf16[64,256]{1,0:T(8,128)(2,1)}, bf16[64,256]{1,0:T(8,128)(2,1)S(1)}, u32[]{:S(2)}, u32[]{:S(2)}) collective-permute-start(bf16[64,256]{1,0:T(8,128)(2,1)} %get-tuple-element.69), channel_id=1, source_target_pairs={{0,64},{32,96},{64,128},{96,160},{128,192},{160,224},{192,0},{224,... | collective-permute-start | bytes 98312 | tf_op jit(solution)/shard_map/ppermute | solution.py:41
  145.7 8.4 %collective-permute-start.32 = (bf16[64,256]{1,0:T(8,128)(2,1)}, bf16[64,256]{1,0:T(8,128)(2,1)S(1)}, u32[]{:S(2)}, u32[]{:S(2)}) collective-permute-start(bf16[64,256]{1,0:T(8,128)(2,1)} %get-tuple-element.70), channel_id=1, source_target_pairs={{0,96},{32,128},{64,160},{96,192},{128,224},{160,0},{192,32},{224,... | collective-permute-start | bytes 98312 | tf_op jit(solution)/shard_map/ppermute | solution.py:41
  146.6 8.4 %collective-permute-start.33 = (bf16[64,256]{1,0:T(8,128)(2,1)}, bf16[64,256]{1,0:T(8,128)(2,1)S(1)}, u32[]{:S(2)}, u32[]{:S(2)}) collective-permute-start(bf16[64,256]{1,0:T(8,128)(2,1)} %get-tuple-element.71), channel_id=1, source_target_pairs={{0,128},{32,160},{64,192},{96,224},{128,0},{160,32},{192,64},{224,... | collective-permute-start | bytes 98312 | tf_op jit(solution)/shard_map/ppermute | solution.py:41
  151.1 5.1 %collective-permute-start.34 = (bf16[64,256]{1,0:T(8,128)(2,1)}, bf16[64,256]{1,0:T(8,128)(2,1)S(1)}, u32[]{:S(2)}, u32[]{:S(2)}) collective-permute-start(bf16[64,256]{1,0:T(8,128)(2,1)} %get-tuple-element.72), channel_id=1, source_target_pairs={{0,160},{32,192},{64,224},{96,0},{128,32},{160,64},{192,96},{224,1... | collective-permute-start | bytes 98312 | tf_op jit(solution)/shard_map/ppermute | solution.py:41
  151.2 7.6 %collective-permute-start.35 = (bf16[64,256]{1,0:T(8,128)(2,1)}, bf16[64,256]{1,0:T(8,128)(2,1)S(1)}, u32[]{:S(2)}, u32[]{:S(2)}) collective-permute-start(bf16[64,256]{1,0:T(8,128)(2,1)} %get-tuple-element.73), channel_id=1, source_target_pairs={{0,192},{32,224},{64,0},{96,32},{128,64},{160,96},{192,128},{224,1... | collective-permute-start | bytes 98312 | tf_op jit(solution)/shard_map/ppermute | solution.py:41
  154.1 4.7 %collective-permute-start.36 = (bf16[64,256]{1,0:T(8,128)(2,1)}, bf16[64,256]{1,0:T(8,128)(2,1)S(1)}, u32[]{:S(2)}, u32[]{:S(2)}) collective-permute-start(bf16[64,256]{1,0:T(8,128)(2,1)} %get-tuple-element.74), channel_id=1, source_target_pairs={{0,224},{32,0},{64,32},{96,64},{128,96},{160,128},{192,160},{224,1... | collective-permute-start | bytes 98312 | tf_op jit(solution)/shard_map/ppermute | solution.py:41
  160.9 30.5 %copy-start.33 = (f32[16,256]{1,0:T(8,128)S(1)}, f32[16,256]{1,0:T(8,128)}, u32[]{:S(2)}) copy-start(f32[16,256]{1,0:T(8,128)} %get-tuple-element.76) | copy-start | bytes 49156
  160.9 38.8 %copy-start.32 = (f32[16,256]{1,0:T(8,128)S(1)}, f32[16,256]{1,0:T(8,128)}, u32[]{:S(2)}) copy-start(f32[16,256]{1,0:T(8,128)} %get-tuple-element.77) | copy-start | bytes 49156
  160.9 11.1 %collective-permute-start.40 = (f32[8,128]{1,0:T(8,128)}, f32[8,128]{1,0:T(8,128)S(1)}, u32[]{:S(2)}, u32[]{:S(2)}) collective-permute-start(f32[8,128]{1,0:T(8,128)} %get-tuple-element.78), channel_id=1, source_target_pairs={{0,4},{4,0},{1,5},{5,1},{2,6},{6,2},{3,7},{7,3},{8,12},{12,8},{9,1... | collective-permute-start | bytes 12296 | tf_op jit(solution)/shard_map/ppermute | solution.py:41
  168.4 44.9 %collective-permute-start.24 = (bf16[128,1024]{1,0:T(8,128)(2,1)}, bf16[128,1024]{1,0:T(8,128)(2,1)S(1)}, u32[]{:S(2)}, u32[]{:S(2)}) collective-permute-start(bf16[128,1024]{1,0:T(8,128)(2,1)} %get-tuple-element.58), channel_id=1, source_target_pairs={{0,3},{1,0},{2,1},{3,2},{4,7},{5,4},{6,5},{7,6},{8,11},{9,8},{10,9... | collective-permute-start | bytes 786440 | tf_op jit(solution)/shard_map/ppermute | solution.py:41
  168.9 44.3 %collective-permute-start.25 = (bf16[128,1024]{1,0:T(8,128)(2,1)}, bf16[128,1024]{1,0:T(8,128)(2,1)S(1)}, u32[]{:S(2)}, u32[]{:S(2)}) collective-permute-start(bf16[128,1024]{1,0:T(8,128)(2,1)} %get-tuple-element.59), channel_id=1, source_target_pairs={{0,2},{1,3},{2,0},{3,1},{4,6},{5,7},{6,4},{7,5},{8,10},{9,11},{10,... | collective-permute-start | bytes 786440 | tf_op jit(solution)/shard_map/ppermute | solution.py:41
  172.0 41.3 %collective-permute-start.26 = (bf16[128,1024]{1,0:T(8,128)(2,1)}, bf16[128,1024]{1,0:T(8,128)(2,1)S(1)}, u32[]{:S(2)}, u32[]{:S(2)}) collective-permute-start(bf16[128,1024]{1,0:T(8,128)(2,1)} %get-tuple-element.60), channel_id=1, source_target_pairs={{0,1},{1,2},{2,3},{3,0},{4,5},{5,6},{6,7},{7,4},{8,9},{9,10},{10,1... | collective-permute-start | bytes 786440 | tf_op jit(solution)/shard_map/ppermute | solution.py:41
  172.0 29.7 %copy-start.25 = (f32[16,128]{1,0:T(8,128)}, f32[16,128]{1,0:T(8,128)S(1)}, u32[]{:S(2)}) copy-start(f32[16,128]{1,0:T(8,128)S(1)} %constant_dynamic-update-slice_fusion.13.refs_0_) | copy-start | bytes 24580
  172.0 10.9 %collective-permute-start.43 = (f32[16,128]{1,0:T(8,128)S(1)}, f32[16,128]{1,0:T(8,128)S(1)}, u32[]{:S(2)}, u32[]{:S(2)}) collective-permute-start(f32[16,128]{1,0:T(8,128)S(1)} %constant_dynamic-update-slice_fusion.13.refs_0_), channel_id=1, source_target_pairs={{0,3},{1,0},{2,1},{3,2},{4,7},{5,4},{6,5},{7,6},{8,11},{9,8},{10,9... | collective-permute-start | bytes 24584 | tf_op jit(solution)/shard_map/ppermute | solution.py:41
  173.5 15.1 %collective-permute-start.42 = (f32[16,128]{1,0:T(8,128)S(1)}, f32[16,128]{1,0:T(8,128)S(1)}, u32[]{:S(2)}, u32[]{:S(2)}) collective-permute-start(f32[16,128]{1,0:T(8,128)S(1)} %constant_dynamic-update-slice_fusion.13.refs_0_), channel_id=1, source_target_pairs={{0,2},{1,3},{2,0},{3,1},{4,6},{5,7},{6,4},{7,5},{8,10},{9,11},{10,... | collective-permute-start | bytes 24584 | tf_op jit(solution)/shard_map/ppermute | solution.py:41
  182.9 16.9 %collective-permute-start.37 = (f32[16,256]{1,0:T(8,128)S(1)}, f32[16,256]{1,0:T(8,128)S(1)}, u32[]{:S(2)}, u32[]{:S(2)}) collective-permute-start(f32[16,256]{1,0:T(8,128)S(1)} %copy-done.34), channel_id=1, source_target_pairs={{0,0},{8,1},{16,2},{24,3},{96,4},{104,5},{112,6},{120,7},{192,8},{... | collective-permute-start | bytes 49160 | tf_op jit(solution)/shard_map/ppermute | solution.py:372
  188.6 2.9 %collective-permute-start.41 = (f32[16,128]{1,0:T(8,128)S(1)}, f32[16,128]{1,0:T(8,128)S(1)}, u32[]{:S(2)}, u32[]{:S(2)}) collective-permute-start(f32[16,128]{1,0:T(8,128)S(1)} %constant_dynamic-update-slice_fusion.13.refs_0_), channel_id=1, source_target_pairs={{0,1},{1,2},{2,3},{3,0},{4,5},{5,6},{6,7},{7,4},{8,9},{9,10},{10,1... | collective-permute-start | bytes 24584 | tf_op jit(solution)/shard_map/ppermute | solution.py:41
  191.5 13.8 %collective-permute-start.38 = (f32[16,256]{1,0:T(8,128)S(1)}, f32[16,256]{1,0:T(8,128)S(1)}, u32[]{:S(2)}, u32[]{:S(2)}) collective-permute-start(f32[16,256]{1,0:T(8,128)S(1)} %copy-done.33), channel_id=1, source_target_pairs={{32,0},{40,1},{48,2},{56,3},{128,4},{136,5},{144,6},{152,7},{224,8... | collective-permute-start | bytes 49160 | tf_op jit(solution)/shard_map/ppermute | solution.py:372
  199.8 12.9 %collective-permute-start.39 = (f32[16,256]{1,0:T(8,128)S(1)}, f32[16,256]{1,0:T(8,128)S(1)}, u32[]{:S(2)}, u32[]{:S(2)}) collective-permute-start(f32[16,256]{1,0:T(8,128)S(1)} %copy-done.32), channel_id=1, source_target_pairs={{64,0},{72,1},{80,2},{88,3},{160,4},{168,5},{176,6},{184,7},{1,8},... | collective-permute-start | bytes 49160 | tf_op jit(solution)/shard_map/ppermute | solution.py:372
  (31 other events, 188.0 us)

commit v2 on v1

v2 whole, which is shorter than its diff:
```python
import functools
import math

import jax
import jax.numpy as jnp
from jax import lax
from jax.experimental import pallas as pl
from jax.experimental.pallas import tpu as pltpu
from jax.sharding import Mesh
from jax.sharding import PartitionSpec as P

SEQ = ("z", "y", "c")
ALL = ("z", "y", "c", "x")
NZ, NY, NC, NX = 8, 4, 2, 4
T = 128
F = 1024
H = 1024
W = 128
UNIT = 16
CB = F // 4
FAR = 2.0
CHUNK = 32
BF = jnp.bfloat16
F32 = jnp.float32


def around(a, axis, k):
    n = lax.axis_size(axis)
    return lax.ppermute(a, axis, [(i, (i + k) % n) for i in range(n)])


def exchange(a, axes):
    return lax.all_to_all(a, axes, split_axis=0, concat_axis=0, tiled=True)


def place(share, yc, k):
    plane = lax.rem(3 * (share + 8 - ((3 * yc + k) >> 3)), 8)
    unit = 24 * plane + 3 * yc + k
    return plane, unit >> 6, unit & 7


def along(a, axis, n, k):
    return lax.ppermute(a, axis, [(i, i + k) for i in range(n) if 0 <= i + k < n])


def call(body, outs, args, scratch=(), name=None):
    vmem = pl.BlockSpec(memory_space=pltpu.VMEM)
    return pl.pallas_call(
        body,
        out_shape=[jax.ShapeDtypeStruct(s, d) for s, d in outs],
        in_specs=[pl.BlockSpec(memory_space=pltpu.SMEM)] + [vmem] * (len(args) - 1),
        out_specs=[vmem] * len(outs),
        scratch_shapes=list(scratch),
        name=name,
    )(*args)


def at(start, size, step):
    return pl.ds(pl.multiple_of(start, step), size)


def split2(v):
    high = v.astype(BF)
    return high, (v - high.astype(F32)).astype(BF)


MSG = F + 3 * 2 * W


def messages_body(idx, inputs, states, ids, grads, tail, *outs):
    first = (idx[0] == 0) & (idx[1] == 0) & (idx[2] == 0)
    row = lax.broadcasted_iota(jnp.int32, (T, W), 0)
    before = jnp.where(row == 0, tail[1:2, 0:W], pltpu.roll(ids[...], 1, 0))
    same = (before == ids[...]) & ((row > 0) | jnp.logical_not(first))
    for k in range(NX):
        out = outs[k]
        x = lax.rem(idx[3] + k, NX)
        out[:, 0:F] = inputs[...]
        for c in range(NC):
            lanes = at(c * 512 + x * W, W, W)
            prior = jnp.where(row == 0, tail[0:1, lanes], pltpu.roll(states[:, lanes], 1, 0))
            high, low = split2(jnp.where(same, prior, FAR))
            out[:, F + c * W : F + (c + 1) * W] = high
            out[:, F + (2 + c) * W : F + (3 + c) * W] = low
            out[:, F + (4 + c) * W : F + (5 + c) * W] = grads[:, lanes]


def choose_body(idx, column, out):
    yc = idx[1] * NC + idx[2]
    for share in range(8):
        for k in range(3):
            plane, _, _ = place(share, yc, k)
            rows = column[plane, k * UNIT : (k + 1) * UNIT, :]
            for y in range(NY):
                out[y * 8 + share, k * UNIT : (k + 1) * UNIT, :] = rows


def forward_body(idx, recur, bias, *refs):
    mine, other, parts, *refs = refs[:4], refs[4:8], *refs[8:]
    az, ac, ar, pr, rp, loc, fac, ends, weight, pre, jac, upg = refs
    c, x = idx[2], idx[3]
    share = c * 4 + x
    for yc in range(NY * NC):
        for k in range(3):
            _, gate, unit = place(share, yc, k)
            rows = at(gate * W + unit * UNIT, UNIT, UNIT)
            for b in range(NX):
                weight[b, rows, :] = parts[yc * NX + b, k * UNIT : (k + 1) * UNIT, :]
    feats = jnp.concatenate([b[k][:, 0:F] for k in range(4) for b in (mine, other)], 0)
    rows = jnp.concatenate([weight[b] for b in range(4)], 1)
    pre[...] = lax.dot_general(feats, rows, (((1,), (1,)), ((), ())), preferred_element_type=F32)
    lanes = at(share * W, W, W)
    rz, rr, rc = (recur[g : g + 1, lanes] for g in range(3))
    bz, br, bc = (bias[g : g + 1, lanes] for g in range(3))
    for k in range(4):
        jac[k, 2 * T : 2 * T + 8, :] = jnp.ones((8, W), F32)
        for side in range(2):
            block = (other if side else mine)[k]
            base = k * 256 + side * T
            half = lax.rem(c + side, 2) * T

            def step(i, carry, block=block, base=base, half=half, k=k):
                own = at(i * CHUNK, CHUNK, CHUNK)
                here = at(base + i * CHUNK, CHUNK, CHUNK)
                when = at(half + i * CHUNK, CHUNK, CHUNK)
                coded = block[own, at(F + c * W, W, W)].astype(F32) + block[
                    own, at(F + 2 * W + c * W, W, W)
                ].astype(F32)
                same = coded < 1.5
                prior = jnp.where(same, coded, 0.0)
                gz = jax.nn.sigmoid(pre[here, 0:W] + rz * prior + bz)
                gr = jax.nn.sigmoid(pre[here, W : 2 * W] + rr * prior + br)
                reset = gr * prior
                gc = jnp.tanh(pre[here, 2 * W : 3 * W] + rc * reset + bc)
                keep = 1.0 - gz
                fz = (gc - prior) * gz * keep
                fc = gz * (1.0 - gc * gc)
                side_r = prior * gr * (1.0 - gr)
                value = keep + fz * rz + fc * rc * (gr + side_r * rr)
                jac[k, when, :] = jnp.where(same, value, 0.0)
                upg[k, when, :] = block[own, at(F + 4 * W + c * W, W, W)].astype(F32)
                az[here, :] = fz
                ac[here, :] = fc
                ar[here, :] = fc * rc * side_r
                pr[here, :] = prior
                rp[here, :] = reset
                return carry

            lax.fori_loop(0, T // CHUNK, step, 0)
    sub = lax.broadcasted_iota(jnp.int32, (8, 8, W), 1)
    for k in range(4):
        for n in range(4):
            f = jac[k, n * 64 + 1 : n * 64 + 65, :].reshape(8, 8, W)
            a = upg[k, n * 64 : n * 64 + 64, :].reshape(8, 8, W)
            for d in (1, 2, 4):
                valid = sub < 8 - d
                a = jnp.where(valid, a + f * pltpu.roll(a, 8 - d, 1), a)
                f = jnp.where(valid, f * pltpu.roll(f, 8 - d, 1), f)
            loc[k * 256 + n * 64 : k * 256 + n * 64 + 64, :] = a.reshape(64, W)
            fac[k * 256 + n * 64 : k * 256 + n * 64 + 64, :] = f.reshape(64, W)

    def chain(i, carry):
        new = []
        for k in range(4):
            a0, f0 = carry[2 * k], carry[2 * k + 1]
            here = at(k * 256 + (31 - i) * 8, 8, 8)
            f = fac[here, :]
            a = loc[here, :] + f * a0
            f = f * f0
            loc[here, :] = a
            fac[here, :] = f
            new += [jnp.broadcast_to(a[0:1], (8, W)), jnp.broadcast_to(f[0:1], (8, W))]
        return tuple(new)

    start = (jnp.zeros((8, W), F32), jnp.ones((8, W), F32)) * 4
    last = lax.fori_loop(0, 32, chain, start, unroll=4)
    for k in range(4):
        ends[k : k + 1, :] = jac[k, 0:1, :] * last[2 * k + 1][0:1]
        ends[4 + k : 5 + k, :] = jac[k, 0:1, :] * last[2 * k][0:1]


def backward_body(idx, one, two, az, ac, ar, pr, rp, loc, fac, *refs):
    mine, other, grads, sent, total = refs[:4], refs[4:8], *refs[8:]
    c = idx[2]
    share = c * 4 + idx[3]
    enter = one[4:8, :] + one[0:4, :] * two[4:8, :]
    sums = (jnp.zeros((8, W), F32),) * 6
    for k in range(4):
        came = enter[k : k + 1]
        for side in range(2):
            base = k * 256 + side * T
            half = k * 256 + lax.rem(c + side, 2) * T

            def step(i, sums, base=base, half=half, came=came):
                here = at(base + i * CHUNK, CHUNK, CHUNK)
                when = at(half + i * CHUNK, CHUNK, CHUNK)
                adj = loc[when, :] + fac[when, :] * came
                gz, gc, gr = adj * az[here, :], adj * ac[here, :], adj * ar[here, :]
                prior = pr[here, :]
                grads[here, 0:W] = gz.astype(BF)
                grads[here, W : 2 * W] = gr.astype(BF)
                grads[here, 2 * W : 3 * W] = gc.astype(BF)
                terms = (gz, gr, gc, gz * prior, gr * prior, gc * rp[here, :])
                return tuple(s + t.reshape(CHUNK // 8, 8, W).sum(0) for s, t in zip(sums, terms))

            sums = lax.fori_loop(0, T // CHUNK, step, sums)
    feats = jnp.concatenate([b[k][:, 0:F] for k in range(4) for b in (mine, other)], 0)
    whole = lax.dot_general(
        grads[...], feats, (((0,), (0,)), ((), ())), preferred_element_type=F32
    )
    for b in range(4):
        total[b] = whole[:, b * CB : (b + 1) * CB]
    stats = jnp.concatenate([jnp.sum(s, 0, keepdims=True) for s in sums], 0)
    high, low = split2(jnp.concatenate([stats, jnp.zeros((10, W), F32)], 0))
    for yc in range(NY * NC):
        for k in range(3):
            _, gate, unit = place(share, yc, k)
            rows = at(gate * W + unit * UNIT, UNIT, UNIT)
            for b in range(NX):
                piece = total[b, rows, :].astype(BF)
                sent[yc * NX + b, k * UNIT : (k + 1) * UNIT, :] = piece
        for b in range(NX):
            sent[yc * NX + b, 48:64, 0:W] = high
            sent[yc * NX + b, 48:64, W : 2 * W] = low


def input_grad_body(idx, grads, weight, mine, other):
    rows = jnp.concatenate([weight[b] for b in range(4)], 1)
    for k in range(4):
        part = jnp.dot(grads[k * 256 : k * 256 + 256, :], rows, preferred_element_type=F32)
        mine[k] = part[0:T]
        other[k] = part[T : 2 * T].astype(BF)


def core_sum_body(idx, mine, other, own, *sent):
    own[...] = mine[0] + other[0].astype(F32)
    for k in range(1, NX):
        sent[k - 1][...] = (mine[k] + other[k].astype(F32)).astype(BF)


def block_sum_body(idx, own, *refs):
    *came, out = refs
    out[...] = (own[...] + sum(r[...].astype(F32) for r in came)).astype(BF)


def y_sum_body(idx, came, piece, stats, sent, total):
    yc = idx[1] * NC + idx[2]
    for share in range(8):
        rows = sum(came[y * 8 + share].astype(F32) for y in range(NY))
        for k in range(3):
            plane, _, _ = place(share, yc, k)
            total[plane, k * UNIT : (k + 1) * UNIT, :] = rows[k * UNIT : (k + 1) * UNIT]
        lanes = slice(share * W, share * W + W)
        stats[:, lanes] = rows[48:56, 0:W] + rows[48:56, W : 2 * W]
    lines = jnp.concatenate([stats[:, b * CB : (b + 1) * CB] for b in range(4)], 0).astype(BF)
    for z in range(NZ):
        sent[z, 0:48, :] = total[z].astype(BF)
        sent[z, 48:80, :] = lines
    piece[...] = total[idx[0]]


def z_sum_body(scale, idx, piece, stats, came, weight_grad, param_grad):
    rows = sum(came[lax.rem(idx[0] + k, NZ)].astype(F32) for k in range(1, NZ))
    weight_grad[...] = (piece[...] + rows[0:48]) * scale
    for b in range(4):
        lanes = slice(b * CB, (b + 1) * CB)
        param_grad[:, lanes] = (stats[0:6, lanes] + rows[48 + b * 8 : 54 + b * 8]) * scale


def local(inputs, weight_t, states, doc_ids, recur, bias, out_grad):
    device = lax.axis_index(ALL)
    sizes = jnp.array([NZ, NY, NC, NX], jnp.int32)
    idx = (device // jnp.array([32, 8, 4, 1], jnp.int32)) % sizes
    states, out_grad = states[0], out_grad[0]
    plane = ("y", "c", "x")

    ids = doc_ids[0].astype(F32)
    tail = jnp.concatenate([states[-1:], jnp.broadcast_to(ids[-1:], (1, H))], 0)
    tail = along(tail, SEQ, NZ * NY * NC, 1)
    ids = jnp.broadcast_to(ids[:, None], (T, W))
    sent = call(
        messages_body,
        [((T, MSG), BF)] * NX,
        (idx, inputs[0], states, ids, out_grad, tail),
        name="messages",
    )
    mine = [sent[0]] + [around(sent[k], "x", k) for k in range(1, NX)]
    blocks = mine + [around(m, "c", 1) for m in mine]

    column = exchange(jnp.broadcast_to(weight_t, (NZ, 48, CB)), "z")
    (parts,) = call(choose_body, [((32, 48, CB), BF)], (idx, column), name="choose")
    parts = exchange(parts, plane)

    tokens = ((8 * T, W), F32)
    *kept, ends, weight = call(
        forward_body,
        [tokens] * 7 + [((8, W), F32), ((4, 3 * W, CB), BF)],
        (idx, recur, bias, *blocks, parts),
        [
            pltpu.VMEM((8 * T, 3 * W), F32),
            pltpu.VMEM((4, 2 * T + 8, W), F32),
            pltpu.VMEM((4, 2 * T, W), F32),
        ],
        name="forward",
    )
    one = along(ends, ("z", "y"), NZ * NY, -1)
    two = along(ends, ("z", "y"), NZ * NY, -2)
    grads, sent = call(
        backward_body,
        [((8 * T, 3 * W), BF), ((32, 64, CB), BF)],
        (idx, one, two, *kept, *blocks),
        [pltpu.VMEM((4, 3 * W, CB), F32)],
        name="backward",
    )

    came = exchange(sent, plane)
    piece, stats, sent = call(
        y_sum_body,
        [((48, CB), F32), ((8, H), F32), ((NZ, 80, CB), BF)],
        (idx, came),
        [pltpu.VMEM((NZ, 48, CB), F32)],
        name="y_sum",
    )
    came = exchange(sent, "z")
    scale = 1.0 / math.sqrt(inputs.shape[0] * T * NZ * NY * NC * NX)
    weight_grad, param_grad = call(
        functools.partial(z_sum_body, scale),
        [((48, CB), F32), ((6, H), F32)],
        (idx, piece, stats, came),
        name="z_sum",
    )

    mine, other = call(
        input_grad_body,
        [((4, T, F), F32), ((4, T, F), BF)],
        (idx, grads, weight),
        name="input_grad",
    )
    other = lax.ppermute(other, "c", [(0, 1), (1, 0)])
    own, *sent = call(
        core_sum_body,
        [((T, F), F32)] + [((T, F), BF)] * 3,
        (idx, mine, other),
        name="core_sum",
    )
    came = [around(sent[k - 1], "x", NX - k) for k in range(1, NX)]
    (input_grad,) = call(block_sum_body, [((T, F), BF)], (idx, own, *came), name="block_sum")
    return input_grad[None], weight_grad, param_grad


def solution(mesh):
    torus = Mesh(mesh.devices.reshape(NZ, NY, NC, NX), ALL)
    in_specs = (
        P("x", SEQ, None),
        P(SEQ, "x"),
        P("x", SEQ, None),
        P("x", SEQ),
        P(),
        P(),
        P("x", SEQ, None),
    )
    out_specs = (P("x", SEQ, None), P(SEQ, "x"), P())
    return jax.shard_map(local, mesh=torus, in_specs=in_specs, out_specs=out_specs, check_vma=False)
```

time: 217 us -> 141 us (0.65)
  the two profiles are of different devices: /device:TPU:5 before, /device:TPU:1 now
where the time goes in v2:
time: 141 us
  starting transfers between devices  49.6 us (35%)
  waiting for transfers between devices  46.7 us (33%)
  Pallas kernels  30.7 us (22%)
  local copies, waits for them, and re-layouts  10.5 us (7%)
  other arithmetic  2.15 us (2%)
    all_to_all x4, starting transfers between devices, exchange(): return lax.all_to_all(a, axes, split_axis=0, concat_axis=0, tiled=True)  33.4 us
    pallas_call x9, Pallas kernels, call(): pl.pallas_call(body, out_shape=[jax.ShapeDtypeStruct(s, d) for s, d in ou...  30.7 us
    ppermute x10, waiting for transfers between devices, around(): return lax.ppermute(a, axis, [(i, (i + k) % n) for i in range(n)])  23.8 us
    all_to_all x4, waiting for transfers between devices, exchange(): return lax.all_to_all(a, axes, split_axis=0, concat_axis=0, tiled=True)  19.5 us
    ppermute x10, starting transfers between devices, around(): return lax.ppermute(a, axis, [(i, (i + k) % n) for i in range(n)])  8.78 us
    ppermute x3, starting transfers between devices, along(): lax.ppermute(a, axis, [(i, i + k) for i in range(n) if 0 <= i + k < n])  7.16 us
    unnamed x36, local copies, waits for them, and re-layouts  6.41 us
    ppermute x3, waiting for transfers between devices, along(): lax.ppermute(a, axis, [(i, i + k) for i in range(n) if 0 <= i + k < n])  3.47 us
  transfers between devices with their start and end apart: 18, of which 9 were waited for; matrix products, arithmetic and copies ran while one was open for 3% of the time, Pallas kernels for 11%

profile of v2, /device:TPU:1, one launch (start us, length us, event | category | flops | bytes accessed | tf_op | source)
XLA Modules:
  0.0 140.5 jit_solution(7548057641630532802)
XLA Ops:
  0.6 0.7 fusion
  1.3 0.6 slice.14
  1.9 0.8 slice_bitcast_fusion
  2.6 0.6 concatenate.3
  3.3 4.6 %collective-permute-start = (f32[2,1024]{1,0:T(2,128)S(1)}, f32[2,1024]{1,0:T(2,128)S(1)}, u32[]{:S(2)}, u32[]{:S(2)}) collective-permute-start(f32[2,1024]{1,0:T(2,128)S(1)} %concatenate.3), channel_id=1, source_target_pairs={{0,4},{4,8},{8,12},{12,16},{16,20},{20,24},{24,28},{28,32},{32,36}... | collective-permute-start | bytes 24584 | tf_op jit(solution)/shard_map/ppermute | solution.py:43
  7.9 1.4 %broadcast_in_dim.7 = bf16[8,48,256]{2,1,0:T(8,128)(2,1)} broadcast(bf16[48,256]{1,0:T(8,128)(2,1)} %param.10), dimensions={1,2} | broadcast | bytes 221184 | tf_op jit(solution)/shard_map/broadcast_in_dim | solution.py:290
  9.3 8.2 %all-to-all-start = ((bf16[8,48,256]{2,1,0:T(8,128)(2,1)}), bf16[8,48,256]{2,1,0:T(8,128)(2,1)S(1)}, u32[]{:S(2)}, u32[]{:S(2)}) async-start(bf16[8,48,256]{2,1,0:T(8,128)(2,1)} %broadcast_in_dim.7), calls=%async_computation | async-start | bytes 393216 | tf_op jit(solution)/shard_map/all_to_all | solution.py:33
  17.5 1.5 %and_select_fusion.idx = s32[4]{0:T(128)} fusion(s32[4]{0:T(128)} %constant.50, s32[4]{0:T(128)} %constant.40.clone, pred[]{:T(512)S(6)} %ne.25, s32[]{:T(128)S(6)} %add.18), kind=kLoop, calls=%fused_computation.1 | loop fusion | flops 48 | bytes 53 | tf_op jit(solution)/shard_map/jit(remainder)/select_n | solution.py:273
  19.0 0.7 broadcast_in_dim.6.ids
  19.7 2.5 %messages.1 = (bf16[128,1792]{1,0:T(8,128)(2,1)}, bf16[128,1792]{1,0:T(8,128)(2,1)}, bf16[128,1792]{1,0:T(8,128)(2,1)}, bf16[128,1792]{1,0:T(8,128)(2,1)}) custom-call(s32[4]{0:T(128)} %and_select_fusion.idx, bf16[128,1024]{1,0:T(8,128)(2,1)} %bitcast.10, f32[128,1024]{1,0:T(8,128)} %bitcast.9, f32[128,128]{1,0:T(8,128)} %broadcast_in_dim.6.ids, ...), custom_call_target="tpu_custom_call" | custom-call | tf_op jit(solution)/shard_map/messages/pallas_call | solution.py:48
  22.2 1.2 collective-permute-start.1
  23.4 2.4 %collective-permute-start.2 = (bf16[128,1792]{1,0:T(8,128)(2,1)}, bf16[128,1792]{1,0:T(8,128)(2,1)S(1)}, u32[]{:S(2)}, u32[]{:S(2)}) collective-permute-start(bf16[128,1792]{1,0:T(8,128)(2,1)} %get-tuple-element.31), channel_id=1, source_target_pairs={{0,2},{1,3},{2,0},{3,1},{4,6},{5,7},{6,4},{7,5},{8,10},{9,11},{10,... | collective-permute-start | bytes 1376264 | tf_op jit(solution)/shard_map/ppermute | solution.py:29
  25.9 1.2 collective-permute-start.3
  27.1 0.8 all-to-all-done.column
  27.8 0.7 copy-done.11
  28.5 1.9 %choose.1 = bf16[32,48,256]{2,1,0:T(8,128)(2,1)} custom-call(s32[4]{0:T(128)} %and_select_fusion.idx, bf16[8,48,256]{2,1,0:T(8,128)(2,1)} %copy-done.11), custom_call_target="tpu_custom_call" | custom-call | tf_op jit(solution)/shard_map/choose/pallas_call | solution.py:48
  30.4 7.8 %all-to-all-start.1 = ((bf16[32,48,256]{2,1,0:T(8,128)(2,1)}), bf16[32,48,256]{2,1,0:T(8,128)(2,1)S(1)}, u32[]{:S(2)}, u32[]{:S(2)}) async-start(bf16[32,48,256]{2,1,0:T(8,128)(2,1)} %choose.1), calls=%async_computation.1 | async-start | bytes 1572864 | tf_op jit(solution)/shard_map/all_to_all | solution.py:33
  38.2 0.3 collective-permute-start.4
  38.8 8.0 %collective-permute-done.2.refs_2_ = bf16[128,1792]{1,0:T(8,128)(2,1)S(1)} collective-permute-done((bf16[128,1792]{1,0:T(8,128)(2,1)}, bf16[128,1792]{1,0:T(8,128)(2,1)S(1)}, u32[]{:S(2)}, u32[]{:S(2)}) %collective-permute-start.2) | collective-permute-done | bytes 458784 | tf_op jit(solution)/shard_map/ppermute | solution.py:29
  46.8 0.5 collective-permute-start.7
  47.3 1.3 collective-permute-done.6.refs_6_
  48.6 0.8 copy-done.8
  49.4 7.2 %all-to-all-done.1.refs_8_ = bf16[32,48,256]{2,1,0:T(8,128)(2,1)S(1)} async-done(((bf16[32,48,256]{2,1,0:T(8,128)(2,1)}), bf16[32,48,256]{2,1,0:T(8,128)(2,1)S(1)}, u32[]{:S(2)}, u32[]{:S(2)}) %all-to-all-start.1) | async-done | bytes 786464 | tf_op jit(solution)/shard_map/all_to_all | solution.py:33
  56.6 0.9 copy-done.1
  57.5 7.5 %forward.1 = (f32[1024,128]{1,0:T(8,128)}, f32[1024,128]{1,0:T(8,128)}, f32[1024,128]{1,0:T(8,128)}, f32[1024,128]{1,0:T(8,128)}, f32[1024,128]{1,0:T(8,128)}, /...) custom-call(s32[4]{0:T(128)} %and_select_fusion.idx, ...), custom_call_target="tpu_custom_call" | custom-call | tf_op jit(solution)/shard_map/forward/pallas_call | solution.py:48
  65.0 1.3 collective-permute-start.9
  66.2 1.3 collective-permute-start.8
  67.5 3.5 %collective-permute-done.9.two = f32[8,128]{1,0:T(8,128)S(1)} collective-permute-done((f32[8,128]{1,0:T(8,128)}, f32[8,128]{1,0:T(8,128)S(1)}, u32[]{:S(2)}, u32[]{:S(2)}) %collective-permute-start.9) | collective-permute-done | bytes 4128 | tf_op jit(solution)/shard_map/ppermute | solution.py:43
  71.0 0.6 copy-done.16
  71.6 5.7 %backward.1 = (bf16[1024,384]{1,0:T(8,128)(2,1)}, bf16[32,64,256]{2,1,0:T(8,128)(2,1)}) custom-call(s32[4]{0:T(128)} %and_select_fusion.idx, f32[8,128]{1,0:T(8,128)} %copy-done.17, f32[8,128]{1,0:T(8,128)} %copy-done.16, f32[1024,128]{1,0:T(8,128)} %get-tuple-element.34.az, f32[1024,128]{1,0:T(8,128)} %get-tuple-element.35.ac, ...), custom_call_target="tpu_custom_call" | custom-call | tf_op jit(solution)/shard_map/backward/pallas_call | solution.py:48
  77.4 10.7 %all-to-all-start.2 = ((bf16[32,64,256]{2,1,0:T(8,128)(2,1)}), bf16[32,64,256]{2,1,0:T(8,128)(2,1)S(1)}, u32[]{:S(2)}, u32[]{:S(2)}) async-start(bf16[32,64,256]{2,1,0:T(8,128)(2,1)} %get-tuple-element.49), calls=%async_computation.2 | async-start | bytes 2097152 | tf_op jit(solution)/shard_map/all_to_all | solution.py:33
  88.1 4.3 %input_grad.1 = (f32[4,128,1024]{2,1,0:T(8,128)}, bf16[4,128,1024]{2,1,0:T(8,128)(2,1)}) custom-call(s32[4]{0:T(128)} %and_select_fusion.idx, bf16[1024,384]{1,0:T(8,128)(2,1)} %get-tuple-element.41.grads, bf16[4,384,256]{2,1,0:T(8,128)(2,1)} %get-tuple-element.42.weight), custom_call_target="tpu_custom_call" | custom-call | tf_op jit(solution)/shard_map/input_grad/pallas_call | solution.py:48
  92.6 11.5 %all-to-all-done.2.came = bf16[32,64,256]{2,1,0:T(8,128)(2,1)S(1)} async-done(((bf16[32,64,256]{2,1,0:T(8,128)(2,1)}), bf16[32,64,256]{2,1,0:T(8,128)(2,1)S(1)}, u32[]{:S(2)}, u32[]{:S(2)}) %all-to-all-start.2) | async-done | bytes 1048608 | tf_op jit(solution)/shard_map/all_to_all | solution.py:33
  104.1 1.0 copy-done
  105.1 2.1 %y_sum.1 = (f32[48,256]{1,0:T(8,128)}, f32[8,1024]{1,0:T(8,128)}, bf16[8,80,256]{2,1,0:T(8,128)(2,1)}) custom-call(s32[4]{0:T(128)} %and_select_fusion.idx, bf16[32,64,256]{2,1,0:T(8,128)(2,1)} %copy-done), custom_call_target="tpu_custom_call" | custom-call | tf_op jit(solution)/shard_map/y_sum/pallas_call | solution.py:48
  107.2 6.7 %all-to-all-start.3 = ((bf16[8,80,256]{2,1,0:T(8,128)(2,1)}), bf16[8,80,256]{2,1,0:T(8,128)(2,1)S(1)}, u32[]{:S(2)}, u32[]{:S(2)}) async-start(bf16[8,80,256]{2,1,0:T(8,128)(2,1)} %get-tuple-element.52), calls=%async_computation.3 | async-start | bytes 655360 | tf_op jit(solution)/shard_map/all_to_all | solution.py:33
  114.0 1.0 copy-done.10
  115.0 2.9 %core_sum.1 = (f32[128,1024]{1,0:T(8,128)}, bf16[128,1024]{1,0:T(8,128)(2,1)}, bf16[128,1024]{1,0:T(8,128)(2,1)}, bf16[128,1024]{1,0:T(8,128)(2,1)}) custom-call(s32[4]{0:T(128)} %and_select_fusion.idx, f32[4,128,1024]{2,1,0:T(8,128)} %get-tuple-element.43.mine, bf16[4,128,1024]{2,1,0:T(8,128)(2,1)} %copy-done.10), custom_call_target="tpu_custom_call" | custom-call | tf_op jit(solution)/shard_map/core_sum/pallas_call | solution.py:48
  117.9 1.8 %collective-permute-start.11 = (bf16[128,1024]{1,0:T(8,128)(2,1)}, bf16[128,1024]{1,0:T(8,128)(2,1)S(1)}, u32[]{:S(2)}, u32[]{:S(2)}) collective-permute-start(bf16[128,1024]{1,0:T(8,128)(2,1)} %get-tuple-element.46), channel_id=1, source_target_pairs={{0,3},{1,0},{2,1},{3,2},{4,7},{5,4},{6,5},{7,6},{8,11},{9,8},{10,9... | collective-permute-start | bytes 786440 | tf_op jit(solution)/shard_map/ppermute | solution.py:29
  119.8 0.4 collective-permute-start.12
  120.2 0.6 collective-permute-start.13
  120.8 6.0 %collective-permute-done.11.refs_0_ = bf16[128,1024]{1,0:T(8,128)(2,1)S(1)} collective-permute-done((bf16[128,1024]{1,0:T(8,128)(2,1)}, bf16[128,1024]{1,0:T(8,128)(2,1)S(1)}, u32[]{:S(2)}, u32[]{:S(2)}) %collective-permute-start.11) | collective-permute-done | bytes 262176 | tf_op jit(solution)/shard_map/ppermute | solution.py:29
  126.8 2.0 %collective-permute-done.12.refs_1_ = bf16[128,1024]{1,0:T(8,128)(2,1)S(1)} collective-permute-done((bf16[128,1024]{1,0:T(8,128)(2,1)}, bf16[128,1024]{1,0:T(8,128)(2,1)S(1)}, u32[]{:S(2)}, u32[]{:S(2)}) %collective-permute-start.12) | collective-permute-done | bytes 262176 | tf_op jit(solution)/shard_map/ppermute | solution.py:29
  128.8 6.5 %collective-permute-done.13.refs_2_ = bf16[128,1024]{1,0:T(8,128)(2,1)S(1)} collective-permute-done((bf16[128,1024]{1,0:T(8,128)(2,1)}, bf16[128,1024]{1,0:T(8,128)(2,1)S(1)}, u32[]{:S(2)}, u32[]{:S(2)}) %collective-permute-start.13) | collective-permute-done | bytes 262176 | tf_op jit(solution)/shard_map/ppermute | solution.py:29
  135.3 0.7 copy-done.14
  136.0 2.1 %block_sum.1 = bf16[128,1024]{1,0:T(8,128)(2,1)} custom-call(s32[4]{0:T(128)} %and_select_fusion.idx, f32[128,1024]{1,0:T(8,128)} %get-tuple-element.45.own, bf16[128,1024]{1,0:T(8,128)(2,1)} %copy-done.12, bf16[128,1024]{1,0:T(8,128)(2,1)} %copy-done.13, bf16[128,1024]{1,0:T(8,128)(2,1)} %copy-done.14), custom_call_target="tpu_custom_call" | custom-call | tf_op jit(solution)/shard_map/block_sum/pallas_call | solution.py:48
  138.1 0.7 copy-done.9
  138.8 1.7 %z_sum.1 = (f32[48,256]{1,0:T(8,128)}, f32[6,1024]{1,0:T(8,128)}) custom-call(s32[4]{0:T(128)} %and_select_fusion.idx, f32[48,256]{1,0:T(8,128)} %get-tuple-element.50.piece, f32[8,1024]{1,0:T(8,128)} %get-tuple-element.51.stats, bf16[8,80,256]{2,1,0:T(8,128)(2,1)} %copy-done.9), custom_call_target="tpu_custom_call" | custom-call | tf_op jit(solution)/shard_map/z_sum/pallas_call | solution.py:48
  (40 shorter events, 0.6 us)
Async XLA Ops:
  3.3 15.7 %collective-permute-start = (f32[2,1024]{1,0:T(2,128)S(1)}, f32[2,1024]{1,0:T(2,128)S(1)}, u32[]{:S(2)}, u32[]{:S(2)}) collective-permute-start(f32[2,1024]{1,0:T(2,128)S(1)} %concatenate.3), channel_id=1, source_target_pairs={{0,4},{4,8},{8,12},{12,16},{16,20},{20,24},{24,28},{28,32},{32,36}... | collective-permute-start | bytes 24584 | tf_op jit(solution)/shard_map/ppermute | solution.py:43
  9.3 18.5 %all-to-all-start = ((bf16[8,48,256]{2,1,0:T(8,128)(2,1)}), bf16[8,48,256]{2,1,0:T(8,128)(2,1)S(1)}, u32[]{:S(2)}, u32[]{:S(2)}) async-start(bf16[8,48,256]{2,1,0:T(8,128)(2,1)} %broadcast_in_dim.7), calls=%async_computation | async-start | bytes 393216 | tf_op jit(solution)/shard_map/all_to_all | solution.py:33
  19.0 0.7 copy-start.15
  22.2 15.9 %copy-start.2 = (bf16[128,1792]{1,0:T(8,128)(2,1)S(1)}, bf16[128,1792]{1,0:T(8,128)(2,1)}, u32[]{:S(2)}) copy-start(bf16[128,1792]{1,0:T(8,128)(2,1)} %get-tuple-element.29.refs_0_) | copy-start | bytes 1376260
  22.2 16.3 %collective-permute-start.1 = (bf16[128,1792]{1,0:T(8,128)(2,1)}, bf16[128,1792]{1,0:T(8,128)(2,1)S(1)}, u32[]{:S(2)}, u32[]{:S(2)}) collective-permute-start(bf16[128,1792]{1,0:T(8,128)(2,1)} %get-tuple-element.30), channel_id=1, source_target_pairs={{0,1},{1,2},{2,3},{3,0},{4,5},{5,6},{6,7},{7,4},{8,9},{9,10},{10,1... | collective-permute-start | bytes 1376264 | tf_op jit(solution)/shard_map/ppermute | solution.py:29
  23.4 23.3 %collective-permute-start.2 = (bf16[128,1792]{1,0:T(8,128)(2,1)}, bf16[128,1792]{1,0:T(8,128)(2,1)S(1)}, u32[]{:S(2)}, u32[]{:S(2)}) collective-permute-start(bf16[128,1792]{1,0:T(8,128)(2,1)} %get-tuple-element.31), channel_id=1, source_target_pairs={{0,2},{1,3},{2,0},{3,1},{4,6},{5,7},{6,4},{7,5},{8,10},{9,11},{10,... | collective-permute-start | bytes 1376264 | tf_op jit(solution)/shard_map/ppermute | solution.py:29
  25.9 20.9 %collective-permute-start.3 = (bf16[128,1792]{1,0:T(8,128)(2,1)}, bf16[128,1792]{1,0:T(8,128)(2,1)S(1)}, u32[]{:S(2)}, u32[]{:S(2)}) collective-permute-start(bf16[128,1792]{1,0:T(8,128)(2,1)} %get-tuple-element.32), channel_id=1, source_target_pairs={{0,3},{1,0},{2,1},{3,2},{4,7},{5,4},{6,5},{7,6},{8,11},{9,8},{10,9... | collective-permute-start | bytes 1376264 | tf_op jit(solution)/shard_map/ppermute | solution.py:29
  27.8 0.7 copy-start.11
  30.4 26.2 %all-to-all-start.1 = ((bf16[32,48,256]{2,1,0:T(8,128)(2,1)}), bf16[32,48,256]{2,1,0:T(8,128)(2,1)S(1)}, u32[]{:S(2)}, u32[]{:S(2)}) async-start(bf16[32,48,256]{2,1,0:T(8,128)(2,1)} %choose.1), calls=%async_computation.1 | async-start | bytes 1572864 | tf_op jit(solution)/shard_map/all_to_all | solution.py:33
  38.2 9.1 %collective-permute-start.4 = (bf16[128,1792]{1,0:T(8,128)(2,1)S(1)}, bf16[128,1792]{1,0:T(8,128)(2,1)S(1)}, u32[]{:S(2)}, u32[]{:S(2)}) collective-permute-start(bf16[128,1792]{1,0:T(8,128)(2,1)S(1)} %copy-done.2), channel_id=1, source_target_pairs={{0,4},{4,0},{1,5},{5,1},{2,6},{6,2},{3,7},{7,3},{8,12},{12,8},{9,1... | collective-permute-start | bytes 1376264 | tf_op jit(solution)/shard_map/ppermute | solution.py:29
  38.5 18.1 %copy-start.3 = (bf16[128,1792]{1,0:T(8,128)(2,1)}, bf16[128,1792]{1,0:T(8,128)(2,1)S(1)}, u32[]{:S(2)}) copy-start(bf16[128,1792]{1,0:T(8,128)(2,1)S(1)} %collective-permute-done.1.refs_1_) | copy-start | bytes 1376260
  38.5 8.8 %collective-permute-start.5 = (bf16[128,1792]{1,0:T(8,128)(2,1)S(1)}, bf16[128,1792]{1,0:T(8,128)(2,1)S(1)}, u32[]{:S(2)}, u32[]{:S(2)}) collective-permute-start(bf16[128,1792]{1,0:T(8,128)(2,1)S(1)} %collective-permute-done.1.refs_1_), channel_id=1, source_target_pairs={{0,4},{4,0},{1,5},{5,1},{2,6},{6,2},{3,7},{7,3},{8,12},{12,8},{9,1... | collective-permute-start | bytes 1376264 | tf_op jit(solution)/shard_map/ppermute | solution.py:29
  46.8 9.8 %copy-start.4 = (bf16[128,1792]{1,0:T(8,128)(2,1)}, bf16[128,1792]{1,0:T(8,128)(2,1)S(1)}, u32[]{:S(2)}) copy-start(bf16[128,1792]{1,0:T(8,128)(2,1)S(1)} %collective-permute-done.2.refs_2_) | copy-start | bytes 1376260
  46.8 1.8 %collective-permute-start.6 = (bf16[128,1792]{1,0:T(8,128)(2,1)S(1)}, bf16[128,1792]{1,0:T(8,128)(2,1)S(1)}, u32[]{:S(2)}, u32[]{:S(2)}) collective-permute-start(bf16[128,1792]{1,0:T(8,128)(2,1)S(1)} %collective-permute-done.2.refs_2_), channel_id=1, source_target_pairs={{0,4},{4,0},{1,5},{5,1},{2,6},{6,2},{3,7},{7,3},{8,12},{12,8},{9,1... | collective-permute-start | bytes 1376264 | tf_op jit(solution)/shard_map/ppermute | solution.py:29
  46.8 9.8 %copy-start.5 = (bf16[128,1792]{1,0:T(8,128)(2,1)}, bf16[128,1792]{1,0:T(8,128)(2,1)S(1)}, u32[]{:S(2)}) copy-start(bf16[128,1792]{1,0:T(8,128)(2,1)S(1)} %collective-permute-done.3.refs_3_) | copy-start | bytes 1376260
  46.8 2.6 %collective-permute-start.7 = (bf16[128,1792]{1,0:T(8,128)(2,1)S(1)}, bf16[128,1792]{1,0:T(8,128)(2,1)}, u32[]{:S(2)}, u32[]{:S(2)}) collective-permute-start(bf16[128,1792]{1,0:T(8,128)(2,1)S(1)} %collective-permute-done.3.refs_3_), channel_id=1, source_target_pairs={{0,4},{4,0},{1,5},{5,1},{2,6},{6,2},{3,7},{7,3},{8,12},{12,8},{9,1... | collective-permute-start | bytes 1376264 | tf_op jit(solution)/shard_map/ppermute | solution.py:29
  47.3 9.3 %copy-start.6 = (bf16[128,1792]{1,0:T(8,128)(2,1)}, bf16[128,1792]{1,0:T(8,128)(2,1)S(1)}, u32[]{:S(2)}) copy-start(bf16[128,1792]{1,0:T(8,128)(2,1)S(1)} %collective-permute-done.4.refs_4_) | copy-start | bytes 1376260
  47.3 9.3 %copy-start.7 = (bf16[128,1792]{1,0:T(8,128)(2,1)}, bf16[128,1792]{1,0:T(8,128)(2,1)S(1)}, u32[]{:S(2)}) copy-start(bf16[128,1792]{1,0:T(8,128)(2,1)S(1)} %collective-permute-done.5.refs_5_) | copy-start | bytes 1376260
  48.6 0.8 copy-start.8
  56.6 0.9 copy-start.1
  65.0 6.1 %collective-permute-start.9 = (f32[8,128]{1,0:T(8,128)}, f32[8,128]{1,0:T(8,128)S(1)}, u32[]{:S(2)}, u32[]{:S(2)}) collective-permute-start(f32[8,128]{1,0:T(8,128)} %get-tuple-element.33), channel_id=1, source_target_pairs={{16,0},{24,8},{32,16},{40,24},{48,32},{56,40},{64,48},{72,56},{80,... | collective-permute-start | bytes 12296 | tf_op jit(solution)/shard_map/ppermute | solution.py:43
  66.2 4.8 %collective-permute-start.8 = (f32[8,128]{1,0:T(8,128)}, f32[8,128]{1,0:T(8,128)S(1)}, u32[]{:S(2)}, u32[]{:S(2)}) collective-permute-start(f32[8,128]{1,0:T(8,128)} %get-tuple-element.33), channel_id=1, source_target_pairs={{8,0},{16,8},{24,16},{32,24},{40,32},{48,40},{56,48},{64,56},{72,6... | collective-permute-start | bytes 12296 | tf_op jit(solution)/shard_map/ppermute | solution.py:43
  71.0 0.6 copy-start.16
  71.0 0.6 copy-start.17
  77.4 26.8 %all-to-all-start.2 = ((bf16[32,64,256]{2,1,0:T(8,128)(2,1)}), bf16[32,64,256]{2,1,0:T(8,128)(2,1)S(1)}, u32[]{:S(2)}, u32[]{:S(2)}) async-start(bf16[32,64,256]{2,1,0:T(8,128)(2,1)} %get-tuple-element.49), calls=%async_computation.2 | async-start | bytes 2097152 | tf_op jit(solution)/shard_map/all_to_all | solution.py:33
  92.4 21.6 %collective-permute-start.10 = (bf16[4,128,1024]{2,1,0:T(8,128)(2,1)}, bf16[4,128,1024]{2,1,0:T(8,128)(2,1)S(1)}, u32[]{:S(2)}, u32[]{:S(2)}) collective-permute-start(bf16[4,128,1024]{2,1,0:T(8,128)(2,1)} %get-tuple-element.44), channel_id=1, source_target_pairs={{0,4},{4,0},{1,5},{5,1},{2,6},{6,2},{3,7},{7,3},{8,12},{12,8},{9,1... | collective-permute-start | bytes 3145736 | tf_op jit(solution)/shard_map/ppermute | solution.py:339
  104.1 1.0 copy-start
  107.2 30.9 %all-to-all-start.3 = ((bf16[8,80,256]{2,1,0:T(8,128)(2,1)}), bf16[8,80,256]{2,1,0:T(8,128)(2,1)S(1)}, u32[]{:S(2)}, u32[]{:S(2)}) async-start(bf16[8,80,256]{2,1,0:T(8,128)(2,1)} %get-tuple-element.52), calls=%async_computation.3 | async-start | bytes 655360 | tf_op jit(solution)/shard_map/all_to_all | solution.py:33
  114.0 1.0 copy-start.10
  117.9 8.9 %collective-permute-start.11 = (bf16[128,1024]{1,0:T(8,128)(2,1)}, bf16[128,1024]{1,0:T(8,128)(2,1)S(1)}, u32[]{:S(2)}, u32[]{:S(2)}) collective-permute-start(bf16[128,1024]{1,0:T(8,128)(2,1)} %get-tuple-element.46), channel_id=1, source_target_pairs={{0,3},{1,0},{2,1},{3,2},{4,7},{5,4},{6,5},{7,6},{8,11},{9,8},{10,9... | collective-permute-start | bytes 786440 | tf_op jit(solution)/shard_map/ppermute | solution.py:29
  119.8 9.0 %collective-permute-start.12 = (bf16[128,1024]{1,0:T(8,128)(2,1)}, bf16[128,1024]{1,0:T(8,128)(2,1)S(1)}, u32[]{:S(2)}, u32[]{:S(2)}) collective-permute-start(bf16[128,1024]{1,0:T(8,128)(2,1)} %get-tuple-element.47), channel_id=1, source_target_pairs={{0,2},{1,3},{2,0},{3,1},{4,6},{5,7},{6,4},{7,5},{8,10},{9,11},{10,... | collective-permute-start | bytes 786440 | tf_op jit(solution)/shard_map/ppermute | solution.py:29
  120.2 15.1 %collective-permute-start.13 = (bf16[128,1024]{1,0:T(8,128)(2,1)}, bf16[128,1024]{1,0:T(8,128)(2,1)S(1)}, u32[]{:S(2)}, u32[]{:S(2)}) collective-permute-start(bf16[128,1024]{1,0:T(8,128)(2,1)} %get-tuple-element.48), channel_id=1, source_target_pairs={{0,1},{1,2},{2,3},{3,0},{4,5},{5,6},{6,7},{7,4},{8,9},{9,10},{10,1... | collective-permute-start | bytes 786440 | tf_op jit(solution)/shard_map/ppermute | solution.py:29
  126.8 8.5 %copy-start.12 = (bf16[128,1024]{1,0:T(8,128)(2,1)}, bf16[128,1024]{1,0:T(8,128)(2,1)S(1)}, u32[]{:S(2)}) copy-start(bf16[128,1024]{1,0:T(8,128)(2,1)S(1)} %collective-permute-done.11.refs_0_) | copy-start | bytes 786436
  128.8 6.5 %copy-start.13 = (bf16[128,1024]{1,0:T(8,128)(2,1)}, bf16[128,1024]{1,0:T(8,128)(2,1)S(1)}, u32[]{:S(2)}) copy-start(bf16[128,1024]{1,0:T(8,128)(2,1)S(1)} %collective-permute-done.12.refs_1_) | copy-start | bytes 786436
  135.3 0.7 copy-start.14
  138.1 0.7 copy-start.9

commit v3 on v2

v3 whole, which is shorter than its diff:
```python
import functools
import math

import jax
import jax.numpy as jnp
from jax import lax
from jax.experimental import pallas as pl
from jax.experimental.pallas import tpu as pltpu
from jax.sharding import Mesh
from jax.sharding import PartitionSpec as P

SEQ = ("z", "y", "c")
ALL = ("z", "y", "c", "x")
NZ, NY, NC, NX = 8, 4, 2, 4
T = 128
F = 1024
H = 1024
W = 128
UNIT = 16
CB = F // 4
FAR = 2.0
CHUNK = 32
BF = jnp.bfloat16
F32 = jnp.float32


def around(a, axis, k):
    n = lax.axis_size(axis)
    return lax.ppermute(a, axis, [(i, (i + k) % n) for i in range(n)])


def exchange(a, axes):
    return lax.all_to_all(a, axes, split_axis=0, concat_axis=0, tiled=True)


def place(share, yc, k):
    plane = lax.rem(3 * (share + 8 - ((3 * yc + k) >> 3)), 8)
    unit = 24 * plane + 3 * yc + k
    return plane, unit >> 6, unit & 7


def along(a, axis, n, k):
    return lax.ppermute(a, axis, [(i, i + k) for i in range(n) if 0 <= i + k < n])


def call(body, outs, args, scratch=()):
    vmem = pl.BlockSpec(memory_space=pltpu.VMEM)
    return pl.pallas_call(
        body,
        out_shape=[jax.ShapeDtypeStruct(s, d) for s, d in outs],
        in_specs=[pl.BlockSpec(memory_space=pltpu.SMEM)] + [vmem] * (len(args) - 1),
        out_specs=[vmem] * len(outs),
        scratch_shapes=list(scratch),
    )(*args)


def coords(idx):
    n = idx[0]
    return n >> 5, (n >> 3) & 3, (n >> 2) & 1, n & 3


def at(start, size, step):
    return pl.ds(pl.multiple_of(start, step), size)


def split2(v):
    high = v.astype(BF)
    return high, (v - high.astype(F32)).astype(BF)


MSG = F + 2 * 2 * W


def prepare_body(weight, states, ids, copies, tail):
    for z in range(NZ):
        copies[z] = weight[...]
    tail[0:1, :] = states[7:8, :]
    tail[1:2, :] = jnp.broadcast_to(ids[0:1, T - 1 : T].astype(F32), (1, H))


def messages_body(idx, inputs, states, ids, grads, tail, *outs):
    z, y, c, x_own = coords(idx)
    row = lax.broadcasted_iota(jnp.int32, (T, W), 0)
    lane = lax.broadcasted_iota(jnp.int32, (T, W), 1)
    number = ids[...].astype(F32)
    column = jnp.sum(jnp.where(row == lane, number, 0.0), 1, keepdims=True)
    column = jnp.broadcast_to(column, (T, W))
    before = jnp.where(row == 0, tail[1:2, 0:W], pltpu.roll(column, 1, 0))
    same = (before == column) & ((row > 0) | (z + y + c > 0))
    for k in range(NX):
        out = outs[k]
        x = lax.rem(x_own + k, NX)
        out[:, 0:F] = inputs[...]
        for c in range(NC):
            lanes = at(c * 512 + x * W, W, W)
            prior = jnp.where(row == 0, tail[0:1, lanes], pltpu.roll(states[:, lanes], 1, 0))
            out[:, F + c * W : F + (c + 1) * W] = jnp.where(same, prior, FAR).astype(BF)
            out[:, F + (2 + c) * W : F + (3 + c) * W] = grads[:, lanes]


def choose_body(idx, column, out):
    _, y, c, _ = coords(idx)
    yc = y * NC + c
    for share in range(8):
        for k in range(3):
            plane, _, _ = place(share, yc, k)
            rows = column[plane, k * UNIT : (k + 1) * UNIT, :]
            for to in range(NY):
                out[to * 8 + share, k * UNIT : (k + 1) * UNIT, :] = rows


def forward_body(idx, recur, bias, *refs):
    mine, other, parts, *refs = refs[:4], refs[4:8], *refs[8:]
    az, ac, ar, pr, rp, loc, fac, ends, weight, pre, jac, upg = refs
    _, _, c, x = coords(idx)
    share = c * 4 + x
    for yc in range(NY * NC):
        for k in range(3):
            _, gate, unit = place(share, yc, k)
            rows = at(gate * W + unit * UNIT, UNIT, UNIT)
            for b in range(NX):
                weight[b, rows, :] = parts[yc * NX + b, k * UNIT : (k + 1) * UNIT, :]
    feats = jnp.concatenate([b[k][:, 0:F] for k in range(4) for b in (mine, other)], 0)
    rows = jnp.concatenate([weight[b] for b in range(4)], 1)
    pre[...] = lax.dot_general(feats, rows, (((1,), (1,)), ((), ())), preferred_element_type=F32)
    lanes = at(share * W, W, W)
    rz, rr, rc = (recur[g : g + 1, lanes] for g in range(3))
    bz, br, bc = (bias[g : g + 1, lanes] for g in range(3))
    for k in range(4):
        jac[k, 2 * T : 2 * T + 8, :] = jnp.ones((8, W), F32)
        for side in range(2):
            block = (other if side else mine)[k]
            base = k * 256 + side * T
            half = lax.rem(c + side, 2) * T

            def step(i, carry, block=block, base=base, half=half, k=k):
                own = at(i * CHUNK, CHUNK, CHUNK)
                here = at(base + i * CHUNK, CHUNK, CHUNK)
                when = at(half + i * CHUNK, CHUNK, CHUNK)
                coded = block[own, at(F + c * W, W, W)].astype(F32)
                same = coded < 1.5
                prior = jnp.where(same, coded, 0.0)
                gz = jax.nn.sigmoid(pre[here, 0:W] + rz * prior + bz)
                gr = jax.nn.sigmoid(pre[here, W : 2 * W] + rr * prior + br)
                reset = gr * prior
                gc = jnp.tanh(pre[here, 2 * W : 3 * W] + rc * reset + bc)
                keep = 1.0 - gz
                fz = (gc - prior) * gz * keep
                fc = gz * (1.0 - gc * gc)
                side_r = prior * gr * (1.0 - gr)
                value = keep + fz * rz + fc * rc * (gr + side_r * rr)
                jac[k, when, :] = jnp.where(same, value, 0.0)
                upg[k, when, :] = block[own, at(F + 2 * W + c * W, W, W)].astype(F32)
                az[here, :] = fz
                ac[here, :] = fc
                ar[here, :] = fc * rc * side_r
                pr[here, :] = prior
                rp[here, :] = reset
                return carry

            lax.fori_loop(0, T // CHUNK, step, 0)
    sub = lax.broadcasted_iota(jnp.int32, (8, 8, W), 1)
    for k in range(4):
        for n in range(4):
            f = jac[k, n * 64 + 1 : n * 64 + 65, :].reshape(8, 8, W)
            a = upg[k, n * 64 : n * 64 + 64, :].reshape(8, 8, W)
            for d in (1, 2, 4):
                valid = sub < 8 - d
                a = jnp.where(valid, a + f * pltpu.roll(a, 8 - d, 1), a)
                f = jnp.where(valid, f * pltpu.roll(f, 8 - d, 1), f)
            loc[k * 256 + n * 64 : k * 256 + n * 64 + 64, :] = a.reshape(64, W)
            fac[k * 256 + n * 64 : k * 256 + n * 64 + 64, :] = f.reshape(64, W)

    def chain(i, carry):
        new = []
        for k in range(4):
            a0, f0 = carry[2 * k], carry[2 * k + 1]
            here = at(k * 256 + (31 - i) * 8, 8, 8)
            f = fac[here, :]
            a = loc[here, :] + f * a0
            f = f * f0
            loc[here, :] = a
            fac[here, :] = f
            new += [jnp.broadcast_to(a[0:1], (8, W)), jnp.broadcast_to(f[0:1], (8, W))]
        return tuple(new)

    start = (jnp.zeros((8, W), F32), jnp.ones((8, W), F32)) * 4
    last = lax.fori_loop(0, 32, chain, start, unroll=4)
    for k in range(4):
        ends[k : k + 1, :] = jac[k, 0:1, :] * last[2 * k + 1][0:1]
        ends[4 + k : 5 + k, :] = jac[k, 0:1, :] * last[2 * k][0:1]


def backward_body(idx, one, two, az, ac, ar, pr, rp, loc, fac, *refs):
    mine, other, near, far, sent, total = refs[:4], refs[4:8], *refs[8:]
    _, _, c, x = coords(idx)
    share = c * 4 + x
    enter = one[4:8, :] + one[0:4, :] * two[4:8, :]
    sums = (jnp.zeros((8, W), F32),) * 6
    for k in range(4):
        came = enter[k : k + 1]
        for side in range(2):
            base = k * 256 + side * T
            half = k * 256 + lax.rem(c + side, 2) * T
            grads = far if side else near

            def step(i, sums, base=base, half=half, came=came, k=k, grads=grads):
                here = at(base + i * CHUNK, CHUNK, CHUNK)
                when = at(half + i * CHUNK, CHUNK, CHUNK)
                adj = loc[when, :] + fac[when, :] * came
                gz, gc, gr = adj * az[here, :], adj * ac[here, :], adj * ar[here, :]
                prior = pr[here, :]
                rows = at(k * T + i * CHUNK, CHUNK, CHUNK)
                grads[rows, 0:W] = gz.astype(BF)
                grads[rows, W : 2 * W] = gr.astype(BF)
                grads[rows, 2 * W : 3 * W] = gc.astype(BF)
                terms = (gz, gr, gc, gz * prior, gr * prior, gc * rp[here, :])
                return tuple(s + t.reshape(CHUNK // 8, 8, W).sum(0) for s, t in zip(sums, terms))

            sums = lax.fori_loop(0, T // CHUNK, step, sums)
    feats = jnp.concatenate([b[:, 0:F] for b in (*mine, *other)], 0)
    grads = jnp.concatenate([near[...], far[...]], 0)
    whole = lax.dot_general(grads, feats, (((0,), (0,)), ((), ())), preferred_element_type=F32)
    for b in range(4):
        total[b] = whole[:, b * CB : (b + 1) * CB]
    stats = jnp.concatenate([jnp.sum(s, 0, keepdims=True) for s in sums], 0)
    high, low = split2(jnp.concatenate([stats, jnp.zeros((2, W), F32)], 0))
    for yc in range(NY * NC):
        for k in range(3):
            _, gate, unit = place(share, yc, k)
            rows = at(gate * W + unit * UNIT, UNIT, UNIT)
            for b in range(NX):
                piece = total[b, rows, :].astype(BF)
                sent[yc * NX + b, k * UNIT : (k + 1) * UNIT, :] = piece
        for b in range(NX):
            sent[yc * NX + b, 48:56, 0:W] = high
            sent[yc * NX + b, 48:56, W : 2 * W] = low


def input_grad_body(idx, near, came, weight, other, own, *sent):
    grads = jnp.concatenate([near[...], came[...]], 1)
    rows = [jnp.concatenate([w[b] for b in range(4)], 1) for w in (weight, other)]
    part = jnp.dot(grads, jnp.concatenate(rows, 0), preferred_element_type=F32)
    own[...] = part[0:T]
    for k in range(1, NX):
        sent[k - 1][...] = part[k * T : (k + 1) * T].astype(BF)


def block_sum_body(idx, own, *refs):
    *came, out = refs
    out[...] = (own[...] + sum(r[...].astype(F32) for r in came)).astype(BF)


def y_sum_body(idx, came, piece, stats, sent, total):
    z_own, y_own, c, _ = coords(idx)
    yc = y_own * NC + c
    for share in range(8):
        rows = sum(came[y * 8 + share].astype(F32) for y in range(NY))
        for k in range(3):
            plane, _, _ = place(share, yc, k)
            total[plane, k * UNIT : (k + 1) * UNIT, :] = rows[k * UNIT : (k + 1) * UNIT]
        lanes = slice(share * W, share * W + W)
        stats[:, lanes] = rows[48:56, 0:W] + rows[48:56, W : 2 * W]
    lines = jnp.concatenate([stats[0:6, b * CB : (b + 1) * CB] for b in range(4)], 0).astype(BF)
    for z in range(NZ):
        sent[z, 0:48, :] = total[z].astype(BF)
        sent[z, 48:72, :] = lines
    piece[...] = total[z_own]


def z_sum_body(scale, idx, piece, stats, came, weight_grad, param_grad):
    z_own, _, _, _ = coords(idx)
    rows = sum(came[lax.rem(z_own + k, NZ)].astype(F32) for k in range(1, NZ))
    weight_grad[...] = (piece[...] + rows[0:48]) * scale
    for b in range(4):
        lanes = slice(b * CB, (b + 1) * CB)
        param_grad[:, lanes] = (stats[0:6, lanes] + rows[48 + b * 6 : 54 + b * 6]) * scale


def program(inputs, weight_t, states, doc_ids, recur, bias, out_grad):
    idx = lax.axis_index(ALL).reshape(1)
    states, out_grad = states[0], out_grad[0]
    plane = ("y", "c", "x")
    copies, tail = pl.pallas_call(
        prepare_body,
        out_shape=[
            jax.ShapeDtypeStruct((NZ, 48, CB), BF),
            jax.ShapeDtypeStruct((2, H), F32),
        ],
        grid=(1,),
        in_specs=[
            pl.BlockSpec((48, CB), lambda i: (0, 0)),
            pl.BlockSpec((8, H), lambda i: (T // 8 - 1, 0)),
            pl.BlockSpec((1, T), lambda i: (0, 0)),
        ],
        out_specs=[
            pl.BlockSpec((NZ, 48, CB), lambda i: (0, 0, 0)),
            pl.BlockSpec((2, H), lambda i: (0, 0)),
        ],
        name="prepare",
    )(weight_t, states, doc_ids)
    column = exchange(copies, "z")

    tail = along(tail, SEQ, NZ * NY * NC, 1)
    sent = call(
        messages_body, [((T, MSG), BF)] * NX, (idx, inputs[0], states, doc_ids, out_grad, tail)
    )
    mine = [sent[0]] + [around(sent[k], "x", k) for k in range(1, NX)]
    blocks = mine + [around(m, "c", 1) for m in mine]

    (parts,) = call(choose_body, [((32, 48, CB), BF)], (idx, column))
    parts = exchange(parts, plane)

    tokens = ((8 * T, W), F32)
    *kept, ends, weight = call(
        forward_body,
        [tokens] * 7 + [((8, W), F32), ((4, 3 * W, CB), BF)],
        (idx, recur, bias, *blocks, parts),
        [
            pltpu.VMEM((8 * T, 3 * W), F32),
            pltpu.VMEM((4, 2 * T + 8, W), F32),
            pltpu.VMEM((4, 2 * T, W), F32),
        ],
    )
    one = along(ends, ("z", "y"), NZ * NY, -1)
    two = along(ends, ("z", "y"), NZ * NY, -2)
    other_weight = around(weight, "c", 1)
    near, far, sent = call(
        backward_body,
        [((4 * T, 3 * W), BF), ((4 * T, 3 * W), BF), ((32, 56, CB), BF)],
        (idx, one, two, *kept, *blocks),
        [pltpu.VMEM((4, 3 * W, CB), F32)],
    )

    far = around(far, "c", 1)
    own, *sent_x = call(
        input_grad_body,
        [((T, F), F32)] + [((T, F), BF)] * 3,
        (idx, near, far, weight, other_weight),
    )
    back = []
    for k in range(1, NX):
        back.append(around(sent_x[k - 1], "x", NX - k))
    (input_grad,) = call(block_sum_body, [((T, F), BF)], (idx, own, *back))
    came = exchange(sent, plane)
    piece, stats, sent = call(
        y_sum_body,
        [((48, CB), F32), ((8, H), F32), ((NZ, 72, CB), BF)],
        (idx, came),
        [pltpu.VMEM((NZ, 48, CB), F32)],
    )
    came = exchange(sent, "z")
    scale = 1.0 / math.sqrt(inputs.shape[0] * T * NZ * NY * NC * NX)
    weight_grad, param_grad = call(
        functools.partial(z_sum_body, scale),
        [((48, CB), F32), ((6, H), F32)],
        (idx, piece, stats, came),
    )

    return input_grad[None], weight_grad, param_grad


def solution(mesh):
    torus = Mesh(mesh.devices.reshape(NZ, NY, NC, NX), ALL)
    in_specs = (
        P("x", SEQ, None),
        P(SEQ, "x"),
        P("x", SEQ, None),
        P("x", SEQ),
        P(),
        P(),
        P("x", SEQ, None),
    )
    out_specs = (P("x", SEQ, None), P(SEQ, "x"), P())
    return jax.shard_map(
        program, mesh=torus, in_specs=in_specs, out_specs=out_specs, check_vma=False
    )
```

time: 141 us -> 135 us (0.957)
  local copies, waits for them, and re-layouts: 10.5 us -> 6.17 us
  waiting for transfers between devices: 46.7 us -> 49.7 us
  Pallas kernels: 30.7 us -> 27.9 us
  other arithmetic: 2.15 us -> 0 us
    pallas_call x9 -> x8, Pallas kernels: 30.7 us -> 26.5 us  [call(): pl.pallas_call(body, out_shape=[jax.ShapeDtypeStruct(s, d) for s, d in ou...]
    all_to_all x4, waiting for transfers between devices: 19.5 us -> 21.7 us  [exchange(): return lax.all_to_all(a, axes, split_axis=0, concat_axis=0, tiled=True)]
    broadcast_in_dim x2 -> x0, local copies, waits for them, and re-layouts: 2.14 us -> none  [the longest x1 1.43 us: local(): column = exchange(jnp.broadcast_to(weight_t, (NZ, 48, CB)), 'z')]
    select_n x1 -> x0, other arithmetic: 1.49 us -> none  [local(): idx = device // jnp.array([32, 8, 4, 1], jnp.int32) % sizes]
    pallas_call x0 -> x1, Pallas kernels: none -> 1.45 us  [program(): pl.pallas_call(prepare_body, out_shape=[jax.ShapeDtypeStruct((NZ, 48, CB)...]
    ppermute x10 -> x12, starting transfers between devices: 8.78 us -> 9.04 us  [around(): return lax.ppermute(a, axis, [(i, (i + k) % n) for i in range(n)])]
    unnamed x36 -> x44, local copies, waits for them, and re-layouts: 6.41 us -> 6.17 us
    ppermute x10 -> x12, waiting for transfers between devices: 23.8 us -> 23.8 us  [around(): return lax.ppermute(a, axis, [(i, (i + k) % n) for i in range(n)])]
  transfers between devices with their start and end apart: 18 -> 19, of which waited for: 9 -> 10; matrix products, arithmetic and copies ran while one was open for 3% -> 0% of each run, Pallas kernels for 11% -> 9%
where the time goes in v3:
time: 135 us; the launch traced here: 134 us
  waiting for transfers between devices  49.7 us (37%)
  starting transfers between devices  49.4 us (37%)
  Pallas kernels  27.9 us (21%)
  local copies, waits for them, and re-layouts  6.17 us (5%)
    all_to_all x4, starting transfers between devices, exchange(): return lax.all_to_all(a, axes, split_axis=0, concat_axis=0, tiled=True)  33.7 us
    pallas_call x8, Pallas kernels, call(): pl.pallas_call(body, out_shape=[jax.ShapeDtypeStruct(s, d) for s, d in ou...  26.5 us
    ppermute x12, waiting for transfers between devices, around(): return lax.ppermute(a, axis, [(i, (i + k) % n) for i in range(n)])  23.8 us
    all_to_all x4, waiting for transfers between devices, exchange(): return lax.all_to_all(a, axes, split_axis=0, concat_axis=0, tiled=True)  21.7 us
    ppermute x12, starting transfers between devices, around(): return lax.ppermute(a, axis, [(i, (i + k) % n) for i in range(n)])  9.04 us
    ppermute x3, starting transfers between devices, along(): lax.ppermute(a, axis, [(i, i + k) for i in range(n) if 0 <= i + k < n])  6.62 us
    unnamed x44, local copies, waits for them, and re-layouts  6.17 us
    ppermute x3, waiting for transfers between devices, along(): lax.ppermute(a, axis, [(i, i + k) for i in range(n) if 0 <= i + k < n])  4.23 us
  transfers between devices with their start and end apart: 19, of which 10 were waited for; matrix products, arithmetic and copies ran while one was open for 0% of the time, Pallas kernels for 9%

profile of v3, /device:TPU:1, one launch (start us, length us, event | category | flops | bytes accessed | tf_op | source)
XLA Modules:
  0.0 134.0 jit_solution(7723471313480687310)
XLA Ops:
  0.6 1.5 %prepare.1 = (bf16[8,48,256]{2,1,0:T(8,128)(2,1)}, f32[2,1024]{1,0:T(2,128)}) custom-call(bf16[48,256]{1,0:T(8,128)(2,1)} %weight.1, f32[128,1024]{1,0:T(8,128)} %bitcast.5, s32[1,128]{1,0:T(1,128)} %ids.3), custom_call_target="tpu_custom_call" | custom-call | tf_op jit(solution)/shard_map/prepare/pallas_call | solution.py:284
  2.1 9.1 %all-to-all-start = ((bf16[8,48,256]{2,1,0:T(8,128)(2,1)}), bf16[8,48,256]{2,1,0:T(8,128)(2,1)S(1)}, u32[]{:S(2)}, u32[]{:S(2)}) async-start(bf16[8,48,256]{2,1,0:T(8,128)(2,1)} %get-tuple-element.35), calls=%async_computation | async-start | bytes 393216 | tf_op jit(solution)/shard_map/all_to_all | solution.py:33
  11.2 4.0 %collective-permute-start = (f32[2,1024]{1,0:T(2,128)S(1)}, f32[2,1024]{1,0:T(2,128)S(1)}, u32[]{:S(2)}, u32[]{:S(2)}) collective-permute-start(f32[2,1024]{1,0:T(2,128)S(1)} %copy-done.21), channel_id=1, source_target_pairs={{0,4},{4,8},{8,12},{12,16},{16,20},{20,24},{24,28},{28,32},{32,36}... | collective-permute-start | bytes 24584 | tf_op jit(solution)/shard_map/ppermute | solution.py:43
  15.3 0.8 collective-permute-done.tail
  16.1 0.6 copy-done.17
  16.6 2.6 %shard_map.94 = (bf16[128,1536]{1,0:T(8,128)(2,1)}, bf16[128,1536]{1,0:T(8,128)(2,1)}, bf16[128,1536]{1,0:T(8,128)(2,1)}, bf16[128,1536]{1,0:T(8,128)(2,1)}) custom-call(s32[1]{0:T(128)} %bitcast.idx, bf16[128,1024]{1,0:T(8,128)(2,1)} %bitcast.7, f32[128,1024]{1,0:T(8,128)} %bitcast.6, s32[1,128]{1,0:T(1,128)} %ids.3, bf16[128,1024]{1,0:T(8,128)(2,1)} %bitcast.8, ...), custom_call_target="tpu_custom_call" | custom-call | tf_op jit(solution)/shard_map/pallas_call | solution.py:48
  19.2 1.2 collective-permute-start.1
  20.5 2.5 %collective-permute-start.2 = (bf16[128,1536]{1,0:T(8,128)(2,1)}, bf16[128,1536]{1,0:T(8,128)(2,1)S(1)}, u32[]{:S(2)}, u32[]{:S(2)}) collective-permute-start(bf16[128,1536]{1,0:T(8,128)(2,1)} %get-tuple-element.33), channel_id=1, source_target_pairs={{0,2},{1,3},{2,0},{3,1},{4,6},{5,7},{6,4},{7,5},{8,10},{9,11},{10,... | collective-permute-start | bytes 1179656 | tf_op jit(solution)/shard_map/ppermute | solution.py:29
  22.9 1.2 collective-permute-start.3
  24.1 0.7 copy-done.12
  24.7 1.9 %shard_map.95 = bf16[32,48,256]{2,1,0:T(8,128)(2,1)} custom-call(s32[1]{0:T(128)} %bitcast.idx, bf16[8,48,256]{2,1,0:T(8,128)(2,1)} %copy-done.12), custom_call_target="tpu_custom_call" | custom-call | tf_op jit(solution)/shard_map/pallas_call | solution.py:48
  26.6 6.7 %all-to-all-start.1 = ((bf16[32,48,256]{2,1,0:T(8,128)(2,1)}), bf16[32,48,256]{2,1,0:T(8,128)(2,1)S(1)}, u32[]{:S(2)}, u32[]{:S(2)}) async-start(bf16[32,48,256]{2,1,0:T(8,128)(2,1)} %shard_map.95), calls=%async_computation.1 | async-start | bytes 1572864 | tf_op jit(solution)/shard_map/all_to_all | solution.py:33
  33.4 0.3 collective-permute-start.4
  33.7 0.3 collective-permute-start.5
  34.0 7.3 %collective-permute-done.2.refs_2_ = bf16[128,1536]{1,0:T(8,128)(2,1)S(1)} collective-permute-done((bf16[128,1536]{1,0:T(8,128)(2,1)}, bf16[128,1536]{1,0:T(8,128)(2,1)S(1)}, u32[]{:S(2)}, u32[]{:S(2)}) %collective-permute-start.2) | collective-permute-done | bytes 393248 | tf_op jit(solution)/shard_map/ppermute | solution.py:29
  41.2 0.0 collective-permute-start.6
  41.3 0.5 collective-permute-start.7
  41.8 1.2 collective-permute-done.6.refs_6_
  43.0 0.7 collective-permute-done.7.refs_7_
  43.7 7.4 %all-to-all-done.1.refs_8_ = bf16[32,48,256]{2,1,0:T(8,128)(2,1)S(1)} async-done(((bf16[32,48,256]{2,1,0:T(8,128)(2,1)}), bf16[32,48,256]{2,1,0:T(8,128)(2,1)S(1)}, u32[]{:S(2)}, u32[]{:S(2)}) %all-to-all-start.1) | async-done | bytes 786464 | tf_op jit(solution)/shard_map/all_to_all | solution.py:33
  51.1 0.9 copy-done.1
  52.0 7.2 %shard_map.96 = (f32[1024,128]{1,0:T(8,128)}, f32[1024,128]{1,0:T(8,128)}, f32[1024,128]{1,0:T(8,128)}, f32[1024,128]{1,0:T(8,128)}, f32[1024,128]{1,0:T(8,128)}...) custom-call(s32[1]{0:T(128)} %bitcast.idx, f32[3,1024]{1,0:T(4,128)} %recur.1, ...), custom_call_target="tpu_custom_call" | custom-call | tf_op jit(solution)/shard_map/pallas_call | solution.py:48
  59.2 1.3 collective-permute-start.9
  60.5 1.3 collective-permute-start.8
  61.8 3.5 %collective-permute-done.9.two = f32[8,128]{1,0:T(8,128)S(1)} collective-permute-done((f32[8,128]{1,0:T(8,128)}, f32[8,128]{1,0:T(8,128)S(1)}, u32[]{:S(2)}, u32[]{:S(2)}) %collective-permute-start.9) | collective-permute-done | bytes 4128 | tf_op jit(solution)/shard_map/ppermute | solution.py:43
  65.3 0.6 copy-done.18
  65.9 0.0 copy-done.19
  65.9 5.5 %shard_map.97 = (bf16[512,384]{1,0:T(8,128)(2,1)}, bf16[512,384]{1,0:T(8,128)(2,1)}, bf16[32,56,256]{2,1,0:T(8,128)(2,1)}) custom-call(s32[1]{0:T(128)} %bitcast.idx, f32[8,128]{1,0:T(8,128)} %copy-done.19, f32[8,128]{1,0:T(8,128)} %copy-done.18, f32[1024,128]{1,0:T(8,128)} %get-tuple-element.37.az, f32[1024,128]{1,0:T(8,128)} %get-tuple-element.38.ac, ...), custom_call_target="tpu_custom_call" | custom-call | tf_op jit(solution)/shard_map/pallas_call | solution.py:48
  71.4 11.2 %all-to-all-start.2 = ((bf16[32,56,256]{2,1,0:T(8,128)(2,1)}), bf16[32,56,256]{2,1,0:T(8,128)(2,1)S(1)}, u32[]{:S(2)}, u32[]{:S(2)}) async-start(bf16[32,56,256]{2,1,0:T(8,128)(2,1)} %get-tuple-element.51), calls=%async_computation.2 | async-start | bytes 1835008 | tf_op jit(solution)/shard_map/all_to_all | solution.py:33
  82.6 0.3 collective-permute-start.11
  82.9 0.3 collective-permute-start.10
  83.2 14.3 %all-to-all-done.2.came = bf16[32,56,256]{2,1,0:T(8,128)(2,1)S(1)} async-done(((bf16[32,56,256]{2,1,0:T(8,128)(2,1)}), bf16[32,56,256]{2,1,0:T(8,128)(2,1)S(1)}, u32[]{:S(2)}, u32[]{:S(2)}) %all-to-all-start.2) | async-done | bytes 917536 | tf_op jit(solution)/shard_map/all_to_all | solution.py:33
  97.5 0.9 copy-done
  98.4 2.0 %shard_map.100 = (f32[48,256]{1,0:T(8,128)}, f32[8,1024]{1,0:T(8,128)}, bf16[8,72,256]{2,1,0:T(8,128)(2,1)}) custom-call(s32[1]{0:T(128)} %bitcast.idx, bf16[32,56,256]{2,1,0:T(8,128)(2,1)} %copy-done), custom_call_target="tpu_custom_call" | custom-call | tf_op jit(solution)/shard_map/pallas_call | solution.py:48
  100.5 6.7 %all-to-all-start.3 = ((bf16[8,72,256]{2,1,0:T(8,128)(2,1)}), bf16[8,72,256]{2,1,0:T(8,128)(2,1)S(1)}, u32[]{:S(2)}, u32[]{:S(2)}) async-start(bf16[8,72,256]{2,1,0:T(8,128)(2,1)} %get-tuple-element.54), calls=%async_computation.3 | async-start | bytes 589824 | tf_op jit(solution)/shard_map/all_to_all | solution.py:33
  107.2 0.7 copy-done.13
  107.9 0.3 copy-done.11
  108.2 3.5 %shard_map.98 = (f32[128,1024]{1,0:T(8,128)}, bf16[128,1024]{1,0:T(8,128)(2,1)}, bf16[128,1024]{1,0:T(8,128)(2,1)}, bf16[128,1024]{1,0:T(8,128)(2,1)}) custom-call(s32[1]{0:T(128)} %bitcast.idx, bf16[512,384]{1,0:T(8,128)(2,1)} %get-tuple-element.44.near, bf16[512,384]{1,0:T(8,128)(2,1)} %copy-done.13, bf16[4,384,256]{2,1,0:T(8,128)(2,1)} %get-tuple-element.46.weight, ...), custom_call_target="tpu_custom_call" | custom-call | tf_op jit(solution)/shard_map/pallas_call | solution.py:48
  111.7 1.6 %collective-permute-start.12 = (bf16[128,1024]{1,0:T(8,128)(2,1)}, bf16[128,1024]{1,0:T(8,128)(2,1)S(1)}, u32[]{:S(2)}, u32[]{:S(2)}) collective-permute-start(bf16[128,1024]{1,0:T(8,128)(2,1)} %get-tuple-element.48), channel_id=1, source_target_pairs={{0,3},{1,0},{2,1},{3,2},{4,7},{5,4},{6,5},{7,6},{8,11},{9,8},{10,9... | collective-permute-start | bytes 786440 | tf_op jit(solution)/shard_map/ppermute | solution.py:29
  113.3 0.6 collective-permute-start.13
  113.9 0.4 collective-permute-start.14
  114.3 5.6 %collective-permute-done.12.refs_0_ = bf16[128,1024]{1,0:T(8,128)(2,1)S(1)} collective-permute-done((bf16[128,1024]{1,0:T(8,128)(2,1)}, bf16[128,1024]{1,0:T(8,128)(2,1)S(1)}, u32[]{:S(2)}, u32[]{:S(2)}) %collective-permute-start.12) | collective-permute-done | bytes 262176 | tf_op jit(solution)/shard_map/ppermute | solution.py:29
  119.8 2.5 %collective-permute-done.13.refs_1_ = bf16[128,1024]{1,0:T(8,128)(2,1)S(1)} collective-permute-done((bf16[128,1024]{1,0:T(8,128)(2,1)}, bf16[128,1024]{1,0:T(8,128)(2,1)S(1)}, u32[]{:S(2)}, u32[]{:S(2)}) %collective-permute-start.13) | collective-permute-done | bytes 262176 | tf_op jit(solution)/shard_map/ppermute | solution.py:29
  122.3 6.6 %collective-permute-done.14.refs_2_ = bf16[128,1024]{1,0:T(8,128)(2,1)S(1)} collective-permute-done((bf16[128,1024]{1,0:T(8,128)(2,1)}, bf16[128,1024]{1,0:T(8,128)(2,1)S(1)}, u32[]{:S(2)}, u32[]{:S(2)}) %collective-permute-start.14) | collective-permute-done | bytes 262176 | tf_op jit(solution)/shard_map/ppermute | solution.py:29
  128.9 0.7 copy-done.16
  129.6 2.1 %shard_map.99 = bf16[128,1024]{1,0:T(8,128)(2,1)} custom-call(s32[1]{0:T(128)} %bitcast.idx, f32[128,1024]{1,0:T(8,128)} %get-tuple-element.47.own, bf16[128,1024]{1,0:T(8,128)(2,1)} %copy-done.14, bf16[128,1024]{1,0:T(8,128)(2,1)} %copy-done.15, bf16[128,1024]{1,0:T(8,128)(2,1)} %copy-done.16), custom_call_target="tpu_custom_call" | custom-call | tf_op jit(solution)/shard_map/pallas_call | solution.py:48
  131.7 0.7 copy-done.9
  132.4 1.7 %shard_map.101 = (f32[48,256]{1,0:T(8,128)}, f32[6,1024]{1,0:T(8,128)}) custom-call(s32[1]{0:T(128)} %bitcast.idx, f32[48,256]{1,0:T(8,128)} %get-tuple-element.52.piece, f32[8,1024]{1,0:T(8,128)} %get-tuple-element.53.stats, bf16[8,72,256]{2,1,0:T(8,128)(2,1)} %copy-done.9), custom_call_target="tpu_custom_call" | custom-call | tf_op jit(solution)/shard_map/pallas_call | solution.py:48
  (43 shorter events, 0.1 us)
Async XLA Ops:
  2.1 9.1 %copy-start.21 = (f32[2,1024]{1,0:T(2,128)S(1)}, f32[2,1024]{1,0:T(2,128)}, u32[]{:S(2)}) copy-start(f32[2,1024]{1,0:T(2,128)} %get-tuple-element.30) | copy-start | bytes 24580
  2.1 22.0 %all-to-all-start = ((bf16[8,48,256]{2,1,0:T(8,128)(2,1)}), bf16[8,48,256]{2,1,0:T(8,128)(2,1)S(1)}, u32[]{:S(2)}, u32[]{:S(2)}) async-start(bf16[8,48,256]{2,1,0:T(8,128)(2,1)} %get-tuple-element.35), calls=%async_computation | async-start | bytes 393216 | tf_op jit(solution)/shard_map/all_to_all | solution.py:33
  11.2 4.8 %collective-permute-start = (f32[2,1024]{1,0:T(2,128)S(1)}, f32[2,1024]{1,0:T(2,128)S(1)}, u32[]{:S(2)}, u32[]{:S(2)}) collective-permute-start(f32[2,1024]{1,0:T(2,128)S(1)} %copy-done.21), channel_id=1, source_target_pairs={{0,4},{4,8},{8,12},{12,16},{16,20},{20,24},{24,28},{28,32},{32,36}... | collective-permute-start | bytes 24584 | tf_op jit(solution)/shard_map/ppermute | solution.py:43
  16.1 0.6 copy-start.17
  19.2 14.4 %collective-permute-start.1 = (bf16[128,1536]{1,0:T(8,128)(2,1)}, bf16[128,1536]{1,0:T(8,128)(2,1)S(1)}, u32[]{:S(2)}, u32[]{:S(2)}) collective-permute-start(bf16[128,1536]{1,0:T(8,128)(2,1)} %get-tuple-element.32), channel_id=1, source_target_pairs={{0,1},{1,2},{2,3},{3,0},{4,5},{5,6},{6,7},{7,4},{8,9},{9,10},{10,1... | collective-permute-start | bytes 1179656 | tf_op jit(solution)/shard_map/ppermute | solution.py:29
  20.5 20.8 %collective-permute-start.2 = (bf16[128,1536]{1,0:T(8,128)(2,1)}, bf16[128,1536]{1,0:T(8,128)(2,1)S(1)}, u32[]{:S(2)}, u32[]{:S(2)}) collective-permute-start(bf16[128,1536]{1,0:T(8,128)(2,1)} %get-tuple-element.33), channel_id=1, source_target_pairs={{0,2},{1,3},{2,0},{3,1},{4,6},{5,7},{6,4},{7,5},{8,10},{9,11},{10,... | collective-permute-start | bytes 1179656 | tf_op jit(solution)/shard_map/ppermute | solution.py:29
  22.9 18.3 %collective-permute-start.3 = (bf16[128,1536]{1,0:T(8,128)(2,1)}, bf16[128,1536]{1,0:T(8,128)(2,1)S(1)}, u32[]{:S(2)}, u32[]{:S(2)}) collective-permute-start(bf16[128,1536]{1,0:T(8,128)(2,1)} %get-tuple-element.34), channel_id=1, source_target_pairs={{0,3},{1,0},{2,1},{3,2},{4,7},{5,4},{6,5},{7,6},{8,11},{9,8},{10,9... | collective-permute-start | bytes 1179656 | tf_op jit(solution)/shard_map/ppermute | solution.py:29
  24.1 0.7 copy-start.12
  26.6 6.7 %copy-start.2 = (bf16[128,1536]{1,0:T(8,128)(2,1)S(1)}, bf16[128,1536]{1,0:T(8,128)(2,1)}, u32[]{:S(2)}) copy-start(bf16[128,1536]{1,0:T(8,128)(2,1)} %get-tuple-element.31.refs_0_) | copy-start | bytes 1179652
  26.6 24.5 %all-to-all-start.1 = ((bf16[32,48,256]{2,1,0:T(8,128)(2,1)}), bf16[32,48,256]{2,1,0:T(8,128)(2,1)S(1)}, u32[]{:S(2)}, u32[]{:S(2)}) async-start(bf16[32,48,256]{2,1,0:T(8,128)(2,1)} %shard_map.95), calls=%async_computation.1 | async-start | bytes 1572864 | tf_op jit(solution)/shard_map/all_to_all | solution.py:33
  33.4 8.4 %collective-permute-start.4 = (bf16[128,1536]{1,0:T(8,128)(2,1)S(1)}, bf16[128,1536]{1,0:T(8,128)(2,1)S(1)}, u32[]{:S(2)}, u32[]{:S(2)}) collective-permute-start(bf16[128,1536]{1,0:T(8,128)(2,1)S(1)} %copy-done.2), channel_id=1, source_target_pairs={{0,4},{4,0},{1,5},{5,1},{2,6},{6,2},{3,7},{7,3},{8,12},{12,8},{9,1... | collective-permute-start | bytes 1179656 | tf_op jit(solution)/shard_map/ppermute | solution.py:29
  33.7 17.4 %copy-start.3 = (bf16[128,1536]{1,0:T(8,128)(2,1)}, bf16[128,1536]{1,0:T(8,128)(2,1)S(1)}, u32[]{:S(2)}) copy-start(bf16[128,1536]{1,0:T(8,128)(2,1)S(1)} %collective-permute-done.1.refs_1_) | copy-start | bytes 1179652
  33.7 8.1 %collective-permute-start.5 = (bf16[128,1536]{1,0:T(8,128)(2,1)S(1)}, bf16[128,1536]{1,0:T(8,128)(2,1)S(1)}, u32[]{:S(2)}, u32[]{:S(2)}) collective-permute-start(bf16[128,1536]{1,0:T(8,128)(2,1)S(1)} %collective-permute-done.1.refs_1_), channel_id=1, source_target_pairs={{0,4},{4,0},{1,5},{5,1},{2,6},{6,2},{3,7},{7,3},{8,12},{12,8},{9,1... | collective-permute-start | bytes 1179656 | tf_op jit(solution)/shard_map/ppermute | solution.py:29
  41.2 9.9 %copy-start.4 = (bf16[128,1536]{1,0:T(8,128)(2,1)}, bf16[128,1536]{1,0:T(8,128)(2,1)S(1)}, u32[]{:S(2)}) copy-start(bf16[128,1536]{1,0:T(8,128)(2,1)S(1)} %collective-permute-done.2.refs_2_) | copy-start | bytes 1179652
  41.2 1.7 %collective-permute-start.6 = (bf16[128,1536]{1,0:T(8,128)(2,1)S(1)}, bf16[128,1536]{1,0:T(8,128)(2,1)S(1)}, u32[]{:S(2)}, u32[]{:S(2)}) collective-permute-start(bf16[128,1536]{1,0:T(8,128)(2,1)S(1)} %collective-permute-done.2.refs_2_), channel_id=1, source_target_pairs={{0,4},{4,0},{1,5},{5,1},{2,6},{6,2},{3,7},{7,3},{8,12},{12,8},{9,1... | collective-permute-start | bytes 1179656 | tf_op jit(solution)/shard_map/ppermute | solution.py:29
  41.2 9.9 %copy-start.5 = (bf16[128,1536]{1,0:T(8,128)(2,1)}, bf16[128,1536]{1,0:T(8,128)(2,1)S(1)}, u32[]{:S(2)}) copy-start(bf16[128,1536]{1,0:T(8,128)(2,1)S(1)} %collective-permute-done.3.refs_3_) | copy-start | bytes 1179652
  41.3 2.4 %collective-permute-start.7 = (bf16[128,1536]{1,0:T(8,128)(2,1)S(1)}, bf16[128,1536]{1,0:T(8,128)(2,1)}, u32[]{:S(2)}, u32[]{:S(2)}) collective-permute-start(bf16[128,1536]{1,0:T(8,128)(2,1)S(1)} %collective-permute-done.3.refs_3_), channel_id=1, source_target_pairs={{0,4},{4,0},{1,5},{5,1},{2,6},{6,2},{3,7},{7,3},{8,12},{12,8},{9,1... | collective-permute-start | bytes 1179656 | tf_op jit(solution)/shard_map/ppermute | solution.py:29
  41.8 9.4 %copy-start.6 = (bf16[128,1536]{1,0:T(8,128)(2,1)}, bf16[128,1536]{1,0:T(8,128)(2,1)S(1)}, u32[]{:S(2)}) copy-start(bf16[128,1536]{1,0:T(8,128)(2,1)S(1)} %collective-permute-done.4.refs_4_) | copy-start | bytes 1179652
  41.8 9.4 %copy-start.7 = (bf16[128,1536]{1,0:T(8,128)(2,1)}, bf16[128,1536]{1,0:T(8,128)(2,1)S(1)}, u32[]{:S(2)}) copy-start(bf16[128,1536]{1,0:T(8,128)(2,1)S(1)} %collective-permute-done.5.refs_5_) | copy-start | bytes 1179652
  43.0 8.2 %copy-start.8 = (bf16[128,1536]{1,0:T(8,128)(2,1)}, bf16[128,1536]{1,0:T(8,128)(2,1)S(1)}, u32[]{:S(2)}) copy-start(bf16[128,1536]{1,0:T(8,128)(2,1)S(1)} %collective-permute-done.6.refs_6_) | copy-start | bytes 1179652
  51.1 0.9 copy-start.1
  59.2 6.1 %collective-permute-start.9 = (f32[8,128]{1,0:T(8,128)}, f32[8,128]{1,0:T(8,128)S(1)}, u32[]{:S(2)}, u32[]{:S(2)}) collective-permute-start(f32[8,128]{1,0:T(8,128)} %get-tuple-element.36), channel_id=1, source_target_pairs={{16,0},{24,8},{32,16},{40,24},{48,32},{56,40},{64,48},{72,56},{80,... | collective-permute-start | bytes 12296 | tf_op jit(solution)/shard_map/ppermute | solution.py:43
  60.5 4.8 %collective-permute-start.8 = (f32[8,128]{1,0:T(8,128)}, f32[8,128]{1,0:T(8,128)S(1)}, u32[]{:S(2)}, u32[]{:S(2)}) collective-permute-start(f32[8,128]{1,0:T(8,128)} %get-tuple-element.36), channel_id=1, source_target_pairs={{8,0},{16,8},{24,16},{32,24},{40,32},{48,40},{56,48},{64,56},{72,6... | collective-permute-start | bytes 12296 | tf_op jit(solution)/shard_map/ppermute | solution.py:43
  65.3 0.6 copy-start.18
  65.3 0.6 copy-start.19
  71.4 11.2 %copy-start.10 = (bf16[4,384,256]{2,1,0:T(8,128)(2,1)S(1)}, bf16[4,384,256]{2,1,0:T(8,128)(2,1)}, u32[]{:S(2)}) copy-start(bf16[4,384,256]{2,1,0:T(8,128)(2,1)} %get-tuple-element.46.weight) | copy-start | bytes 2359300
  71.4 11.5 %copy-start.20 = (bf16[512,384]{1,0:T(8,128)(2,1)S(1)}, bf16[512,384]{1,0:T(8,128)(2,1)}, u32[]{:S(2)}) copy-start(bf16[512,384]{1,0:T(8,128)(2,1)} %get-tuple-element.45) | copy-start | bytes 1179652
  71.4 26.1 %all-to-all-start.2 = ((bf16[32,56,256]{2,1,0:T(8,128)(2,1)}), bf16[32,56,256]{2,1,0:T(8,128)(2,1)S(1)}, u32[]{:S(2)}, u32[]{:S(2)}) async-start(bf16[32,56,256]{2,1,0:T(8,128)(2,1)} %get-tuple-element.51), calls=%async_computation.2 | async-start | bytes 1835008 | tf_op jit(solution)/shard_map/all_to_all | solution.py:33
  82.6 24.6 %collective-permute-start.11 = (bf16[4,384,256]{2,1,0:T(8,128)(2,1)S(1)}, bf16[4,384,256]{2,1,0:T(8,128)(2,1)S(1)}, u32[]{:S(2)}, u32[]{:S(2)}) collective-permute-start(bf16[4,384,256]{2,1,0:T(8,128)(2,1)S(1)} %copy-done.10), channel_id=1, source_target_pairs={{0,4},{4,0},{1,5},{5,1},{2,6},{6,2},{3,7},{7,3},{8,12},{12,8},{9,1... | collective-permute-start | bytes 2359304 | tf_op jit(solution)/shard_map/ppermute | solution.py:29
  82.9 24.2 %collective-permute-start.10 = (bf16[512,384]{1,0:T(8,128)(2,1)S(1)}, bf16[512,384]{1,0:T(8,128)(2,1)S(1)}, u32[]{:S(2)}, u32[]{:S(2)}) collective-permute-start(bf16[512,384]{1,0:T(8,128)(2,1)S(1)} %copy-done.20), channel_id=1, source_target_pairs={{0,4},{4,0},{1,5},{5,1},{2,6},{6,2},{3,7},{7,3},{8,12},{12,8},{9,1... | collective-permute-start | bytes 1179656 | tf_op jit(solution)/shard_map/ppermute | solution.py:29
  97.5 1.0 copy-start
  100.5 31.2 %all-to-all-start.3 = ((bf16[8,72,256]{2,1,0:T(8,128)(2,1)}), bf16[8,72,256]{2,1,0:T(8,128)(2,1)S(1)}, u32[]{:S(2)}, u32[]{:S(2)}) async-start(bf16[8,72,256]{2,1,0:T(8,128)(2,1)} %get-tuple-element.54), calls=%async_computation.3 | async-start | bytes 589824 | tf_op jit(solution)/shard_map/all_to_all | solution.py:33
  107.2 0.8 copy-start.13
  107.2 1.0 copy-start.11
  111.7 8.1 %collective-permute-start.12 = (bf16[128,1024]{1,0:T(8,128)(2,1)}, bf16[128,1024]{1,0:T(8,128)(2,1)S(1)}, u32[]{:S(2)}, u32[]{:S(2)}) collective-permute-start(bf16[128,1024]{1,0:T(8,128)(2,1)} %get-tuple-element.48), channel_id=1, source_target_pairs={{0,3},{1,0},{2,1},{3,2},{4,7},{5,4},{6,5},{7,6},{8,11},{9,8},{10,9... | collective-permute-start | bytes 786440 | tf_op jit(solution)/shard_map/ppermute | solution.py:29
  113.3 9.0 %collective-permute-start.13 = (bf16[128,1024]{1,0:T(8,128)(2,1)}, bf16[128,1024]{1,0:T(8,128)(2,1)S(1)}, u32[]{:S(2)}, u32[]{:S(2)}) collective-permute-start(bf16[128,1024]{1,0:T(8,128)(2,1)} %get-tuple-element.49), channel_id=1, source_target_pairs={{0,2},{1,3},{2,0},{3,1},{4,6},{5,7},{6,4},{7,5},{8,10},{9,11},{10,... | collective-permute-start | bytes 786440 | tf_op jit(solution)/shard_map/ppermute | solution.py:29
  113.9 15.0 %collective-permute-start.14 = (bf16[128,1024]{1,0:T(8,128)(2,1)}, bf16[128,1024]{1,0:T(8,128)(2,1)S(1)}, u32[]{:S(2)}, u32[]{:S(2)}) collective-permute-start(bf16[128,1024]{1,0:T(8,128)(2,1)} %get-tuple-element.50), channel_id=1, source_target_pairs={{0,1},{1,2},{2,3},{3,0},{4,5},{5,6},{6,7},{7,4},{8,9},{9,10},{10,1... | collective-permute-start | bytes 786440 | tf_op jit(solution)/shard_map/ppermute | solution.py:29
  119.8 9.0 %copy-start.14 = (bf16[128,1024]{1,0:T(8,128)(2,1)}, bf16[128,1024]{1,0:T(8,128)(2,1)S(1)}, u32[]{:S(2)}) copy-start(bf16[128,1024]{1,0:T(8,128)(2,1)S(1)} %collective-permute-done.12.refs_0_) | copy-start | bytes 786436
  122.3 6.6 %copy-start.15 = (bf16[128,1024]{1,0:T(8,128)(2,1)}, bf16[128,1024]{1,0:T(8,128)(2,1)S(1)}, u32[]{:S(2)}) copy-start(bf16[128,1024]{1,0:T(8,128)(2,1)S(1)} %collective-permute-done.13.refs_1_) | copy-start | bytes 786436
  128.9 0.7 copy-start.16
  131.7 0.7 copy-start.9

commit v4 on v3

--- a/solution.py
+++ b/solution.py
@@ -20,6 +20,7 @@
 CB = F // 4
 FAR = 2.0
 CHUNK = 32
+GRANT = 20 << 20
 BF = jnp.bfloat16
 F32 = jnp.float32
 
@@ -43,15 +44,26 @@
     return lax.ppermute(a, axis, [(i, i + k) for i in range(n) if 0 <= i + k < n])
 
 
-def call(body, outs, args, scratch=()):
+def call(body, outs, args, scratch=(), far=(), far_outs=()):
     vmem = pl.BlockSpec(memory_space=pltpu.VMEM)
-    return pl.pallas_call(
+    hbm = pl.BlockSpec(memory_space=pltpu.HBM)
+    smem = pl.BlockSpec(memory_space=pltpu.SMEM)
+    kernel = pl.pallas_call(
         body,
-        out_shape=[jax.ShapeDtypeStruct(s, d) for s, d in outs],
-        in_specs=[pl.BlockSpec(memory_space=pltpu.SMEM)] + [vmem] * (len(args) - 1),
-        out_specs=[vmem] * len(outs),
+        out_shape=[
+            (pltpu.HBM if n in far_outs else jax.ShapeDtypeStruct)(s, d)
+            for n, (s, d) in enumerate(outs)
+        ],
+        in_specs=[smem] + [hbm if n in far else vmem for n in range(1, len(args))],
+        out_specs=[hbm if n in far_outs else vmem for n in range(len(outs))],
         scratch_shapes=list(scratch),
-    )(*args)
+        compiler_params=pltpu.CompilerParams(vmem_limit_bytes=GRANT),
+    )
+    args = [
+        pltpu.with_memory_space_constraint(a, pltpu.HBM) if n in far else a
+        for n, a in enumerate(args)
+    ]
+    return kernel(*args)
 
 
 def coords(idx):
@@ -68,17 +80,26 @@
     return high, (v - high.astype(F32)).astype(BF)
 
 
-MSG = F + 2 * 2 * W
-
-
-def prepare_body(weight, states, ids, copies, tail):
+MSG = 2 * 2 * W
+
+
+def prepare_body(idx, weight, states, ids, copies, tail, block, last, number, sem):
+    moves = [
+        pltpu.make_async_copy(weight, block, sem.at[0]),
+        pltpu.make_async_copy(states.at[pl.ds(T - 8, 8)], last, sem.at[1]),
+        pltpu.make_async_copy(ids, number, sem.at[2]),
+    ]
+    for move in moves:
+        move.start()
+    for move in moves:
+        move.wait()
+    tail[0:1, :] = last[7:8, :]
+    tail[1:2, :] = jnp.broadcast_to(number[0:1, T - 1 : T].astype(F32), (1, H))
     for z in range(NZ):
-        copies[z] = weight[...]
-    tail[0:1, :] = states[7:8, :]
-    tail[1:2, :] = jnp.broadcast_to(ids[0:1, T - 1 : T].astype(F32), (1, H))
-
-
-def messages_body(idx, inputs, states, ids, grads, tail, *outs):
+        copies[z] = block[...]
+
+
+def messages_body(idx, states, ids, grads, tail, *outs):
     z, y, c, x_own = coords(idx)
     row = lax.broadcasted_iota(jnp.int32, (T, W), 0)
     lane = lax.broadcasted_iota(jnp.int32, (T, W), 1)
@@ -90,12 +111,11 @@
     for k in range(NX):
         out = outs[k]
         x = lax.rem(x_own + k, NX)
-        out[:, 0:F] = inputs[...]
         for c in range(NC):
             lanes = at(c * 512 + x * W, W, W)
             prior = jnp.where(row == 0, tail[0:1, lanes], pltpu.roll(states[:, lanes], 1, 0))
-            out[:, F + c * W : F + (c + 1) * W] = jnp.where(same, prior, FAR).astype(BF)
-            out[:, F + (2 + c) * W : F + (3 + c) * W] = grads[:, lanes]
+            out[:, c * W : (c + 1) * W] = jnp.where(same, prior, FAR).astype(BF)
+            out[:, (2 + c) * W : (3 + c) * W] = grads[:, lanes]
 
 
 def choose_body(idx, column, out):
@@ -110,9 +130,18 @@
 
 
 def forward_body(idx, recur, bias, *refs):
-    mine, other, parts, *refs = refs[:4], refs[4:8], *refs[8:]
-    az, ac, ar, pr, rp, loc, fac, ends, weight, pre, jac, upg = refs
+    feats, mine, other, parts, *refs = refs[:8], refs[8:12], refs[12:16], *refs[16:]
+    az, ac, ar, pr, rp, loc, fac, ends, weight_out, *refs = refs
+    weight, pre, jac, upg, gates, tokens, sem = refs
     _, _, c, x = coords(idx)
+    params = [
+        pltpu.make_async_copy(recur, gates.at[0], sem.at[0]),
+        pltpu.make_async_copy(bias, gates.at[1], sem.at[1]),
+    ]
+    for n, block in enumerate((*mine, *other)):
+        params.append(pltpu.make_async_copy(block, tokens.at[n], sem.at[3 + n]))
+    for move in params:
+        move.start()
     share = c * 4 + x
     for yc in range(NY * NC):
         for k in range(3):
@@ -120,16 +149,20 @@
             rows = at(gate * W + unit * UNIT, UNIT, UNIT)
             for b in range(NX):
                 weight[b, rows, :] = parts[yc * NX + b, k * UNIT : (k + 1) * UNIT, :]
-    feats = jnp.concatenate([b[k][:, 0:F] for k in range(4) for b in (mine, other)], 0)
+    leave = pltpu.make_async_copy(weight, weight_out, sem.at[2])
+    leave.start()
+    feats = jnp.concatenate([feats[k + n][...] for k in range(4) for n in (0, 4)], 0)
     rows = jnp.concatenate([weight[b] for b in range(4)], 1)
     pre[...] = lax.dot_general(feats, rows, (((1,), (1,)), ((), ())), preferred_element_type=F32)
     lanes = at(share * W, W, W)
-    rz, rr, rc = (recur[g : g + 1, lanes] for g in range(3))
-    bz, br, bc = (bias[g : g + 1, lanes] for g in range(3))
+    for move in params:
+        move.wait()
+    rz, rr, rc = (gates[0, g : g + 1, lanes] for g in range(3))
+    bz, br, bc = (gates[1, g : g + 1, lanes] for g in range(3))
     for k in range(4):
         jac[k, 2 * T : 2 * T + 8, :] = jnp.ones((8, W), F32)
         for side in range(2):
-            block = (other if side else mine)[k]
+            block = tokens.at[k + 4 * side]
             base = k * 256 + side * T
             half = lax.rem(c + side, 2) * T
 
@@ -137,7 +170,7 @@
                 own = at(i * CHUNK, CHUNK, CHUNK)
                 here = at(base + i * CHUNK, CHUNK, CHUNK)
                 when = at(half + i * CHUNK, CHUNK, CHUNK)
-                coded = block[own, at(F + c * W, W, W)].astype(F32)
+                coded = block[own, at(c * W, W, W)].astype(F32)
                 same = coded < 1.5
                 prior = jnp.where(same, coded, 0.0)
                 gz = jax.nn.sigmoid(pre[here, 0:W] + rz * prior + bz)
@@ -150,7 +183,7 @@
                 side_r = prior * gr * (1.0 - gr)
                 value = keep + fz * rz + fc * rc * (gr + side_r * rr)
                 jac[k, when, :] = jnp.where(same, value, 0.0)
-                upg[k, when, :] = block[own, at(F + 2 * W + c * W, W, W)].astype(F32)
+                upg[k, when, :] = block[own, at(2 * W + c * W, W, W)].astype(F32)
                 az[here, :] = fz
                 ac[here, :] = fc
                 ar[here, :] = fc * rc * side_r
@@ -189,10 +222,11 @@
     for k in range(4):
         ends[k : k + 1, :] = jac[k, 0:1, :] * last[2 * k + 1][0:1]
         ends[4 + k : 5 + k, :] = jac[k, 0:1, :] * last[2 * k][0:1]
+    leave.wait()
 
 
 def backward_body(idx, one, two, az, ac, ar, pr, rp, loc, fac, *refs):
-    mine, other, near, far, sent, total = refs[:4], refs[4:8], *refs[8:]
+    feats, near, far, sent, total = refs[:8], *refs[8:]
     _, _, c, x = coords(idx)
     share = c * 4 + x
     enter = one[4:8, :] + one[0:4, :] * two[4:8, :]
@@ -218,23 +252,21 @@
                 return tuple(s + t.reshape(CHUNK // 8, 8, W).sum(0) for s, t in zip(sums, terms))
 
             sums = lax.fori_loop(0, T // CHUNK, step, sums)
-    feats = jnp.concatenate([b[:, 0:F] for b in (*mine, *other)], 0)
+    feats = jnp.concatenate([b[...] for b in feats], 0)
     grads = jnp.concatenate([near[...], far[...]], 0)
     whole = lax.dot_general(grads, feats, (((0,), (0,)), ((), ())), preferred_element_type=F32)
     for b in range(4):
         total[b] = whole[:, b * CB : (b + 1) * CB]
     stats = jnp.concatenate([jnp.sum(s, 0, keepdims=True) for s in sums], 0)
     high, low = split2(jnp.concatenate([stats, jnp.zeros((2, W), F32)], 0))
-    for yc in range(NY * NC):
-        for k in range(3):
-            _, gate, unit = place(share, yc, k)
-            rows = at(gate * W + unit * UNIT, UNIT, UNIT)
-            for b in range(NX):
-                piece = total[b, rows, :].astype(BF)
-                sent[yc * NX + b, k * UNIT : (k + 1) * UNIT, :] = piece
-        for b in range(NX):
-            sent[yc * NX + b, 48:56, 0:W] = high
-            sent[yc * NX + b, 48:56, W : 2 * W] = low
+    for b in range(NX):
+        for yc in range(NY * NC):
+            for k in range(3):
+                _, gate, unit = place(share, yc, k)
+                rows = at(gate * W + unit * UNIT, UNIT, UNIT)
+                sent[yc, b, k * UNIT : (k + 1) * UNIT, :] = total[b, rows, :].astype(BF)
+            sent[yc, b, 48:56, 0:W] = high
+            sent[yc, b, 48:56, W : 2 * W] = low
 
 
 def input_grad_body(idx, near, came, weight, other, own, *sent):
@@ -281,31 +313,31 @@
     idx = lax.axis_index(ALL).reshape(1)
     states, out_grad = states[0], out_grad[0]
     plane = ("y", "c", "x")
-    copies, tail = pl.pallas_call(
+    features = [inputs[0]]
+    for k in range(1, NX):
+        features.append(around(inputs[0], "x", k))
+    features += [around(m, "c", 1) for m in features]
+    copies, tail = call(
         prepare_body,
-        out_shape=[
-            jax.ShapeDtypeStruct((NZ, 48, CB), BF),
-            jax.ShapeDtypeStruct((2, H), F32),
+        [((NZ, 48, CB), BF), ((2, H), F32)],
+        (idx, weight_t, states, doc_ids),
+        [
+            pltpu.VMEM((48, CB), BF),
+            pltpu.VMEM((8, H), F32),
+            pltpu.VMEM((1, T), jnp.int32),
+            pltpu.SemaphoreType.DMA((3,)),
         ],
-        grid=(1,),
-        in_specs=[
-            pl.BlockSpec((48, CB), lambda i: (0, 0)),
-            pl.BlockSpec((8, H), lambda i: (T // 8 - 1, 0)),
-            pl.BlockSpec((1, T), lambda i: (0, 0)),
-        ],
-        out_specs=[
-            pl.BlockSpec((NZ, 48, CB), lambda i: (0, 0, 0)),
-            pl.BlockSpec((2, H), lambda i: (0, 0)),
-        ],
-        name="prepare",
-    )(weight_t, states, doc_ids)
+        far=(1, 2, 3),
+    )
     column = exchange(copies, "z")
 
     tail = along(tail, SEQ, NZ * NY * NC, 1)
     sent = call(
-        messages_body, [((T, MSG), BF)] * NX, (idx, inputs[0], states, doc_ids, out_grad, tail)
-    )
-    mine = [sent[0]] + [around(sent[k], "x", k) for k in range(1, NX)]
+        messages_body, [((T, MSG), BF)] * NX, (idx, states, doc_ids, out_grad, tail)
+    )
+    mine = [sent[0]]
+    for k in range(1, NX):
+        mine.append(around(sent[k], "x", k))
     blocks = mine + [around(m, "c", 1) for m in mine]
 
     (parts,) = call(choose_body, [((32, 48, CB), BF)], (idx, column))
@@ -315,22 +347,29 @@
     *kept, ends, weight = call(
         forward_body,
         [tokens] * 7 + [((8, W), F32), ((4, 3 * W, CB), BF)],
-        (idx, recur, bias, *blocks, parts),
+        (idx, recur, bias, *features, *blocks, parts),
         [
+            pltpu.VMEM((4, 3 * W, CB), BF),
             pltpu.VMEM((8 * T, 3 * W), F32),
             pltpu.VMEM((4, 2 * T + 8, W), F32),
             pltpu.VMEM((4, 2 * T, W), F32),
+            pltpu.VMEM((2, 3, H), F32),
+            pltpu.VMEM((8, T, MSG), BF),
+            pltpu.SemaphoreType.DMA((11,)),
         ],
+        far=(1, 2, *range(11, 19)),
+        far_outs=(8,),
     )
     one = along(ends, ("z", "y"), NZ * NY, -1)
     two = along(ends, ("z", "y"), NZ * NY, -2)
     other_weight = around(weight, "c", 1)
     near, far, sent = call(
         backward_body,
-        [((4 * T, 3 * W), BF), ((4 * T, 3 * W), BF), ((32, 56, CB), BF)],
-        (idx, one, two, *kept, *blocks),
+        [((4 * T, 3 * W), BF), ((4 * T, 3 * W), BF), ((8, NX, 56, CB), BF)],
+        (idx, one, two, *kept, *features),
         [pltpu.VMEM((4, 3 * W, CB), F32)],
     )
+    sent = sent.reshape(32, 56, CB)
 
     far = around(far, "c", 1)
     own, *sent_x = call(

time: 135 us -> 128 us (0.948)
  blocking collectives: 0 us -> 17.8 us
  Pallas kernels: 27.9 us -> 10.8 us
  local copies, waits for them, and re-layouts: 6.17 us -> 3.06 us
  starting transfers between devices: 49.4 us -> 47.1 us
  waiting for transfers between devices: 49.7 us -> 47.7 us
    all_to_all x0 -> x1, blocking collectives: none -> 17.8 us  [exchange(): return lax.all_to_all(a, axes, split_axis=0, concat_axis=0, tiled=True)]
    pallas_call x9, Pallas kernels: 27.9 us -> 10.8 us  [call(): return kernel(*args)]
    all_to_all x4 -> x3, starting transfers between devices: 33.7 us -> 25.1 us  [exchange(): return lax.all_to_all(a, axes, split_axis=0, concat_axis=0, tiled=True)]
    all_to_all x4 -> x3, waiting for transfers between devices: 21.7 us -> 14.3 us  [exchange(): return lax.all_to_all(a, axes, split_axis=0, concat_axis=0, tiled=True)]
    ppermute x12 -> x19, starting transfers between devices: 9.04 us -> 15.7 us  [around(): return lax.ppermute(a, axis, [(i, (i + k) % n) for i in range(n)])]
    ppermute x12 -> x19, waiting for transfers between devices: 23.8 us -> 28.6 us  [around(): return lax.ppermute(a, axis, [(i, (i + k) % n) for i in range(n)])]
    unnamed x44 -> x32, local copies, waits for them, and re-layouts: 6.17 us -> 3.06 us
  transfers between devices with their start and end apart: 19 -> 25, of which waited for: 10 -> 15; matrix products, arithmetic and copies ran while one was open for 0% -> 0% of each run, Pallas kernels for 9% -> 2%
where the time goes in v4:
time: 128 us; the launch traced here: 127 us
  waiting for transfers between devices  47.7 us (37%)
  starting transfers between devices  47.1 us (37%)
  blocking collectives  17.8 us (14%)
  Pallas kernels  10.8 us (8%)
  local copies, waits for them, and re-layouts  3.06 us (2%)
    ppermute x19, waiting for transfers between devices, around(): return lax.ppermute(a, axis, [(i, (i + k) % n) for i in range(n)])  28.6 us
    all_to_all x3, starting transfers between devices, exchange(): return lax.all_to_all(a, axes, split_axis=0, concat_axis=0, tiled=True)  25.1 us
    all_to_all x1, blocking collectives, exchange(): return lax.all_to_all(a, axes, split_axis=0, concat_axis=0, tiled=True)  17.8 us
    ppermute x19, starting transfers between devices, around(): return lax.ppermute(a, axis, [(i, (i + k) % n) for i in range(n)])  15.7 us
    all_to_all x3, waiting for transfers between devices, exchange(): return lax.all_to_all(a, axes, split_axis=0, concat_axis=0, tiled=True)  14.3 us
    pallas_call x9, Pallas kernels, call(): return kernel(*args)  10.8 us
    ppermute x3, starting transfers between devices, along(): lax.ppermute(a, axis, [(i, i + k) for i in range(n) if 0 <= i + k < n])  6.31 us
    ppermute x3, waiting for transfers between devices, along(): lax.ppermute(a, axis, [(i, i + k) for i in range(n) if 0 <= i + k < n])  4.81 us
  transfers between devices with their start and end apart: 25, of which 15 were waited for; matrix products, arithmetic and copies ran while one was open for 0% of the time, Pallas kernels for 2%

profile of v4, /device:TPU:1, one launch (start us, length us, event | category | flops | bytes accessed | tf_op | source)
XLA Modules:
  0.0 127.4 jit_solution(5766284008340217694)
XLA Ops:
  0.6 0.9 shard_map.94
  1.5 17.8 %all_to_all.20.column = bf16[8,48,256]{2,1,0:T(8,128)(2,1)S(1)} all-to-all(bf16[8,48,256]{2,1,0:T(8,128)(2,1)S(1)} %get-tuple-element.35), channel_id=1, replica_groups=mesh['z'=8,'y'=4,'c'=2,'x'=4] {'z'}, dimensions={0} | all-to-all | bytes 393216 | tf_op jit(solution)/shard_map/all_to_all | solution.py:34
  19.3 0.9 shard_map.96
  20.3 9.7 %all-to-all-start.1 = ((bf16[32,48,256]{2,1,0:T(8,128)(2,1)}), bf16[32,48,256]{2,1,0:T(8,128)(2,1)S(1)}, u32[]{:S(2)}, u32[]{:S(2)}) async-start(bf16[32,48,256]{2,1,0:T(8,128)(2,1)} %shard_map.96), calls=%async_computation.1 | async-start | bytes 1572864 | tf_op jit(solution)/shard_map/all_to_all | solution.py:34
  29.9 3.5 %collective-permute-start.7 = (f32[2,1024]{1,0:T(2,128)S(1)}, f32[2,1024]{1,0:T(2,128)S(1)}, u32[]{:S(2)}, u32[]{:S(2)}) collective-permute-start(f32[2,1024]{1,0:T(2,128)S(1)} %get-tuple-element.30), channel_id=1, source_target_pairs={{0,4},{4,8},{8,12},{12,16},{16,20},{20,24},{24,28},{28,32},{32,36}... | collective-permute-start | bytes 24584 | tf_op jit(solution)/shard_map/ppermute | solution.py:44
  33.5 0.9 collective-permute-done.7.tail
  34.4 0.2 shard_map.95
  34.6 2.8 %collective-permute-start.8 = (bf16[128,512]{1,0:T(8,128)(2,1)S(1)}, bf16[128,512]{1,0:T(8,128)(2,1)S(1)}, u32[]{:S(2)}, u32[]{:S(2)}) collective-permute-start(bf16[128,512]{1,0:T(8,128)(2,1)S(1)} %get-tuple-element.32), channel_id=1, source_target_pairs={{0,1},{1,2},{2,3},{3,0},{4,5},{5,6},{6,7},{7,4},{8,9},{9,10},{10,1... | collective-permute-start | bytes 393224 | tf_op jit(solution)/shard_map/ppermute | solution.py:30
  37.4 3.8 %collective-permute-start.9 = (bf16[128,512]{1,0:T(8,128)(2,1)S(1)}, bf16[128,512]{1,0:T(8,128)(2,1)S(1)}, u32[]{:S(2)}, u32[]{:S(2)}) collective-permute-start(bf16[128,512]{1,0:T(8,128)(2,1)S(1)} %get-tuple-element.33), channel_id=1, source_target_pairs={{0,2},{1,3},{2,0},{3,1},{4,6},{5,7},{6,4},{7,5},{8,10},{9,11},{10,... | collective-permute-start | bytes 393224 | tf_op jit(solution)/shard_map/ppermute | solution.py:30
  41.2 1.9 %collective-permute-start.10 = (bf16[128,512]{1,0:T(8,128)(2,1)S(1)}, bf16[128,512]{1,0:T(8,128)(2,1)S(1)}, u32[]{:S(2)}, u32[]{:S(2)}) collective-permute-start(bf16[128,512]{1,0:T(8,128)(2,1)S(1)} %get-tuple-element.34), channel_id=1, source_target_pairs={{0,3},{1,0},{2,1},{3,2},{4,7},{5,4},{6,5},{7,6},{8,11},{9,8},{10,9... | collective-permute-start | bytes 393224 | tf_op jit(solution)/shard_map/ppermute | solution.py:30
  43.1 1.4 %collective-permute-start.1 = (bf16[128,1024]{1,0:T(8,128)(2,1)S(1)}, bf16[128,1024]{1,0:T(8,128)(2,1)S(1)}, u32[]{:S(2)}, u32[]{:S(2)}) collective-permute-start(bf16[128,1024]{1,0:T(8,128)(2,1)S(1)} %bitcast.9), channel_id=1, source_target_pairs={{0,2},{1,3},{2,0},{3,1},{4,6},{5,7},{6,4},{7,5},{8,10},{9,11},{10,... | collective-permute-start | bytes 786440 | tf_op jit(solution)/shard_map/ppermute | solution.py:30
  44.7 3.4 %collective-permute-done.9.refs_10_ = bf16[128,512]{1,0:T(8,128)(2,1)S(1)} collective-permute-done((bf16[128,512]{1,0:T(8,128)(2,1)S(1)}, bf16[128,512]{1,0:T(8,128)(2,1)S(1)}, u32[]{:S(2)}, u32[]{:S(2)}) %collective-permute-start.9) | collective-permute-done | bytes 131104 | tf_op jit(solution)/shard_map/ppermute | solution.py:30
  48.1 0.5 collective-permute-start.11
  48.7 0.9 collective-permute-done.11.refs_12_
  49.6 0.4 collective-permute-start.12
  50.0 3.2 %collective-permute-done.2.refs_3_ = bf16[128,1024]{1,0:T(8,128)(2,1)S(1)} collective-permute-done((bf16[128,1024]{1,0:T(8,128)(2,1)S(1)}, bf16[128,1024]{1,0:T(8,128)(2,1)S(1)}, u32[]{:S(2)}, u32[]{:S(2)}) %collective-permute-start.2) | collective-permute-done | bytes 262176 | tf_op jit(solution)/shard_map/ppermute | solution.py:30
  53.2 0.5 collective-permute-done.1.refs_2_
  53.8 0.5 collective-permute-start.5
  54.3 5.0 %collective-permute-done.refs_1_ = bf16[128,1024]{1,0:T(8,128)(2,1)S(1)} collective-permute-done((bf16[128,1024]{1,0:T(8,128)(2,1)S(1)}, bf16[128,1024]{1,0:T(8,128)(2,1)S(1)}, u32[]{:S(2)}, u32[]{:S(2)}) %collective-permute-start) | collective-permute-done | bytes 262176 | tf_op jit(solution)/shard_map/ppermute | solution.py:30
  59.3 0.5 collective-permute-start.4
  59.8 0.5 collective-permute-start.14
  60.3 0.8 collective-permute-done.13.refs_14_
  61.1 0.2 collective-permute-done.14.refs_15_
  61.4 0.4 copy-done.14
  61.8 0.2 copy-done.15
  62.0 4.6 %shard_map.97 = (f32[1024,128]{1,0:T(8,128)S(1)}, f32[1024,128]{1,0:T(8,128)S(1)}, f32[1024,128]{1,0:T(8,128)S(1)}, f32[1024,128]{1,0:T(8,128)S(1)}, f32[1024,12...) custom-call(s32[1]{0:T(128)} %bitcast.idx, ...), custom_call_target="tpu_custom_call" | custom-call | tf_op jit(solution)/shard_map/pallas_call | solution.py:66
  66.6 1.3 %collective-permute-start.16 = (f32[8,128]{1,0:T(8,128)S(1)}, f32[8,128]{1,0:T(8,128)S(1)}, u32[]{:S(2)}, u32[]{:S(2)}) collective-permute-start(f32[8,128]{1,0:T(8,128)S(1)} %get-tuple-element.36), channel_id=1, source_target_pairs={{16,0},{24,8},{32,16},{40,24},{48,32},{56,40},{64,48},{72,56},{80,... | collective-permute-start | bytes 12296 | tf_op jit(solution)/shard_map/ppermute | solution.py:44
  67.9 1.5 %collective-permute-start.15 = (f32[8,128]{1,0:T(8,128)S(1)}, f32[8,128]{1,0:T(8,128)S(1)}, u32[]{:S(2)}, u32[]{:S(2)}) collective-permute-start(f32[8,128]{1,0:T(8,128)S(1)} %get-tuple-element.36), channel_id=1, source_target_pairs={{8,0},{16,8},{24,16},{32,24},{40,32},{48,40},{56,48},{64,56},{72,6... | collective-permute-start | bytes 12296 | tf_op jit(solution)/shard_map/ppermute | solution.py:44
  69.4 3.1 %collective-permute-done.16.two = f32[8,128]{1,0:T(8,128)S(1)} collective-permute-done((f32[8,128]{1,0:T(8,128)S(1)}, f32[8,128]{1,0:T(8,128)S(1)}, u32[]{:S(2)}, u32[]{:S(2)}) %collective-permute-start.16) | collective-permute-done | bytes 4128 | tf_op jit(solution)/shard_map/ppermute | solution.py:44
  72.4 0.9 collective-permute-done.15.one
  73.3 1.6 %shard_map.98 = (bf16[512,384]{1,0:T(8,128)(2,1)S(1)}, bf16[512,384]{1,0:T(8,128)(2,1)S(1)}, bf16[8,4,56,256]{3,2,1,0:T(8,128)(2,1)S(1)}) custom-call(s32[1]{0:T(128)} %bitcast.idx, f32[8,128]{1,0:T(8,128)S(1)} %collective-permute-done.15.one, f32[8,128]{1,0:T(8,128)S(1)} %collective-permute-done.16.two, f32[1024,128]{1,0:T(8,128)S(1)} %get-tuple-element.37.az, ...), custom_call_target="tpu_custom_call" | custom-call | tf_op jit(solution)/shard_map/pallas_call | solution.py:66
  74.9 0.9 copy-done.2
  75.9 0.7 copy-done.8
  76.6 12.0 %all-to-all-start.2 = ((bf16[32,56,256]{2,1,0:T(8,128)(2,1)}), bf16[32,56,256]{2,1,0:T(8,128)(2,1)S(1)}, u32[]{:S(2)}, u32[]{:S(2)}) async-start(bf16[32,56,256]{2,1,0:T(8,128)(2,1)} %bitcast.14), calls=%async_computation.2 | async-start | bytes 1835008 | tf_op jit(solution)/shard_map/all_to_all | solution.py:34
  88.7 0.3 collective-permute-start.18
  89.0 0.3 collective-permute-start.17
  89.3 14.3 %all-to-all-done.2.came = bf16[32,56,256]{2,1,0:T(8,128)(2,1)S(1)} async-done(((bf16[32,56,256]{2,1,0:T(8,128)(2,1)}), bf16[32,56,256]{2,1,0:T(8,128)(2,1)S(1)}, u32[]{:S(2)}, u32[]{:S(2)}) %all-to-all-start.2) | async-done | bytes 917536 | tf_op jit(solution)/shard_map/all_to_all | solution.py:34
  103.7 0.7 copy-done.4
  104.4 3.4 %all-to-all-start.3 = ((bf16[8,72,256]{2,1,0:T(8,128)(2,1)}), bf16[8,72,256]{2,1,0:T(8,128)(2,1)S(1)}, u32[]{:S(2)}, u32[]{:S(2)}) async-start(bf16[8,72,256]{2,1,0:T(8,128)(2,1)} %copy-done.4), calls=%async_computation.3 | async-start | bytes 589824 | tf_op jit(solution)/shard_map/all_to_all | solution.py:34
  107.9 1.0 shard_map.99
  108.9 1.7 %collective-permute-start.19 = (bf16[128,1024]{1,0:T(8,128)(2,1)S(1)}, bf16[128,1024]{1,0:T(8,128)(2,1)S(1)}, u32[]{:S(2)}, u32[]{:S(2)}) collective-permute-start(bf16[128,1024]{1,0:T(8,128)(2,1)S(1)} %get-tuple-element.48), channel_id=1, source_target_pairs={{0,3},{1,0},{2,1},{3,2},{4,7},{5,4},{6,5},{7,6},{8,11},{9,8},{10,9... | collective-permute-start | bytes 786440 | tf_op jit(solution)/shard_map/ppermute | solution.py:30
  110.5 0.6 collective-permute-start.20
  111.1 0.4 collective-permute-start.21
  111.5 5.5 %collective-permute-done.19.refs_0_ = bf16[128,1024]{1,0:T(8,128)(2,1)S(1)} collective-permute-done((bf16[128,1024]{1,0:T(8,128)(2,1)S(1)}, bf16[128,1024]{1,0:T(8,128)(2,1)S(1)}, u32[]{:S(2)}, u32[]{:S(2)}) %collective-permute-start.19) | collective-permute-done | bytes 262176 | tf_op jit(solution)/shard_map/ppermute | solution.py:30
  117.0 2.6 %collective-permute-done.20.refs_1_ = bf16[128,1024]{1,0:T(8,128)(2,1)S(1)} collective-permute-done((bf16[128,1024]{1,0:T(8,128)(2,1)S(1)}, bf16[128,1024]{1,0:T(8,128)(2,1)S(1)}, u32[]{:S(2)}, u32[]{:S(2)}) %collective-permute-start.20) | collective-permute-done | bytes 262176 | tf_op jit(solution)/shard_map/ppermute | solution.py:30
  119.6 6.3 %collective-permute-done.21.refs_2_ = bf16[128,1024]{1,0:T(8,128)(2,1)S(1)} collective-permute-done((bf16[128,1024]{1,0:T(8,128)(2,1)S(1)}, bf16[128,1024]{1,0:T(8,128)(2,1)S(1)}, u32[]{:S(2)}, u32[]{:S(2)}) %collective-permute-start.21) | collective-permute-done | bytes 262176 | tf_op jit(solution)/shard_map/ppermute | solution.py:30
  125.9 0.8 shard_map.100
  126.7 0.7 shard_map.102
  (44 shorter events, 0.5 us)
Async XLA Ops:
  20.3 14.1 %copy-start = (f32[1,128,1024]{2,1,0:T(8,128)S(1)}, f32[1,128,1024]{2,1,0:T(8,128)}, u32[]{:S(2)}) copy-start(f32[1,128,1024]{2,1,0:T(8,128)} %param.9) | copy-start | bytes 1572868
  20.3 14.1 %copy-start.5 = (bf16[1,128,1024]{2,1,0:T(8,128)(2,1)S(1)}, bf16[1,128,1024]{2,1,0:T(8,128)(2,1)}, u32[]{:S(2)}) copy-start(bf16[1,128,1024]{2,1,0:T(8,128)(2,1)} %param.13) | copy-start | bytes 786436
  20.3 41.7 %all-to-all-start.1 = ((bf16[32,48,256]{2,1,0:T(8,128)(2,1)}), bf16[32,48,256]{2,1,0:T(8,128)(2,1)S(1)}, u32[]{:S(2)}, u32[]{:S(2)}) async-start(bf16[32,48,256]{2,1,0:T(8,128)(2,1)} %shard_map.96), calls=%async_computation.1 | async-start | bytes 1572864 | tf_op jit(solution)/shard_map/all_to_all | solution.py:34
  29.9 4.4 %copy-start.7 = (s32[1,128]{1,0:T(1,128)S(1)}, s32[1,128]{1,0:T(1,128)}, u32[]{:S(2)}) copy-start(s32[1,128]{1,0:T(1,128)} %ids.3) | copy-start | bytes 1540
  29.9 4.4 %collective-permute-start.7 = (f32[2,1024]{1,0:T(2,128)S(1)}, f32[2,1024]{1,0:T(2,128)S(1)}, u32[]{:S(2)}, u32[]{:S(2)}) collective-permute-start(f32[2,1024]{1,0:T(2,128)S(1)} %get-tuple-element.30), channel_id=1, source_target_pairs={{0,4},{4,8},{8,12},{12,16},{16,20},{20,24},{24,28},{28,32},{32,36}... | collective-permute-start | bytes 24584 | tf_op jit(solution)/shard_map/ppermute | solution.py:44
  34.4 8.7 %copy-start.1 = (bf16[1,128,1024]{2,1,0:T(8,128)(2,1)S(1)}, bf16[1,128,1024]{2,1,0:T(8,128)(2,1)}, u32[]{:S(2)}) copy-start(bf16[1,128,1024]{2,1,0:T(8,128)(2,1)} %param.7) | copy-start | bytes 786436
  34.6 27.4 %copy-start.6 = (bf16[128,512]{1,0:T(8,128)(2,1)}, bf16[128,512]{1,0:T(8,128)(2,1)S(1)}, u32[]{:S(2)}) copy-start(bf16[128,512]{1,0:T(8,128)(2,1)S(1)} %get-tuple-element.31.refs_8_) | copy-start | bytes 393220
  34.6 10.0 %collective-permute-start.8 = (bf16[128,512]{1,0:T(8,128)(2,1)S(1)}, bf16[128,512]{1,0:T(8,128)(2,1)S(1)}, u32[]{:S(2)}, u32[]{:S(2)}) collective-permute-start(bf16[128,512]{1,0:T(8,128)(2,1)S(1)} %get-tuple-element.32), channel_id=1, source_target_pairs={{0,1},{1,2},{2,3},{3,0},{4,5},{5,6},{6,7},{7,4},{8,9},{9,10},{10,1... | collective-permute-start | bytes 393224 | tf_op jit(solution)/shard_map/ppermute | solution.py:30
  37.4 10.7 %collective-permute-start.9 = (bf16[128,512]{1,0:T(8,128)(2,1)S(1)}, bf16[128,512]{1,0:T(8,128)(2,1)S(1)}, u32[]{:S(2)}, u32[]{:S(2)}) collective-permute-start(bf16[128,512]{1,0:T(8,128)(2,1)S(1)} %get-tuple-element.33), channel_id=1, source_target_pairs={{0,2},{1,3},{2,0},{3,1},{4,6},{5,7},{6,4},{7,5},{8,10},{9,11},{10,... | collective-permute-start | bytes 393224 | tf_op jit(solution)/shard_map/ppermute | solution.py:30
  41.2 7.4 %collective-permute-start.10 = (bf16[128,512]{1,0:T(8,128)(2,1)S(1)}, bf16[128,512]{1,0:T(8,128)(2,1)S(1)}, u32[]{:S(2)}, u32[]{:S(2)}) collective-permute-start(bf16[128,512]{1,0:T(8,128)(2,1)S(1)} %get-tuple-element.34), channel_id=1, source_target_pairs={{0,3},{1,0},{2,1},{3,2},{4,7},{5,4},{6,5},{7,6},{8,11},{9,8},{10,9... | collective-permute-start | bytes 393224 | tf_op jit(solution)/shard_map/ppermute | solution.py:30
  43.1 10.1 %collective-permute-start.2 = (bf16[128,1024]{1,0:T(8,128)(2,1)S(1)}, bf16[128,1024]{1,0:T(8,128)(2,1)S(1)}, u32[]{:S(2)}, u32[]{:S(2)}) collective-permute-start(bf16[128,1024]{1,0:T(8,128)(2,1)S(1)} %bitcast.8), channel_id=1, source_target_pairs={{0,3},{1,0},{2,1},{3,2},{4,7},{5,4},{6,5},{7,6},{8,11},{9,8},{10,9... | collective-permute-start | bytes 786440 | tf_op jit(solution)/shard_map/ppermute | solution.py:30
  43.1 10.6 %collective-permute-start.1 = (bf16[128,1024]{1,0:T(8,128)(2,1)S(1)}, bf16[128,1024]{1,0:T(8,128)(2,1)S(1)}, u32[]{:S(2)}, u32[]{:S(2)}) collective-permute-start(bf16[128,1024]{1,0:T(8,128)(2,1)S(1)} %bitcast.9), channel_id=1, source_target_pairs={{0,2},{1,3},{2,0},{3,1},{4,6},{5,7},{6,4},{7,5},{8,10},{9,11},{10,... | collective-permute-start | bytes 786440 | tf_op jit(solution)/shard_map/ppermute | solution.py:30
  44.6 17.4 %copy-start.9 = (bf16[128,512]{1,0:T(8,128)(2,1)}, bf16[128,512]{1,0:T(8,128)(2,1)S(1)}, u32[]{:S(2)}) copy-start(bf16[128,512]{1,0:T(8,128)(2,1)S(1)} %collective-permute-done.8.refs_9_) | copy-start | bytes 393220
  44.6 14.7 %collective-permute-start = (bf16[128,1024]{1,0:T(8,128)(2,1)S(1)}, bf16[128,1024]{1,0:T(8,128)(2,1)S(1)}, u32[]{:S(2)}, u32[]{:S(2)}) collective-permute-start(bf16[128,1024]{1,0:T(8,128)(2,1)S(1)} %bitcast.10), channel_id=1, source_target_pairs={{0,1},{1,2},{2,3},{3,0},{4,5},{5,6},{6,7},{7,4},{8,9},{9,10},{10,1... | collective-permute-start | bytes 786440 | tf_op jit(solution)/shard_map/ppermute | solution.py:30
  48.1 13.9 %copy-start.10 = (bf16[128,512]{1,0:T(8,128)(2,1)}, bf16[128,512]{1,0:T(8,128)(2,1)S(1)}, u32[]{:S(2)}) copy-start(bf16[128,512]{1,0:T(8,128)(2,1)S(1)} %collective-permute-done.9.refs_10_) | copy-start | bytes 393220
  48.1 1.5 %collective-permute-start.11 = (bf16[128,512]{1,0:T(8,128)(2,1)S(1)}, bf16[128,512]{1,0:T(8,128)(2,1)S(1)}, u32[]{:S(2)}, u32[]{:S(2)}) collective-permute-start(bf16[128,512]{1,0:T(8,128)(2,1)S(1)} %get-tuple-element.31.refs_8_), channel_id=1, source_target_pairs={{0,4},{4,0},{1,5},{5,1},{2,6},{6,2},{3,7},{7,3},{8,12},{12,8},{9,1... | collective-permute-start | bytes 393224 | tf_op jit(solution)/shard_map/ppermute | solution.py:30
  48.6 13.4 %copy-start.11 = (bf16[128,512]{1,0:T(8,128)(2,1)}, bf16[128,512]{1,0:T(8,128)(2,1)S(1)}, u32[]{:S(2)}) copy-start(bf16[128,512]{1,0:T(8,128)(2,1)S(1)} %collective-permute-done.10.refs_11_) | copy-start | bytes 393220
  48.6 11.2 %collective-permute-start.3 = (bf16[128,1024]{1,0:T(8,128)(2,1)S(1)}, bf16[128,1024]{1,0:T(8,128)(2,1)S(1)}, u32[]{:S(2)}, u32[]{:S(2)}) collective-permute-start(bf16[128,1024]{1,0:T(8,128)(2,1)S(1)} %bitcast.11), channel_id=1, source_target_pairs={{0,4},{4,0},{1,5},{5,1},{2,6},{6,2},{3,7},{7,3},{8,12},{12,8},{9,1... | collective-permute-start | bytes 786440 | tf_op jit(solution)/shard_map/ppermute | solution.py:30
  49.6 12.4 %copy-start.12 = (bf16[128,512]{1,0:T(8,128)(2,1)}, bf16[128,512]{1,0:T(8,128)(2,1)S(1)}, u32[]{:S(2)}) copy-start(bf16[128,512]{1,0:T(8,128)(2,1)S(1)} %collective-permute-done.11.refs_12_) | copy-start | bytes 393220
  49.6 10.2 %collective-permute-start.12 = (bf16[128,512]{1,0:T(8,128)(2,1)S(1)}, bf16[128,512]{1,0:T(8,128)(2,1)S(1)}, u32[]{:S(2)}, u32[]{:S(2)}) collective-permute-start(bf16[128,512]{1,0:T(8,128)(2,1)S(1)} %collective-permute-done.8.refs_9_), channel_id=1, source_target_pairs={{0,4},{4,0},{1,5},{5,1},{2,6},{6,2},{3,7},{7,3},{8,12},{12,8},{9,1... | collective-permute-start | bytes 393224 | tf_op jit(solution)/shard_map/ppermute | solution.py:30
  53.2 8.1 %collective-permute-start.6 = (bf16[128,1024]{1,0:T(8,128)(2,1)S(1)}, bf16[128,1024]{1,0:T(8,128)(2,1)S(1)}, u32[]{:S(2)}, u32[]{:S(2)}) collective-permute-start(bf16[128,1024]{1,0:T(8,128)(2,1)S(1)} %collective-permute-done.2.refs_3_), channel_id=1, source_target_pairs={{0,4},{4,0},{1,5},{5,1},{2,6},{6,2},{3,7},{7,3},{8,12},{12,8},{9,1... | collective-permute-start | bytes 786440 | tf_op jit(solution)/shard_map/ppermute | solution.py:30
  53.8 7.6 %collective-permute-start.5 = (bf16[128,1024]{1,0:T(8,128)(2,1)S(1)}, bf16[128,1024]{1,0:T(8,128)(2,1)S(1)}, u32[]{:S(2)}, u32[]{:S(2)}) collective-permute-start(bf16[128,1024]{1,0:T(8,128)(2,1)S(1)} %collective-permute-done.1.refs_2_), channel_id=1, source_target_pairs={{0,4},{4,0},{1,5},{5,1},{2,6},{6,2},{3,7},{7,3},{8,12},{12,8},{9,1... | collective-permute-start | bytes 786440 | tf_op jit(solution)/shard_map/ppermute | solution.py:30
  59.3 2.7 %collective-permute-start.4 = (bf16[128,1024]{1,0:T(8,128)(2,1)S(1)}, bf16[128,1024]{1,0:T(8,128)(2,1)S(1)}, u32[]{:S(2)}, u32[]{:S(2)}) collective-permute-start(bf16[128,1024]{1,0:T(8,128)(2,1)S(1)} %collective-permute-done.refs_1_), channel_id=1, source_target_pairs={{0,4},{4,0},{1,5},{5,1},{2,6},{6,2},{3,7},{7,3},{8,12},{12,8},{9,1... | collective-permute-start | bytes 786440 | tf_op jit(solution)/shard_map/ppermute | solution.py:30
  59.8 1.3 %collective-permute-start.13 = (bf16[128,512]{1,0:T(8,128)(2,1)S(1)}, bf16[128,512]{1,0:T(8,128)(2,1)S(1)}, u32[]{:S(2)}, u32[]{:S(2)}) collective-permute-start(bf16[128,512]{1,0:T(8,128)(2,1)S(1)} %collective-permute-done.9.refs_10_), channel_id=1, source_target_pairs={{0,4},{4,0},{1,5},{5,1},{2,6},{6,2},{3,7},{7,3},{8,12},{12,8},{9,1... | collective-permute-start | bytes 393224 | tf_op jit(solution)/shard_map/ppermute | solution.py:30
  59.8 1.5 %copy-start.13 = (bf16[128,512]{1,0:T(8,128)(2,1)}, bf16[128,512]{1,0:T(8,128)(2,1)S(1)}, u32[]{:S(2)}) copy-start(bf16[128,512]{1,0:T(8,128)(2,1)S(1)} %collective-permute-done.12.refs_13_) | copy-start | bytes 393220
  59.8 1.5 %collective-permute-start.14 = (bf16[128,512]{1,0:T(8,128)(2,1)S(1)}, bf16[128,512]{1,0:T(8,128)(2,1)S(1)}, u32[]{:S(2)}, u32[]{:S(2)}) collective-permute-start(bf16[128,512]{1,0:T(8,128)(2,1)S(1)} %collective-permute-done.10.refs_11_), channel_id=1, source_target_pairs={{0,4},{4,0},{1,5},{5,1},{2,6},{6,2},{3,7},{7,3},{8,12},{12,8},{9,1... | collective-permute-start | bytes 393224 | tf_op jit(solution)/shard_map/ppermute | solution.py:30
  61.1 0.7 copy-start.14
  61.3 0.6 copy-start.15
  66.6 5.9 %collective-permute-start.16 = (f32[8,128]{1,0:T(8,128)S(1)}, f32[8,128]{1,0:T(8,128)S(1)}, u32[]{:S(2)}, u32[]{:S(2)}) collective-permute-start(f32[8,128]{1,0:T(8,128)S(1)} %get-tuple-element.36), channel_id=1, source_target_pairs={{16,0},{24,8},{32,16},{40,24},{48,32},{56,40},{64,48},{72,56},{80,... | collective-permute-start | bytes 12296 | tf_op jit(solution)/shard_map/ppermute | solution.py:44
  67.9 5.4 %collective-permute-start.15 = (f32[8,128]{1,0:T(8,128)S(1)}, f32[8,128]{1,0:T(8,128)S(1)}, u32[]{:S(2)}, u32[]{:S(2)}) collective-permute-start(f32[8,128]{1,0:T(8,128)S(1)} %get-tuple-element.36), channel_id=1, source_target_pairs={{8,0},{16,8},{24,16},{32,24},{40,32},{48,40},{56,48},{64,56},{72,6... | collective-permute-start | bytes 12296 | tf_op jit(solution)/shard_map/ppermute | solution.py:44
  74.9 0.9 copy-start.2
  75.9 0.7 copy-start.8
  75.9 12.8 %copy-start.3 = (bf16[4,384,256]{2,1,0:T(8,128)(2,1)S(1)}, bf16[4,384,256]{2,1,0:T(8,128)(2,1)}, u32[]{:S(2)}) copy-start(bf16[4,384,256]{2,1,0:T(8,128)(2,1)} %get-tuple-element.46.weight) | copy-start | bytes 2359300
  76.6 26.9 %all-to-all-start.2 = ((bf16[32,56,256]{2,1,0:T(8,128)(2,1)}), bf16[32,56,256]{2,1,0:T(8,128)(2,1)S(1)}, u32[]{:S(2)}, u32[]{:S(2)}) async-start(bf16[32,56,256]{2,1,0:T(8,128)(2,1)} %bitcast.14), calls=%async_computation.2 | async-start | bytes 1835008 | tf_op jit(solution)/shard_map/all_to_all | solution.py:34
  88.7 19.2 %collective-permute-start.18 = (bf16[4,384,256]{2,1,0:T(8,128)(2,1)S(1)}, bf16[4,384,256]{2,1,0:T(8,128)(2,1)S(1)}, u32[]{:S(2)}, u32[]{:S(2)}) collective-permute-start(bf16[4,384,256]{2,1,0:T(8,128)(2,1)S(1)} %copy-done.3), channel_id=1, source_target_pairs={{0,4},{4,0},{1,5},{5,1},{2,6},{6,2},{3,7},{7,3},{8,12},{12,8},{9,1... | collective-permute-start | bytes 2359304 | tf_op jit(solution)/shard_map/ppermute | solution.py:30
  89.0 18.8 %collective-permute-start.17 = (bf16[512,384]{1,0:T(8,128)(2,1)}, bf16[512,384]{1,0:T(8,128)(2,1)S(1)}, u32[]{:S(2)}, u32[]{:S(2)}) collective-permute-start(bf16[512,384]{1,0:T(8,128)(2,1)} %copy-done.8), channel_id=1, source_target_pairs={{0,4},{4,0},{1,5},{5,1},{2,6},{6,2},{3,7},{7,3},{8,12},{12,8},{9,1... | collective-permute-start | bytes 1179656 | tf_op jit(solution)/shard_map/ppermute | solution.py:30
  103.7 0.7 copy-start.4
  104.4 22.3 %all-to-all-start.3 = ((bf16[8,72,256]{2,1,0:T(8,128)(2,1)}), bf16[8,72,256]{2,1,0:T(8,128)(2,1)S(1)}, u32[]{:S(2)}, u32[]{:S(2)}) async-start(bf16[8,72,256]{2,1,0:T(8,128)(2,1)} %copy-done.4), calls=%async_computation.3 | async-start | bytes 589824 | tf_op jit(solution)/shard_map/all_to_all | solution.py:34
  108.9 8.1 %collective-permute-start.19 = (bf16[128,1024]{1,0:T(8,128)(2,1)S(1)}, bf16[128,1024]{1,0:T(8,128)(2,1)S(1)}, u32[]{:S(2)}, u32[]{:S(2)}) collective-permute-start(bf16[128,1024]{1,0:T(8,128)(2,1)S(1)} %get-tuple-element.48), channel_id=1, source_target_pairs={{0,3},{1,0},{2,1},{3,2},{4,7},{5,4},{6,5},{7,6},{8,11},{9,8},{10,9... | collective-permute-start | bytes 786440 | tf_op jit(solution)/shard_map/ppermute | solution.py:30
  110.5 9.1 %collective-permute-start.20 = (bf16[128,1024]{1,0:T(8,128)(2,1)S(1)}, bf16[128,1024]{1,0:T(8,128)(2,1)S(1)}, u32[]{:S(2)}, u32[]{:S(2)}) collective-permute-start(bf16[128,1024]{1,0:T(8,128)(2,1)S(1)} %get-tuple-element.49), channel_id=1, source_target_pairs={{0,2},{1,3},{2,0},{3,1},{4,6},{5,7},{6,4},{7,5},{8,10},{9,11},{10,... | collective-permute-start | bytes 786440 | tf_op jit(solution)/shard_map/ppermute | solution.py:30
  111.1 14.8 %collective-permute-start.21 = (bf16[128,1024]{1,0:T(8,128)(2,1)S(1)}, bf16[128,1024]{1,0:T(8,128)(2,1)S(1)}, u32[]{:S(2)}, u32[]{:S(2)}) collective-permute-start(bf16[128,1024]{1,0:T(8,128)(2,1)S(1)} %get-tuple-element.50), channel_id=1, source_target_pairs={{0,1},{1,2},{2,3},{3,0},{4,5},{5,6},{6,7},{7,4},{8,9},{9,10},{10,1... | collective-permute-start | bytes 786440 | tf_op jit(solution)/shard_map/ppermute | solution.py:30
